TPU v7x, 128 devices: a whole 4x4x4 slice. The times are simulated.
128 devices in a mesh: rows: 8 (over y_hi, z), bundle: 16 (over y_lo, x, core).
Axes of the slice: x: 4, y: 4 (y_hi: 2, y_lo: 2; y = y_hi * 2 + y_lo), z: 4, core: 2. Of those that a mesh axis runs over, the one named last changes fastest.
Arguments:
- raw_values: float32 [32768, 4096], P(('rows', 'bundle')), may hold values from -2100 to 2100
- bin_edges: float32 [4096, 255], P(('rows', 'bundle')), may hold values from -2100 to 2100, as said below
- feature_column: int32 [4096], replicated, may hold values from 0 to 4095, each once
- bin_offset: int32 [4096], replicated, may hold values from 0 to 63
Outputs:
- bin_codes: int32 [32768, 4096], P('rows', 'bundle')
Inputs may be any that keep to these rules, and one draw needn't show every extreme that they name: Every row of bin_edges is strictly increasing. `feature_column`: each column 0 .. 4095 is named once.
All inputs are finite; a program needn't handle non-finite values.
Results may differ from a plain program's by a relative error of at most 0.0003.
Values may be sent and summed in bfloat16 or wider, within the bound.
No kernel may reach another device: no remote copies, remote signals or barrier semaphores. Data moves between devices by JAX's collectives and lax.ppermute only.
A program may use at most 64 MiB of HBM per device.

v0:
```python
import jax
import jax.numpy as jnp
from jax import lax
from jax.experimental import pallas as pl
from jax.experimental.pallas import tpu as pltpu
from jax.sharding import PartitionSpec as P


AXES = ("rows", "bundle")
SIDE = 4
PIECE = 32
EDGES = 256
SPAN = 256
FEATURES = 4096
CHIPS = 8
ORDER = ((0, 0), (1, 0), (0, 1), (0, 3), (1, 1), (1, 3), (1, 2), (0, 2))
BATCHES = (3, 2, 2, 1)
GROUP = 1024
SUB = 256


def device_at(y, z, x, core):
    return ((y // 2) * 4 + z) * 16 + (y % 2) * 8 + x * 2 + core


def planes():
    ring = range(SIDE)
    return [[device_at(y, z, x, core) for y in ring for x in ring] for z in ring for core in range(2)]


def along_z(value, step):
    pairs = [(h * SIDE + (z + step) % SIDE, h * SIDE + z) for h in range(2) for z in range(SIDE)]
    return lax.ppermute(value, "rows", pairs)


def swap_cores(value):
    return lax.ppermute(value, "bundle", [(i, i ^ 1) for i in range(16)])


def to_chip(value, dy, dx):
    pairs = []
    for y in range(2):
        for x in range(SIDE):
            for core in range(2):
                pairs.append((y * 8 + x * 2 + core, (y ^ dy) * 8 + (x + dx) % SIDE * 2 + core))
    return lax.ppermute(value, "bundle", pairs)


def pick(table, index):
    dims = lax.GatherDimensionNumbers(
        offset_dims=(),
        collapsed_slice_dims=(0,),
        start_index_map=(0,),
        operand_batching_dims=(1,),
        start_indices_batching_dims=(1,),
    )
    return lax.gather(
        table, index[..., None], dims, (1, 1), mode=lax.GatherScatterMode.PROMISE_IN_BOUNDS
    )


def count_below(values, table):
    top = table(31)
    group = jnp.where(values > jnp.broadcast_to(top[3:4], values.shape), 4, 0)
    group = jnp.where(values > pick(top, group + 1), group + 2, group)
    group = jnp.where(values > pick(top, group), group + 1, group)

    def at(o):
        return pick(table(o), group)

    b4 = values > at(15)
    b5 = values > jnp.where(b4, at(23), at(7))
    b6 = values > jnp.where(b4, jnp.where(b5, at(27), at(19)), jnp.where(b5, at(11), at(3)))

    def among(o):
        pairs = [jnp.where(b6, at(8 * i + 4 + o), at(8 * i + o)) for i in range(4)]
        return jnp.where(b4, jnp.where(b5, pairs[3], pairs[2]), jnp.where(b5, pairs[1], pairs[0]))

    b7 = values > among(1)
    b8 = values > jnp.where(b7, among(2), among(0))
    count = group * 32
    for bit, weight in ((b4, 16), (b5, 8), (b6, 4), (b7, 2), (b8, 1)):
        count = count + jnp.where(bit, weight, 0)
    return count


def prep_kernel(spot_ref, raw_ref, *refs):
    outs, buffer, sems, turned = refs[:CHIPS], refs[CHIPS], refs[CHIPS + 1], refs[CHIPS + 2 :]
    i = pl.program_id(0)

    def turn(j):
        flat = raw_ref[:, j * SUB : (j + 1) * SUB].T
        turned[j][pl.ds(0, SUB, stride=2), :] = flat[:, :128]
        turned[j][pl.ds(1, SUB, stride=2), :] = flat[:, 128:]

    def scatter(j):
        base = i * GROUP + j * SUB
        for start in range(0, SUB, 32):
            rows = []
            for q in range(8):
                four = turned[j][2 * start + 8 * q : 2 * start + 8 * q + 8, :]
                rows += [four[2 * k : 2 * k + 2, :] for k in range(4)]
            for k in range(32):
                buffer[spot_ref[base + start + k]] = rows[k]

    turn(0)
    for j in range(len(turned)):
        if j + 1 < len(turned):
            turn(j + 1)
        scatter(j)

    @pl.when(i == pl.num_programs(0) - 1)
    def _():
        copies = []
        for k, ref in enumerate(outs):
            copies.append(pltpu.make_async_copy(buffer.at[pl.ds(512 * k, 512)], ref, sems.at[k]))
        for copy in copies:
            copy.start()
        for copy in copies:
            copy.wait()


def prep(spot, raw):
    return pl.pallas_call(
        prep_kernel,
        grid_spec=pltpu.PrefetchScalarGridSpec(
            num_scalar_prefetch=1,
            grid=(FEATURES // GROUP,),
            in_specs=[pl.BlockSpec((256, GROUP), lambda i, c: (0, i))],
            out_specs=[pl.BlockSpec(memory_space=pltpu.HBM)] * CHIPS,
            scratch_shapes=[pltpu.VMEM((FEATURES, 2, 128), jnp.float32), pltpu.SemaphoreType.DMA((CHIPS,))]
            + [pltpu.VMEM((SUB * 2, 128), jnp.float32)] * (GROUP // SUB),
        ),
        out_shape=[jax.ShapeDtypeStruct((512, 2, 128), jnp.float32)] * CHIPS,
        name="prep",
    )(spot, raw)


def choose_kernel(row_ref, mine_ref, other_ref, out_ref, pool):
    pool[0:512, :] = mine_ref[...]
    pool[512:1024, :] = other_ref[...]
    pool[1024:1032, :] = jnp.zeros((8, EDGES), jnp.float32)

    def eight(i, carry):
        rows = [pool[pl.ds(row_ref[i * 8 + k], 1), :] for k in range(8)]
        out_ref[pl.ds(pl.multiple_of(i * 8, 8), 8), :] = jnp.concatenate(rows, axis=0)
        return carry

    lax.fori_loop(0, SPAN // 8, eight, 0)


def choose(row, mine, other):
    whole = pl.BlockSpec((512, EDGES), lambda i, r: (0, 0))
    return pl.pallas_call(
        choose_kernel,
        grid_spec=pltpu.PrefetchScalarGridSpec(
            num_scalar_prefetch=1,
            grid=(1,),
            in_specs=[whole, whole],
            out_specs=pl.BlockSpec((SPAN, EDGES), lambda i, r: (0, 0)),
            scratch_shapes=[pltpu.VMEM((1032, EDGES), jnp.float32)],
        ),
        out_shape=jax.ShapeDtypeStruct((SPAN, EDGES), jnp.float32),
        name="choose",
    )(row, mine, other)


def table_kernel(a_ref, b_ref, c_ref, d_ref, out_ref):
    total = (a_ref[...] + b_ref[...]) + (c_ref[...] + d_ref[...])
    out_ref[...] = total.T


def make_table(parts):
    return pl.pallas_call(
        table_kernel, out_shape=jax.ShapeDtypeStruct((EDGES, SPAN), jnp.float32), name="make_table"
    )(*parts)


def bin_kernel(row_ref, table_ref, offset_ref, *refs, count, fresh):
    own, swapped = refs[:count], refs[count : 2 * count]
    out_ref, stage, turned, result, in_sems, out_sems = refs[2 * count + (0 if fresh else 1) :]

    def take(i, side):
        source = own[i].at[0] if side == 0 else swapped[i].at[1]
        return pltpu.make_async_copy(source, stage.at[2 * i + side], in_sems.at[2 * i + side])

    def give(part):
        rows = pl.ds(pl.multiple_of(row_ref[part], 256), 256)
        return pltpu.make_async_copy(result.at[part], out_ref.at[rows, :], out_sems.at[part])

    for i in range(count):
        take(i, 0).start()
        take(i, 1).start()

    def arrive(part):
        pltpu.make_async_copy(own[0].at[0], stage.at[part], in_sems.at[part]).wait()

    def turn(tile, slot):
        line = (tile % 4 // 2) * 256 + tile % 2
        turned[slot] = stage[tile // 4, pl.ds(line, 128, stride=2), :].T

    arrive(0)
    turn(0, 0)
    last = 8 * count - 1

    def one_tile(t, carry):
        following = jnp.minimum(t + 1, last)

        @pl.when((t % 4 == 3) & (t < last))
        def _():
            arrive(following // 4)

        lanes = pl.ds(pl.multiple_of((t % 4 // 2) * 128, 128), 128)
        offset = jnp.broadcast_to(offset_ref[:, lanes], (8, 128))
        for r in range(0, 128, 8):
            below = count_below(
                turned[t % 2, r : r + 8, :], lambda o: table_ref[8 * o : 8 * o + 8, lanes]
            )
            rows = pl.ds(pl.multiple_of((t % 2) * 128 + r, 8), 8)
            result[t // 4, rows, lanes] = below + offset
        turn(following, 1 - t % 2)

        @pl.when(t % 4 == 3)
        def _():
            give(t // 4).start()

        return carry

    lax.fori_loop(0, 8 * count, one_tile, 0)
    for part in range(2 * count):
        give(part).wait()


def bin_chips(row, table, offset, own, swapped, out):
    count, fresh = len(own), out is None
    anywhere = pl.BlockSpec(memory_space=pltpu.HBM)
    return pl.pallas_call(
        lambda *refs: bin_kernel(*refs, count=count, fresh=fresh),
        grid_spec=pltpu.PrefetchScalarGridSpec(
            num_scalar_prefetch=1,
            grid=(1,),
            in_specs=[
                pl.BlockSpec((EDGES, SPAN), lambda g, s: (0, 0)),
                pl.BlockSpec((1, SPAN), lambda g, s: (0, 0)),
            ]
            + [anywhere] * (2 * count + (0 if fresh else 1)),
            out_specs=anywhere,
            scratch_shapes=[
                pltpu.VMEM((2 * count, 512, 128), jnp.float32),
                pltpu.VMEM((2, 128, 128), jnp.float32),
                pltpu.VMEM((2 * count, 256, SPAN), jnp.int32),
                pltpu.SemaphoreType.DMA((2 * count,)),
                pltpu.SemaphoreType.DMA((2 * count,)),
            ],
        ),
        out_shape=jax.ShapeDtypeStruct((16 * 256, SPAN), jnp.int32),
        input_output_aliases={} if fresh else {3 + 2 * count: 0},
    )(row, table, offset, *own, *swapped, *([] if fresh else [out]))


def step(raw_values, bin_edges, feature_column, bin_offset):
    row, bundle = lax.axis_index("rows"), lax.axis_index("bundle")
    z, core = row % SIDE, bundle % 2
    padded = jnp.pad(bin_edges, ((0, 0), (0, 1)))
    ordered = padded.reshape(PIECE, 8, 32).transpose(0, 2, 1).reshape(PIECE, EDGES)
    copies = jnp.broadcast_to(ordered[None], (16, PIECE, EDGES))
    mine = lax.all_to_all(copies, AXES, split_axis=0, concat_axis=0, axis_index_groups=planes(), tiled=True)
    mine = mine.reshape(512, EDGES)

    x, y_low = (bundle // 2) % SIDE, bundle // 8
    owner, inside = feature_column // SPAN, feature_column % SPAN
    chip = (owner // 8 ^ y_low) * SIDE + ((owner // 2) % SIDE - x) % SIDE
    spot = chip * 512 + (owner % 2 ^ core) * 256 + inside
    sent = [value.reshape(2, 512, 128) for value in prep(spot, raw_values)]
    arrived = []
    for dy, dx in ORDER:
        value = sent[dy * SIDE + dx]
        arrived.append(to_chip(value, dy, dx) if dy + dx else value)

    wanted = bundle * SPAN + jnp.arange(SPAN, dtype=jnp.int32)
    named = feature_column[None, :] == wanted[:, None]
    feature = jnp.max(jnp.where(named, jnp.arange(FEATURES, dtype=jnp.int32)[None], 0), axis=1)
    offset = jnp.max(jnp.where(named, bin_offset[None], 0), axis=1)
    device = feature // PIECE
    far_y = (device // 64) * 2 + (device // 8) % 2
    line = (far_y * SIDE + (device // 2) % SIDE) * PIECE + feature % PIECE
    line = jnp.where(device % 2 == core, line, line + 512)
    line = jnp.where((device // 16) % SIDE == z, line, 1024)
    part = choose(line, mine, swap_cores(mine))
    groups, done = [], 0
    for count in BATCHES:
        groups.append((ORDER[done : done + count], arrived[done : done + count]))
        done += count
    near, *turned = [along_z(part, step) for step in (1, 3, 2)]
    *own, near = lax.optimization_barrier((*groups[0][1], near))
    swapped = [swap_cores(value) for value in own]
    table = make_table([part, near] + turned)
    *following, table = lax.optimization_barrier((*groups[1][1], table))
    out = None
    for n, (chips, later) in enumerate(groups):
        if n == 1:
            own, swapped = following, [swap_cores(value) for value in following]
        elif n > 1:
            *own, out = lax.optimization_barrier((*later, out))
            swapped = [swap_cores(value) for value in own]
        row = []
        for dy, dx in chips:
            base = ((y_low ^ dy) * SIDE + (x - dx) % SIDE) * 512
            row += [base + core * 256, base + (1 - core) * 256]
        row = jnp.stack(row).astype(jnp.int32)
        out = bin_chips(row, table, offset[None], own, swapped, out)
    return out


def solution(mesh):
    in_specs = (P(AXES, None), P(AXES, None), P(), P())
    return jax.shard_map(step, mesh=mesh, in_specs=in_specs, out_specs=P("rows", "bundle"), check_vma=False)
```

profile of v0, /device:TPU:3, one launch (start us, length us, event | category | flops | bytes accessed | tf_op | source)
XLA Modules:
  0.0 110.9 jit_solution(12872040182227495698)
XLA Ops:
  0.0 0.8 pad.4
  1.1 0.9 broadcast_in_dim.43
  1.9 6.9 %all-to-all-start = ((f32[16,32,256]{2,1,0:T(8,128)}), f32[16,32,256]{2,1,0:T(8,128)S(1)}, u32[]{:S(2)}, u32[]{:S(2)}) async-start(f32[16,32,256]{2,1,0:T(8,128)} %broadcast_in_dim.43), calls=%async_computation | async-start | bytes 1048576 | tf_op jit(solution)/shard_map/all_to_all | solution.py:267
  8.9 1.4 %fusion.8.spot_ref = s32[4096]{0:T(1024)} fusion(s32[4096]{0:T(1024)} %param.6, s32[]{:T(128)S(6)} %select_n.132, s32[]{:T(128)S(6)} %select_n.130, s32[]{:T(128)S(6)} %select_n.128), kind=kLoop, calls=%fused_computation.29 | loop fusion | flops 323584 | bytes 32780 | tf_op jit(solution)/shard_map/add | solution.py:273
  10.2 9.1 %prep.1 = (f32[512,2,128]{2,1,0:T(2,128)}, f32[512,2,128]{2,1,0:T(2,128)}, f32[512,2,128]{2,1,0:T(2,128)}, f32[512,2,128]{2,1,0:T(2,128)}, f32[512,2,128]{2,1,0:...) custom-call(s32[4096]{0:T(1024)} %fusion.8.spot_ref, f32[256,4096]{1,0:T(8,128)} %raw_ref.1), custom_call_target="tpu_custom_call" | custom-call | tf_op jit(solution)/shard_map/prep/pallas_call | solution.py:124
  19.3 1.3 %collective-permute-start.3 = (f32[2,512,128]{2,1,0:T(8,128)}, f32[2,512,128]{2,1,0:T(8,128)S(1)}, u32[]{:S(2)}, u32[]{:S(2)}) collective-permute-start(f32[2,512,128]{2,1,0:T(8,128)} %bitcast.44), channel_id=1, source_target_pairs={{0,8},{1,9},{2,10},{3,11},{4,12},{5,13},{6,14},{7,15},{8,0},{9,1},... | collective-permute-start | bytes 1572872 | tf_op jit(solution)/shard_map/ppermute | solution.py:46
  20.6 1.2 %collective-permute-start.4 = (f32[2,512,128]{2,1,0:T(8,128)}, f32[2,512,128]{2,1,0:T(8,128)S(1)}, u32[]{:S(2)}, u32[]{:S(2)}) collective-permute-start(f32[2,512,128]{2,1,0:T(8,128)} %bitcast.43), channel_id=1, source_target_pairs={{0,2},{1,3},{2,4},{3,5},{4,6},{5,7},{6,0},{7,1},{8,10},{9,11},{10,... | collective-permute-start | bytes 1572872 | tf_op jit(solution)/shard_map/ppermute | solution.py:46
  21.8 1.8 %collective-permute-start.2 = (f32[512,256]{1,0:T(8,128)S(1)}, f32[512,256]{1,0:T(8,128)S(1)}, u32[]{:S(2)}, u32[]{:S(2)}) collective-permute-start(f32[512,256]{1,0:T(8,128)S(1)} %bitcast.29), channel_id=1, source_target_pairs={{0,1},{1,0},{2,3},{3,2},{4,5},{5,4},{6,7},{7,6},{8,9},{9,8},{10,11... | collective-permute-start | bytes 1572872 | tf_op jit(solution)/shard_map/ppermute | solution.py:37
  23.6 1.9 %fusion.1 = (s32[256]{0:T(256)}, s32[256]{0:T(256)S(1)}) fusion(s32[4096]{0:T(1024)S(1)} %copy-done.17, s32[4096]{0:T(1024)S(1)} %copy-done.16, s32[256]{0:T(256)S(1)} %iota_add_fusion), kind=kLoop, calls=%fused_computation.3 | loop fusion | flops 5242368 | bytes 35840 | tf_op jit(solution)/shard_map/reduce_max | solution.py:283
  26.1 0.8 copy-done.12
  26.9 3.3 %choose.1.a_ref = f32[256,256]{1,0:T(8,128)} custom-call(s32[256]{0:T(256)} %compare_select_fusion.9.row_ref, f32[512,256]{1,0:T(8,128)} %bitcast.30, f32[512,256]{1,0:T(8,128)} %copy-done.12), custom_call_target="tpu_custom_call" | custom-call | tf_op jit(solution)/shard_map/choose/pallas_call | solution.py:154
  30.2 3.8 %collective-permute-start.5 = (f32[256,256]{1,0:T(8,128)}, f32[256,256]{1,0:T(8,128)S(1)}, u32[]{:S(2)}, u32[]{:S(2)}) collective-permute-start(f32[256,256]{1,0:T(8,128)} %choose.1.a_ref), channel_id=1, source_target_pairs={{16,0},{32,16},{48,32},{0,48},{80,64},{96,80},{112,96},{64,112},{1... | collective-permute-start | bytes 786440 | tf_op jit(solution)/shard_map/ppermute | solution.py:33
  33.9 0.9 collective-permute-start.1
  35.4 10.1 %collective-permute-done.5.b_ref = f32[256,256]{1,0:T(8,128)S(1)} collective-permute-done((f32[256,256]{1,0:T(8,128)}, f32[256,256]{1,0:T(8,128)S(1)}, u32[]{:S(2)}, u32[]{:S(2)}) %collective-permute-start.5) | collective-permute-done | bytes 262176 | tf_op jit(solution)/shard_map/ppermute | solution.py:33
  45.5 0.9 collective-permute-start.13
  46.8 9.4 %collective-permute-done.6.c_ref = f32[256,256]{1,0:T(8,128)S(1)} collective-permute-done((f32[256,256]{1,0:T(8,128)}, f32[256,256]{1,0:T(8,128)S(1)}, u32[]{:S(2)}, u32[]{:S(2)}) %collective-permute-start.6) | collective-permute-done | bytes 262176 | tf_op jit(solution)/shard_map/ppermute | solution.py:33
  57.2 2.0 %make_table.1.refs_1_ = f32[256,256]{1,0:T(8,128)} custom-call(f32[256,256]{1,0:T(8,128)} %choose.1.a_ref, f32[256,256]{1,0:T(8,128)} %copy-done.13, f32[256,256]{1,0:T(8,128)} %copy-done.15, f32[256,256]{1,0:T(8,128)} %copy-done.14), custom_call_target="tpu_custom_call" | custom-call | tf_op jit(solution)/shard_map/make_table/pallas_call | solution.py:174
  59.3 1.4 %collective-permute-start.15 = (f32[2,512,128]{2,1,0:T(8,128)S(1)}, f32[2,512,128]{2,1,0:T(8,128)}, u32[]{:S(2)}, u32[]{:S(2)}) collective-permute-start(f32[2,512,128]{2,1,0:T(8,128)S(1)} %collective-permute-done.4.refs_5_), channel_id=1, source_target_pairs={{0,1},{1,0},{2,3},{3,2},{4,5},{5,4},{6,7},{7,6},{8,9},{9,8},{10,11... | collective-permute-start | bytes 1572872 | tf_op jit(solution)/shard_map/ppermute | solution.py:37
  61.6 2.7 %collective-permute-start.10 = (f32[2,512,128]{2,1,0:T(8,128)}, f32[2,512,128]{2,1,0:T(8,128)S(1)}, u32[]{:S(2)}, u32[]{:S(2)}) collective-permute-start(f32[2,512,128]{2,1,0:T(8,128)} %bitcast.39), channel_id=1, source_target_pairs={{0,12},{1,13},{2,14},{3,15},{4,8},{5,9},{6,10},{7,11},{8,4},{9,5},... | collective-permute-start | bytes 1572872 | tf_op jit(solution)/shard_map/ppermute | solution.py:46
  65.5 8.9 %shard_map.46.refs_7_ = s32[4096,256]{1,0:T(8,128)} custom-call(s32[6]{0:T(128)} %stack.79.refs_0_, f32[256,256]{1,0:T(8,128)} %make_table.1.refs_1_, s32[1,256]{1,0:T(1,128)} %bitcast.34, f32[2,512,128]{2,1,0:T(8,128)} %bitcast.32, f32[2,512,128]{2,1,0:T(8,128)} %copy-done.1, f32[2,512,128]{2,1,0:T(8,128)} %copy-done.2, f32[2,512,128]{2,1,0:T(8,128)} %copy-done.7, ...), custom_call_target="tpu_custom_call" | custom-call | tf_op jit(solution)/shard_map/pallas_call | solution.py:237
  74.5 7.0 %shard_map.47.refs_7_ = s32[4096,256]{1,0:T(8,128)} custom-call(s32[4]{0:T(128)} %pad_add_fusion.2.refs_0_, f32[256,256]{1,0:T(8,128)} %make_table.1.refs_1_, s32[1,256]{1,0:T(1,128)} %bitcast.35, f32[2,512,128]{2,1,0:T(8,128)} %copy-done.6, f32[2,512,128]{2,1,0:T(8,128)} %copy-done.5, ...), custom_call_target="tpu_custom_call", output_to_operand_aliasing={{}: (7, {})} | custom-call | tf_op jit(solution)/shard_map/pallas_call | solution.py:237
  81.5 3.9 %collective-permute-done.10.refs_4_ = f32[2,512,128]{2,1,0:T(8,128)S(1)} collective-permute-done((f32[2,512,128]{2,1,0:T(8,128)}, f32[2,512,128]{2,1,0:T(8,128)S(1)}, u32[]{:S(2)}, u32[]{:S(2)}) %collective-permute-start.10) | collective-permute-done | bytes 524320 | tf_op jit(solution)/shard_map/ppermute | solution.py:46
  85.5 1.9 %collective-permute-start.16 = (f32[2,512,128]{2,1,0:T(8,128)S(1)}, f32[2,512,128]{2,1,0:T(8,128)S(1)}, u32[]{:S(2)}, u32[]{:S(2)}) collective-permute-start(f32[2,512,128]{2,1,0:T(8,128)S(1)} %collective-permute-done.9.refs_3_), channel_id=1, source_target_pairs={{0,1},{1,0},{2,3},{3,2},{4,5},{5,4},{6,7},{7,6},{8,9},{9,8},{10,11... | collective-permute-start | bytes 1572872 | tf_op jit(solution)/shard_map/ppermute | solution.py:37
  87.3 1.7 %collective-permute-start.8 = (f32[2,512,128]{2,1,0:T(8,128)}, f32[2,512,128]{2,1,0:T(8,128)S(1)}, u32[]{:S(2)}, u32[]{:S(2)}) collective-permute-start(f32[2,512,128]{2,1,0:T(8,128)} %bitcast.38), channel_id=1, source_target_pairs={{0,4},{1,5},{2,6},{3,7},{4,0},{5,1},{6,2},{7,3},{8,12},{9,13},{10,... | collective-permute-start | bytes 1572872 | tf_op jit(solution)/shard_map/ppermute | solution.py:46
  89.7 0.8 copy-done.9
  90.4 0.8 copy-done.10
  91.2 7.0 %shard_map.48.refs_5_ = s32[4096,256]{1,0:T(8,128)} custom-call(s32[4]{0:T(128)} %pad_add_fusion.1.refs_0_, f32[256,256]{1,0:T(8,128)} %make_table.1.refs_1_, s32[1,256]{1,0:T(1,128)} %bitcast.36, f32[2,512,128]{2,1,0:T(8,128)} %copy-done.3, f32[2,512,128]{2,1,0:T(8,128)} %copy-done.4, f32[2,512,128]{2,1,0:T(8,128)} %copy-done.9, ...), custom_call_target="tpu_custom_call", output_to_operand_aliasing={{}: (7, {})} | custom-call | tf_op jit(solution)/shard_map/pallas_call | solution.py:237
  98.3 3.7 %collective-permute-done.8.refs_3_ = f32[2,512,128]{2,1,0:T(8,128)S(1)} collective-permute-done((f32[2,512,128]{2,1,0:T(8,128)}, f32[2,512,128]{2,1,0:T(8,128)S(1)}, u32[]{:S(2)}, u32[]{:S(2)}) %collective-permute-start.8) | collective-permute-done | bytes 524320 | tf_op jit(solution)/shard_map/ppermute | solution.py:46
  102.0 1.4 %collective-permute-start.18 = (f32[2,512,128]{2,1,0:T(8,128)S(1)}, f32[2,512,128]{2,1,0:T(8,128)S(1)}, u32[]{:S(2)}, u32[]{:S(2)}) collective-permute-start(f32[2,512,128]{2,1,0:T(8,128)S(1)} %collective-permute-done.8.refs_3_), channel_id=1, source_target_pairs={{0,1},{1,0},{2,3},{3,2},{4,5},{5,4},{6,7},{7,6},{8,9},{9,8},{10,11... | collective-permute-start | bytes 1572872 | tf_op jit(solution)/shard_map/ppermute | solution.py:37
  103.9 1.0 collective-permute-done.18.refs_4_
  104.9 0.8 copy-done.11
  105.7 5.2 %shard_map.49 = s32[4096,256]{1,0:T(8,128)} custom-call(s32[2]{0:T(128)} %pad_add_fusion.refs_0_, f32[256,256]{1,0:T(8,128)} %make_table.1.refs_1_, s32[1,256]{1,0:T(1,128)} %bitcast.37, f32[2,512,128]{2,1,0:T(8,128)} %copy-done.8, f32[2,512,128]{2,1,0:T(8,128)} %copy-done.11, s32[4096,256]{1,0:T(8,128)} %shard_map.48.refs_5_), custom_call_target="tpu_custom_call", output_to_operand_aliasing={{}: (5, {})} | custom-call | tf_op jit(solution)/shard_map/pallas_call | solution.py:237
  (64 shorter events, 6.3 us)
Async XLA Ops:
  0.0 23.6 %copy-start.16 = (s32[4096]{0:T(1024)S(1)}, s32[4096]{0:T(1024)}, u32[]{:S(2)}) copy-start(s32[4096]{0:T(1024)} %param.6) | copy-start | bytes 49156
  0.0 23.6 %copy-start.17 = (s32[4096]{0:T(1024)S(1)}, s32[4096]{0:T(1024)}, u32[]{:S(2)}) copy-start(s32[4096]{0:T(1024)} %param.7) | copy-start | bytes 49156
  1.9 19.8 %all-to-all-start = ((f32[16,32,256]{2,1,0:T(8,128)}), f32[16,32,256]{2,1,0:T(8,128)S(1)}, u32[]{:S(2)}, u32[]{:S(2)}) async-start(f32[16,32,256]{2,1,0:T(8,128)} %broadcast_in_dim.43), calls=%async_computation | async-start | bytes 1048576 | tf_op jit(solution)/shard_map/all_to_all | solution.py:267
  19.3 15.5 %collective-permute-start.3 = (f32[2,512,128]{2,1,0:T(8,128)}, f32[2,512,128]{2,1,0:T(8,128)S(1)}, u32[]{:S(2)}, u32[]{:S(2)}) collective-permute-start(f32[2,512,128]{2,1,0:T(8,128)} %bitcast.44), channel_id=1, source_target_pairs={{0,8},{1,9},{2,10},{3,11},{4,12},{5,13},{6,14},{7,15},{8,0},{9,1},... | collective-permute-start | bytes 1572872 | tf_op jit(solution)/shard_map/ppermute | solution.py:46
  20.6 14.8 %collective-permute-start.4 = (f32[2,512,128]{2,1,0:T(8,128)}, f32[2,512,128]{2,1,0:T(8,128)S(1)}, u32[]{:S(2)}, u32[]{:S(2)}) collective-permute-start(f32[2,512,128]{2,1,0:T(8,128)} %bitcast.43), channel_id=1, source_target_pairs={{0,2},{1,3},{2,4},{3,5},{4,6},{5,7},{6,0},{7,1},{8,10},{9,11},{10,... | collective-permute-start | bytes 1572872 | tf_op jit(solution)/shard_map/ppermute | solution.py:46
  21.8 4.3 %copy-start = (f32[16,32,256]{2,1,0:T(8,128)}, f32[16,32,256]{2,1,0:T(8,128)S(1)}, u32[]{:S(2)}) copy-start(f32[16,32,256]{2,1,0:T(8,128)S(1)} %all-to-all-done) | copy-start | bytes 1572868
  21.8 4.3 %collective-permute-start.2 = (f32[512,256]{1,0:T(8,128)S(1)}, f32[512,256]{1,0:T(8,128)S(1)}, u32[]{:S(2)}, u32[]{:S(2)}) collective-permute-start(f32[512,256]{1,0:T(8,128)S(1)} %bitcast.29), channel_id=1, source_target_pairs={{0,1},{1,0},{2,3},{3,2},{4,5},{5,4},{6,7},{7,6},{8,9},{9,8},{10,11... | collective-permute-start | bytes 1572872 | tf_op jit(solution)/shard_map/ppermute | solution.py:37
  30.2 15.3 %collective-permute-start.5 = (f32[256,256]{1,0:T(8,128)}, f32[256,256]{1,0:T(8,128)S(1)}, u32[]{:S(2)}, u32[]{:S(2)}) collective-permute-start(f32[256,256]{1,0:T(8,128)} %choose.1.a_ref), channel_id=1, source_target_pairs={{16,0},{32,16},{48,32},{0,48},{80,64},{96,80},{112,96},{64,112},{1... | collective-permute-start | bytes 786440 | tf_op jit(solution)/shard_map/ppermute | solution.py:33
  33.9 12.5 %collective-permute-start.7 = (f32[256,256]{1,0:T(8,128)}, f32[256,256]{1,0:T(8,128)S(1)}, u32[]{:S(2)}, u32[]{:S(2)}) collective-permute-start(f32[256,256]{1,0:T(8,128)} %choose.1.a_ref), channel_id=1, source_target_pairs={{32,0},{48,16},{0,32},{16,48},{96,64},{112,80},{64,96},{80,112},{3... | collective-permute-start | bytes 786440 | tf_op jit(solution)/shard_map/ppermute | solution.py:33
  33.9 25.3 %collective-permute-start.1 = (f32[2,512,128]{2,1,0:T(8,128)}, f32[2,512,128]{2,1,0:T(8,128)S(1)}, u32[]{:S(2)}, u32[]{:S(2)}) collective-permute-start(f32[2,512,128]{2,1,0:T(8,128)} %bitcast.42), channel_id=1, source_target_pairs={{0,10},{1,11},{2,12},{3,13},{4,14},{5,15},{6,8},{7,9},{8,2},{9,3},... | collective-permute-start | bytes 1572872 | tf_op jit(solution)/shard_map/ppermute | solution.py:46
  34.8 30.7 %copy-start.1 = (f32[2,512,128]{2,1,0:T(8,128)}, f32[2,512,128]{2,1,0:T(8,128)S(1)}, u32[]{:S(2)}) copy-start(f32[2,512,128]{2,1,0:T(8,128)S(1)} %collective-permute-done.3.refs_4_) | copy-start | bytes 1572868
  34.8 24.4 %collective-permute-start = (f32[2,512,128]{2,1,0:T(8,128)}, f32[2,512,128]{2,1,0:T(8,128)S(1)}, u32[]{:S(2)}, u32[]{:S(2)}) collective-permute-start(f32[2,512,128]{2,1,0:T(8,128)} %bitcast.41), channel_id=1, source_target_pairs={{0,6},{1,7},{2,0},{3,1},{4,2},{5,3},{6,4},{7,5},{8,14},{9,15},{10,... | collective-permute-start | bytes 1572872 | tf_op jit(solution)/shard_map/ppermute | solution.py:46
  35.4 30.1 %copy-start.2 = (f32[2,512,128]{2,1,0:T(8,128)}, f32[2,512,128]{2,1,0:T(8,128)S(1)}, u32[]{:S(2)}) copy-start(f32[2,512,128]{2,1,0:T(8,128)S(1)} %collective-permute-done.4.refs_5_) | copy-start | bytes 1572868
  45.5 11.7 %copy-start.13 = (f32[256,256]{1,0:T(8,128)}, f32[256,256]{1,0:T(8,128)S(1)}, u32[]{:S(2)}) copy-start(f32[256,256]{1,0:T(8,128)S(1)} %collective-permute-done.5.b_ref) | copy-start | bytes 786436
  45.5 15.2 %collective-permute-start.13 = (f32[2,512,128]{2,1,0:T(8,128)}, f32[2,512,128]{2,1,0:T(8,128)S(1)}, u32[]{:S(2)}, u32[]{:S(2)}) collective-permute-start(f32[2,512,128]{2,1,0:T(8,128)} %bitcast.31), channel_id=1, source_target_pairs={{0,1},{1,0},{2,3},{3,2},{4,5},{5,4},{6,7},{7,6},{8,9},{9,8},{10,11... | collective-permute-start | bytes 1572872 | tf_op jit(solution)/shard_map/ppermute | solution.py:37
  46.4 14.8 %collective-permute-start.14 = (f32[2,512,128]{2,1,0:T(8,128)S(1)}, f32[2,512,128]{2,1,0:T(8,128)}, u32[]{:S(2)}, u32[]{:S(2)}) collective-permute-start(f32[2,512,128]{2,1,0:T(8,128)S(1)} %collective-permute-done.3.refs_4_), channel_id=1, source_target_pairs={{0,1},{1,0},{2,3},{3,2},{4,5},{5,4},{6,7},{7,6},{8,9},{9,8},{10,11... | collective-permute-start | bytes 1572872 | tf_op jit(solution)/shard_map/ppermute | solution.py:37
  46.4 9.8 %copy-start.14 = (f32[256,256]{1,0:T(8,128)}, f32[256,256]{1,0:T(8,128)S(1)}, u32[]{:S(2)}) copy-start(f32[256,256]{1,0:T(8,128)S(1)} %collective-permute-done.7.d_ref) | copy-start | bytes 786436
  46.4 9.8 %collective-permute-start.6 = (f32[256,256]{1,0:T(8,128)}, f32[256,256]{1,0:T(8,128)S(1)}, u32[]{:S(2)}, u32[]{:S(2)}) collective-permute-start(f32[256,256]{1,0:T(8,128)} %choose.1.a_ref), channel_id=1, source_target_pairs={{48,0},{0,16},{16,32},{32,48},{112,64},{64,80},{80,96},{96,112},{4... | collective-permute-start | bytes 786440 | tf_op jit(solution)/shard_map/ppermute | solution.py:33
  57.0 24.6 %collective-permute-start.9 = (f32[2,512,128]{2,1,0:T(8,128)}, f32[2,512,128]{2,1,0:T(8,128)S(1)}, u32[]{:S(2)}, u32[]{:S(2)}) collective-permute-start(f32[2,512,128]{2,1,0:T(8,128)} %bitcast.40), channel_id=1, source_target_pairs={{0,14},{1,15},{2,8},{3,9},{4,10},{5,11},{6,12},{7,13},{8,6},{9,7},... | collective-permute-start | bytes 1572872 | tf_op jit(solution)/shard_map/ppermute | solution.py:46
  59.3 15.2 %copy-start.5 = (f32[2,512,128]{2,1,0:T(8,128)}, f32[2,512,128]{2,1,0:T(8,128)S(1)}, u32[]{:S(2)}) copy-start(f32[2,512,128]{2,1,0:T(8,128)S(1)} %collective-permute-done.1.refs_4_) | copy-start | bytes 1572868
  59.3 15.2 %copy-start.6 = (f32[2,512,128]{2,1,0:T(8,128)}, f32[2,512,128]{2,1,0:T(8,128)S(1)}, u32[]{:S(2)}) copy-start(f32[2,512,128]{2,1,0:T(8,128)S(1)} %collective-permute-done.refs_3_) | copy-start | bytes 1572868
  59.3 6.3 %collective-permute-start.15 = (f32[2,512,128]{2,1,0:T(8,128)S(1)}, f32[2,512,128]{2,1,0:T(8,128)}, u32[]{:S(2)}, u32[]{:S(2)}) collective-permute-start(f32[2,512,128]{2,1,0:T(8,128)S(1)} %collective-permute-done.4.refs_5_), channel_id=1, source_target_pairs={{0,1},{1,0},{2,3},{3,2},{4,5},{5,4},{6,7},{7,6},{8,9},{9,8},{10,11... | collective-permute-start | bytes 1572872 | tf_op jit(solution)/shard_map/ppermute | solution.py:37
  60.7 13.8 %collective-permute-start.11 = (f32[2,512,128]{2,1,0:T(8,128)S(1)}, f32[2,512,128]{2,1,0:T(8,128)}, u32[]{:S(2)}, u32[]{:S(2)}) collective-permute-start(f32[2,512,128]{2,1,0:T(8,128)S(1)} %collective-permute-done.refs_3_), channel_id=1, source_target_pairs={{0,1},{1,0},{2,3},{3,2},{4,5},{5,4},{6,7},{7,6},{8,9},{9,8},{10,11... | collective-permute-start | bytes 1572872 | tf_op jit(solution)/shard_map/ppermute | solution.py:37
  60.8 13.7 %collective-permute-start.12 = (f32[2,512,128]{2,1,0:T(8,128)S(1)}, f32[2,512,128]{2,1,0:T(8,128)}, u32[]{:S(2)}, u32[]{:S(2)}) collective-permute-start(f32[2,512,128]{2,1,0:T(8,128)S(1)} %collective-permute-done.1.refs_4_), channel_id=1, source_target_pairs={{0,1},{1,0},{2,3},{3,2},{4,5},{5,4},{6,7},{7,6},{8,9},{9,8},{10,11... | collective-permute-start | bytes 1572872 | tf_op jit(solution)/shard_map/ppermute | solution.py:37
  61.6 23.9 %collective-permute-start.10 = (f32[2,512,128]{2,1,0:T(8,128)}, f32[2,512,128]{2,1,0:T(8,128)S(1)}, u32[]{:S(2)}, u32[]{:S(2)}) collective-permute-start(f32[2,512,128]{2,1,0:T(8,128)} %bitcast.39), channel_id=1, source_target_pairs={{0,12},{1,13},{2,14},{3,15},{4,8},{5,9},{6,10},{7,11},{8,4},{9,5},... | collective-permute-start | bytes 1572872 | tf_op jit(solution)/shard_map/ppermute | solution.py:46
  81.5 8.1 %copy-start.3 = (f32[2,512,128]{2,1,0:T(8,128)}, f32[2,512,128]{2,1,0:T(8,128)S(1)}, u32[]{:S(2)}) copy-start(f32[2,512,128]{2,1,0:T(8,128)S(1)} %collective-permute-done.9.refs_3_) | copy-start | bytes 1572868
  85.5 4.2 %copy-start.4 = (f32[2,512,128]{2,1,0:T(8,128)}, f32[2,512,128]{2,1,0:T(8,128)S(1)}, u32[]{:S(2)}) copy-start(f32[2,512,128]{2,1,0:T(8,128)S(1)} %collective-permute-done.10.refs_4_) | copy-start | bytes 1572868
  85.5 4.2 %collective-permute-start.16 = (f32[2,512,128]{2,1,0:T(8,128)S(1)}, f32[2,512,128]{2,1,0:T(8,128)S(1)}, u32[]{:S(2)}, u32[]{:S(2)}) collective-permute-start(f32[2,512,128]{2,1,0:T(8,128)S(1)} %collective-permute-done.9.refs_3_), channel_id=1, source_target_pairs={{0,1},{1,0},{2,3},{3,2},{4,5},{5,4},{6,7},{7,6},{8,9},{9,8},{10,11... | collective-permute-start | bytes 1572872 | tf_op jit(solution)/shard_map/ppermute | solution.py:37
  87.3 2.3 %collective-permute-start.17 = (f32[2,512,128]{2,1,0:T(8,128)S(1)}, f32[2,512,128]{2,1,0:T(8,128)S(1)}, u32[]{:S(2)}, u32[]{:S(2)}) collective-permute-start(f32[2,512,128]{2,1,0:T(8,128)S(1)} %collective-permute-done.10.refs_4_), channel_id=1, source_target_pairs={{0,1},{1,0},{2,3},{3,2},{4,5},{5,4},{6,7},{7,6},{8,9},{9,8},{10,11... | collective-permute-start | bytes 1572872 | tf_op jit(solution)/shard_map/ppermute | solution.py:37
  87.3 14.7 %collective-permute-start.8 = (f32[2,512,128]{2,1,0:T(8,128)}, f32[2,512,128]{2,1,0:T(8,128)S(1)}, u32[]{:S(2)}, u32[]{:S(2)}) collective-permute-start(f32[2,512,128]{2,1,0:T(8,128)} %bitcast.38), channel_id=1, source_target_pairs={{0,4},{1,5},{2,6},{3,7},{4,0},{5,1},{6,2},{7,3},{8,12},{9,13},{10,... | collective-permute-start | bytes 1572872 | tf_op jit(solution)/shard_map/ppermute | solution.py:46
  102.0 2.9 %copy-start.8 = (f32[2,512,128]{2,1,0:T(8,128)}, f32[2,512,128]{2,1,0:T(8,128)S(1)}, u32[]{:S(2)}) copy-start(f32[2,512,128]{2,1,0:T(8,128)S(1)} %collective-permute-done.8.refs_3_) | copy-start | bytes 1572868
  102.0 2.9 %collective-permute-start.18 = (f32[2,512,128]{2,1,0:T(8,128)S(1)}, f32[2,512,128]{2,1,0:T(8,128)S(1)}, u32[]{:S(2)}, u32[]{:S(2)}) collective-permute-start(f32[2,512,128]{2,1,0:T(8,128)S(1)} %collective-permute-done.8.refs_3_), channel_id=1, source_target_pairs={{0,1},{1,0},{2,3},{3,2},{4,5},{5,4},{6,7},{7,6},{8,9},{9,8},{10,11... | collective-permute-start | bytes 1572872 | tf_op jit(solution)/shard_map/ppermute | solution.py:37
  (6 other events, 4.7 us)
where the time goes:
time: 112 us; the launch traced here: 111 us
  Pallas kernels  42.5 us (38%)
  waiting for transfers between devices  28.2 us (25%)
  starting transfers between devices  27.5 us (25%)
  local copies, waits for them, and re-layouts  6.87 us (6%)
  other arithmetic  5.66 us (5%)
    pallas_call x4, Pallas kernels, bin_chips(): pl.pallas_call(lambda *refs: bin_kernel(*refs, count=count, fresh=fresh),...  28.1 us
    ppermute x3, waiting for transfers between devices, along_z(): return lax.ppermute(value, 'rows', pairs)  19.5 us
    pallas_call x1, Pallas kernels, prep(): pl.pallas_call(prep_kernel, grid_spec=pltpu.PrefetchScalarGridSpec(num_sc...  9.08 us
    ppermute x7, starting transfers between devices, to_chip(): return lax.ppermute(value, 'bundle', pairs)  8.61 us
    ppermute x9, starting transfers between devices, swap_cores(): return lax.ppermute(value, 'bundle', [(i, i ^ 1) for i in range(16)])  7.8 us
    ppermute x7, waiting for transfers between devices, to_chip(): return lax.ppermute(value, 'bundle', pairs)  7.68 us
    all_to_all x1, starting transfers between devices, step(): lax.all_to_all(copies, AXES, split_axis=0, concat_axis=0, axis_index_grou...  6.92 us
    unnamed x36, local copies, waits for them, and re-layouts  4.34 us
  transfers between devices with their start and end apart: 20, of which 5 were waited for; matrix products, arithmetic and copies ran while one was open for 6% of the time, Pallas kernels for 34%

commit v1 on v0

--- a/solution.py
+++ b/solution.py
@@ -13,8 +13,7 @@
 SPAN = 256
 FEATURES = 4096
 CHIPS = 8
-ORDER = ((0, 0), (1, 0), (0, 1), (0, 3), (1, 1), (1, 3), (1, 2), (0, 2))
-BATCHES = (3, 2, 2, 1)
+PHASES = (((1, 0), (0, 2)), ((1, 1), (0, 3)), ((1, 3), (0, 1)), ((1, 2),))
 GROUP = 1024
 SUB = 256
 
@@ -176,20 +175,23 @@
     )(*parts)
 
 
-def bin_kernel(row_ref, table_ref, offset_ref, *refs, count, fresh):
+def bin_kernel(row_ref, table_hbm, offset_ref, *refs, count, fresh, first):
     own, swapped = refs[:count], refs[count : 2 * count]
-    out_ref, stage, turned, result, in_sems, out_sems = refs[2 * count + (0 if fresh else 1) :]
+    out_ref, stage, turned, result, table_ref, in_sems, out_sems = refs[2 * count + (0 if fresh else 1) :]
 
     def take(i, side):
         source = own[i].at[0] if side == 0 else swapped[i].at[1]
         return pltpu.make_async_copy(source, stage.at[2 * i + side], in_sems.at[2 * i + side])
 
     def give(part):
-        rows = pl.ds(pl.multiple_of(row_ref[part], 256), 256)
+        rows = pl.ds(pl.multiple_of(row_ref[first + part], 256), 256)
         return pltpu.make_async_copy(result.at[part], out_ref.at[rows, :], out_sems.at[part])
 
+    tables = pltpu.make_async_copy(table_hbm, table_ref, in_sems.at[2 * count])
     for i in range(count):
         take(i, 0).start()
+        if i == 0:
+            tables.start()
         take(i, 1).start()
 
     def arrive(part):
@@ -201,6 +203,7 @@
 
     arrive(0)
     turn(0, 0)
+    tables.wait()
     last = 8 * count - 1
 
     def one_tile(t, carry):
@@ -231,16 +234,16 @@
         give(part).wait()
 
 
-def bin_chips(row, table, offset, own, swapped, out):
+def bin_chips(row, first, table, offset, own, swapped, out):
     count, fresh = len(own), out is None
     anywhere = pl.BlockSpec(memory_space=pltpu.HBM)
     return pl.pallas_call(
-        lambda *refs: bin_kernel(*refs, count=count, fresh=fresh),
+        lambda *refs: bin_kernel(*refs, count=count, fresh=fresh, first=first),
         grid_spec=pltpu.PrefetchScalarGridSpec(
             num_scalar_prefetch=1,
             grid=(1,),
             in_specs=[
-                pl.BlockSpec((EDGES, SPAN), lambda g, s: (0, 0)),
+                anywhere,
                 pl.BlockSpec((1, SPAN), lambda g, s: (0, 0)),
             ]
             + [anywhere] * (2 * count + (0 if fresh else 1)),
@@ -249,7 +252,8 @@
                 pltpu.VMEM((2 * count, 512, 128), jnp.float32),
                 pltpu.VMEM((2, 128, 128), jnp.float32),
                 pltpu.VMEM((2 * count, 256, SPAN), jnp.int32),
-                pltpu.SemaphoreType.DMA((2 * count,)),
+                pltpu.VMEM((EDGES, SPAN), jnp.float32),
+                pltpu.SemaphoreType.DMA((2 * count + 1,)),
                 pltpu.SemaphoreType.DMA((2 * count,)),
             ],
         ),
@@ -272,10 +276,17 @@
     chip = (owner // 8 ^ y_low) * SIDE + ((owner // 2) % SIDE - x) % SIDE
     spot = chip * 512 + (owner % 2 ^ core) * 256 + inside
     sent = [value.reshape(2, 512, 128) for value in prep(spot, raw_values)]
-    arrived = []
-    for dy, dx in ORDER:
-        value = sent[dy * SIDE + dx]
-        arrived.append(to_chip(value, dy, dx) if dy + dx else value)
+
+    def carry(chips, values):
+        arrived = []
+        for (dy, dx), value in zip(chips, values):
+            arrived.append(to_chip(value, dy, dx))
+        return arrived
+
+    def picked(phase):
+        return [sent[dy * SIDE + dx] for dy, dx in PHASES[phase]]
+
+    arrived = [carry(PHASES[0], picked(0)), carry(PHASES[1], picked(1))]
 
     wanted = bundle * SPAN + jnp.arange(SPAN, dtype=jnp.int32)
     named = feature_column[None, :] == wanted[:, None]
@@ -287,28 +298,35 @@
     line = jnp.where(device % 2 == core, line, line + 512)
     line = jnp.where((device // 16) % SIDE == z, line, 1024)
     part = choose(line, mine, swap_cores(mine))
-    groups, done = [], 0
-    for count in BATCHES:
-        groups.append((ORDER[done : done + count], arrived[done : done + count]))
-        done += count
-    near, *turned = [along_z(part, step) for step in (1, 3, 2)]
-    *own, near = lax.optimization_barrier((*groups[0][1], near))
-    swapped = [swap_cores(value) for value in own]
-    table = make_table([part, near] + turned)
-    *following, table = lax.optimization_barrier((*groups[1][1], table))
-    out = None
-    for n, (chips, later) in enumerate(groups):
-        if n == 1:
-            own, swapped = following, [swap_cores(value) for value in following]
-        elif n > 1:
-            *own, out = lax.optimization_barrier((*later, out))
-            swapped = [swap_cores(value) for value in own]
-        row = []
-        for dy, dx in chips:
-            base = ((y_low ^ dy) * SIDE + (x - dx) % SIDE) * 512
-            row += [base + core * 256, base + (1 - core) * 256]
-        row = jnp.stack(row).astype(jnp.int32)
-        out = bin_chips(row, table, offset[None], own, swapped, out)
+    turned = []
+    for step in (1, 3, 2):
+        turned.append(along_z(part, step))
+    for phase in (2, 3):
+        *values, arrived[phase - 2] = lax.optimization_barrier((*picked(phase), arrived[phase - 2]))
+        arrived.append(carry(PHASES[phase], values))
+    table = make_table([part] + turned)
+    groups = [((0, 0), *PHASES[0])] + list(PHASES[1:])
+    arrived[0] = [sent[0]] + arrived[0]
+    row = []
+    for dy, dx in sum(map(tuple, groups), ()):
+        base = ((y_low ^ dy) * SIDE + (x - dx) % SIDE) * 512
+        row += [base + core * 256, base + (1 - core) * 256]
+    row = jnp.stack(row).astype(jnp.int32)
+    swapped = []
+    for n in range(2):
+        swapped.append([])
+        for value in arrived[n]:
+            swapped[n].append(swap_cores(value))
+    out, first = None, 0
+    for n in range(4):
+        own, other = arrived[n], swapped[n]
+        if n < 2:
+            out = bin_chips(row, first, table, offset[None], own, other, out)
+            arrived[n + 2], out = lax.optimization_barrier((arrived[n + 2], out))
+            swapped.append([swap_cores(value) for value in arrived[n + 2]])
+        else:
+            out = bin_chips(row, first, table, offset[None], own, other, out)
+        first += 2 * len(own)
     return out
 
 

time: 112 us -> 103 us (0.920)
  the two profiles are of different devices: /device:TPU:3 before, /device:TPU:1 now
where the time goes in v1:
time: 103 us
  Pallas kernels  41.5 us (40%)
  starting transfers between devices  38.8 us (38%)
  waiting for transfers between devices  13.3 us (13%)
  local copies, waits for them, and re-layouts  5.04 us (5%)
  other arithmetic  3.91 us (4%)
    pallas_call x4, Pallas kernels, bin_chips(): pl.pallas_call(lambda *refs: bin_kernel(*refs, count=count, fresh=fresh,...  27.1 us
    ppermute x7, starting transfers between devices, to_chip(): return lax.ppermute(value, 'bundle', pairs)  13 us
    ppermute x9, starting transfers between devices, swap_cores(): return lax.ppermute(value, 'bundle', [(i, i ^ 1) for i in range(16)])  11.9 us
    pallas_call x1, Pallas kernels, prep(): pl.pallas_call(prep_kernel, grid_spec=pltpu.PrefetchScalarGridSpec(num_sc...  9.02 us
    all_to_all x1, starting transfers between devices, step(): lax.all_to_all(copies, AXES, split_axis=0, concat_axis=0, axis_index_grou...  7.57 us
    ppermute x7, waiting for transfers between devices, to_chip(): return lax.ppermute(value, 'bundle', pairs)  7.43 us
    ppermute x3, starting transfers between devices, along_z(): return lax.ppermute(value, 'rows', pairs)  6.27 us
    ppermute x3, waiting for transfers between devices, along_z(): return lax.ppermute(value, 'rows', pairs)  5.86 us
  transfers between devices with their start and end apart: 20, of which 5 were waited for; matrix products, arithmetic and copies ran while one was open for 4% of the time, Pallas kernels for 36%

profile of v1, /device:TPU:1, one launch (start us, length us, event | category | flops | bytes accessed | tf_op | source)
XLA Modules:
  0.0 102.7 jit_solution(13287137979321133167)
XLA Ops:
  0.0 0.8 pad.4
  1.1 0.9 broadcast_in_dim.43
  1.9 7.6 %all-to-all-start = ((f32[16,32,256]{2,1,0:T(8,128)}), f32[16,32,256]{2,1,0:T(8,128)S(1)}, u32[]{:S(2)}, u32[]{:S(2)}) async-start(f32[16,32,256]{2,1,0:T(8,128)} %broadcast_in_dim.43), calls=%async_computation | async-start | bytes 1048576 | tf_op jit(solution)/shard_map/all_to_all | solution.py:271
  9.6 1.4 %fusion.8.spot_ref = s32[4096]{0:T(1024)} fusion(s32[4096]{0:T(1024)} %param.6, s32[]{:T(128)S(6)} %select_n.132, s32[]{:T(128)S(6)} %select_n.130, s32[]{:T(128)S(6)} %select_n.128), kind=kLoop, calls=%fused_computation.29 | loop fusion | flops 323584 | bytes 32780 | tf_op jit(solution)/shard_map/add | solution.py:277
  10.9 9.0 %prep.1 = (f32[512,2,128]{2,1,0:T(2,128)}, f32[512,2,128]{2,1,0:T(2,128)}, f32[512,2,128]{2,1,0:T(2,128)}, f32[512,2,128]{2,1,0:T(2,128)}, f32[512,2,128]{2,1,0:...) custom-call(s32[4096]{0:T(1024)} %fusion.8.spot_ref, f32[256,4096]{1,0:T(8,128)} %raw_ref.1), custom_call_target="tpu_custom_call" | custom-call | tf_op jit(solution)/shard_map/prep/pallas_call | solution.py:123
  20.0 1.4 %collective-permute-start.9 = (f32[2,512,128]{2,1,0:T(8,128)}, f32[2,512,128]{2,1,0:T(8,128)S(1)}, u32[]{:S(2)}, u32[]{:S(2)}) collective-permute-start(f32[2,512,128]{2,1,0:T(8,128)} %bitcast.44), channel_id=1, source_target_pairs={{0,8},{1,9},{2,10},{3,11},{4,12},{5,13},{6,14},{7,15},{8,0},{9,1},... | collective-permute-start | bytes 1572872 | tf_op jit(solution)/shard_map/ppermute | solution.py:45
  21.4 2.7 %collective-permute-start.10 = (f32[2,512,128]{2,1,0:T(8,128)}, f32[2,512,128]{2,1,0:T(8,128)S(1)}, u32[]{:S(2)}, u32[]{:S(2)}) collective-permute-start(f32[2,512,128]{2,1,0:T(8,128)} %bitcast.43), channel_id=1, source_target_pairs={{0,4},{1,5},{2,6},{3,7},{4,0},{5,1},{6,2},{7,3},{8,12},{9,13},{10,... | collective-permute-start | bytes 1572872 | tf_op jit(solution)/shard_map/ppermute | solution.py:45
  24.1 1.8 %collective-permute-start = (f32[512,256]{1,0:T(8,128)S(1)}, f32[512,256]{1,0:T(8,128)}, u32[]{:S(2)}, u32[]{:S(2)}) collective-permute-start(f32[512,256]{1,0:T(8,128)S(1)} %bitcast.29), channel_id=1, source_target_pairs={{0,1},{1,0},{2,3},{3,2},{4,5},{5,4},{6,7},{7,6},{8,9},{9,8},{10,11... | collective-permute-start | bytes 1572872 | tf_op jit(solution)/shard_map/ppermute | solution.py:36
  26.1 2.4 %collective-permute-start.5 = (f32[2,512,128]{2,1,0:T(8,128)}, f32[2,512,128]{2,1,0:T(8,128)S(1)}, u32[]{:S(2)}, u32[]{:S(2)}) collective-permute-start(f32[2,512,128]{2,1,0:T(8,128)} %bitcast.41), channel_id=1, source_target_pairs={{0,6},{1,7},{2,0},{3,1},{4,2},{5,3},{6,4},{7,5},{8,14},{9,15},{10,... | collective-permute-start | bytes 1572872 | tf_op jit(solution)/shard_map/ppermute | solution.py:45
  28.5 4.4 %collective-permute-done.9.refs_4_ = f32[2,512,128]{2,1,0:T(8,128)S(1)} collective-permute-done((f32[2,512,128]{2,1,0:T(8,128)}, f32[2,512,128]{2,1,0:T(8,128)S(1)}, u32[]{:S(2)}, u32[]{:S(2)}) %collective-permute-start.9) | collective-permute-done | bytes 524320 | tf_op jit(solution)/shard_map/ppermute | solution.py:45
  32.9 1.8 %collective-permute-start.13 = (f32[2,512,128]{2,1,0:T(8,128)}, f32[2,512,128]{2,1,0:T(8,128)S(1)}, u32[]{:S(2)}, u32[]{:S(2)}) collective-permute-start(f32[2,512,128]{2,1,0:T(8,128)} %bitcast.31), channel_id=1, source_target_pairs={{0,1},{1,0},{2,3},{3,2},{4,5},{5,4},{6,7},{7,6},{8,9},{9,8},{10,11... | collective-permute-start | bytes 1572872 | tf_op jit(solution)/shard_map/ppermute | solution.py:36
  35.1 4.4 %collective-permute-start.14 = (f32[2,512,128]{2,1,0:T(8,128)S(1)}, f32[2,512,128]{2,1,0:T(8,128)}, u32[]{:S(2)}, u32[]{:S(2)}) collective-permute-start(f32[2,512,128]{2,1,0:T(8,128)S(1)} %collective-permute-done.9.refs_4_), channel_id=1, source_target_pairs={{0,1},{1,0},{2,3},{3,2},{4,5},{5,4},{6,7},{7,6},{8,9},{9,8},{10,11... | collective-permute-start | bytes 1572872 | tf_op jit(solution)/shard_map/ppermute | solution.py:36
  39.5 1.9 %fusion.1 = (s32[256]{0:T(256)}, s32[256]{0:T(256)S(1)}) fusion(s32[4096]{0:T(1024)S(1)} %copy-done.12, s32[4096]{0:T(1024)S(1)} %copy-done.11, s32[256]{0:T(256)S(1)} %iota_add_fusion), kind=kLoop, calls=%fused_computation.3 | loop fusion | flops 5242368 | bytes 35840 | tf_op jit(solution)/shard_map/reduce_max | solution.py:294
  42.1 3.3 %choose.1.a_ref = f32[256,256]{1,0:T(8,128)} custom-call(s32[256]{0:T(256)} %compare_select_fusion.9.row_ref, f32[512,256]{1,0:T(8,128)} %bitcast.30, f32[512,256]{1,0:T(8,128)} %collective-permute-done.other_ref), custom_call_target="tpu_custom_call" | custom-call | tf_op jit(solution)/shard_map/choose/pallas_call | solution.py:153
  45.4 2.7 %collective-permute-done.4.refs_3_ = f32[2,512,128]{2,1,0:T(8,128)S(1)} collective-permute-done((f32[2,512,128]{2,1,0:T(8,128)}, f32[2,512,128]{2,1,0:T(8,128)S(1)}, u32[]{:S(2)}, u32[]{:S(2)}) %collective-permute-start.4) | collective-permute-done | bytes 524320 | tf_op jit(solution)/shard_map/ppermute | solution.py:45
  48.1 3.6 %collective-permute-start.3 = (f32[256,256]{1,0:T(8,128)}, f32[256,256]{1,0:T(8,128)S(1)}, u32[]{:S(2)}, u32[]{:S(2)}) collective-permute-start(f32[256,256]{1,0:T(8,128)} %choose.1.a_ref), channel_id=1, source_target_pairs={{32,0},{48,16},{0,32},{16,48},{96,64},{112,80},{64,96},{80,112},{3... | collective-permute-start | bytes 786440 | tf_op jit(solution)/shard_map/ppermute | solution.py:32
  51.7 0.7 collective-permute-start.2
  52.4 1.9 %collective-permute-start.1 = (f32[256,256]{1,0:T(8,128)}, f32[256,256]{1,0:T(8,128)}, u32[]{:S(2)}, u32[]{:S(2)}) collective-permute-start(f32[256,256]{1,0:T(8,128)} %choose.1.a_ref), channel_id=1, source_target_pairs={{16,0},{32,16},{48,32},{0,48},{80,64},{96,80},{112,96},{64,112},{1... | collective-permute-start | bytes 786440 | tf_op jit(solution)/shard_map/ppermute | solution.py:32
  54.4 2.4 %collective-permute-start.12 = (f32[2,512,128]{2,1,0:T(8,128)}, f32[2,512,128]{2,1,0:T(8,128)}, u32[]{:S(2)}, u32[]{:S(2)}) collective-permute-start(f32[2,512,128]{2,1,0:T(8,128)} %bitcast.39), channel_id=1, source_target_pairs={{0,2},{1,3},{2,4},{3,5},{4,6},{5,7},{6,0},{7,1},{8,10},{9,11},{10,... | collective-permute-start | bytes 1572872 | tf_op jit(solution)/shard_map/ppermute | solution.py:45
  56.9 1.3 %collective-permute-done.3.d_ref = f32[256,256]{1,0:T(8,128)S(1)} collective-permute-done((f32[256,256]{1,0:T(8,128)}, f32[256,256]{1,0:T(8,128)S(1)}, u32[]{:S(2)}, u32[]{:S(2)}) %collective-permute-start.3) | collective-permute-done | bytes 262176 | tf_op jit(solution)/shard_map/ppermute | solution.py:32
  58.2 1.6 %collective-permute-start.7 = (f32[2,512,128]{2,1,0:T(8,128)S(1)}, f32[2,512,128]{2,1,0:T(8,128)}, u32[]{:S(2)}, u32[]{:S(2)}) collective-permute-start(f32[2,512,128]{2,1,0:T(8,128)S(1)} %collective-permute-done.4.refs_3_), channel_id=1, source_target_pairs={{0,1},{1,0},{2,3},{3,2},{4,5},{5,4},{6,7},{7,6},{8,9},{9,8},{10,11... | collective-permute-start | bytes 1572872 | tf_op jit(solution)/shard_map/ppermute | solution.py:36
  59.8 4.6 %collective-permute-done.2.c_ref = f32[256,256]{1,0:T(8,128)} collective-permute-done((f32[256,256]{1,0:T(8,128)}, f32[256,256]{1,0:T(8,128)}, u32[]{:S(2)}, u32[]{:S(2)}) %collective-permute-start.2) | collective-permute-done | bytes 262176 | tf_op jit(solution)/shard_map/ppermute | solution.py:32
  64.9 3.8 %collective-permute-start.6 = (f32[2,512,128]{2,1,0:T(8,128)}, f32[2,512,128]{2,1,0:T(8,128)}, u32[]{:S(2)}, u32[]{:S(2)}) collective-permute-start(f32[2,512,128]{2,1,0:T(8,128)} %bitcast.38), channel_id=1, source_target_pairs={{0,12},{1,13},{2,14},{3,15},{4,8},{5,9},{6,10},{7,11},{8,4},{9,5},... | collective-permute-start | bytes 1572872 | tf_op jit(solution)/shard_map/ppermute | solution.py:45
  69.3 2.1 %make_table.1.refs_1_ = f32[256,256]{1,0:T(8,128)} custom-call(f32[256,256]{1,0:T(8,128)} %choose.1.a_ref, f32[256,256]{1,0:T(8,128)} %collective-permute-done.1.b_ref, f32[256,256]{1,0:T(8,128)} %collective-permute-done.2.c_ref, f32[256,256]{1,0:T(8,128)} %copy-done.10), custom_call_target="tpu_custom_call" | custom-call | tf_op jit(solution)/shard_map/make_table/pallas_call | solution.py:173
  71.4 8.6 %shard_map.46.refs_7_ = s32[4096,256]{1,0:T(8,128)} custom-call(s32[16]{0:T(128)} %stack.67.refs_0_, f32[256,256]{1,0:T(8,128)} %make_table.1.refs_1_, s32[1,256]{1,0:T(1,128)} %bitcast.34, f32[2,512,128]{2,1,0:T(8,128)} %bitcast.32, f32[2,512,128]{2,1,0:T(8,128)} %copy-done.3, f32[2,512,128]{2,1,0:T(8,128)} %copy-done.4, f32[2,512,128]{2,1,0:T(8,128)} %copy-done.5, ...), custom_call_target="tpu_custom_call" | custom-call | tf_op jit(solution)/shard_map/pallas_call | solution.py:240
  80.0 1.1 %collective-permute-start.17 = (f32[2,512,128]{2,1,0:T(8,128)S(1)}, f32[2,512,128]{2,1,0:T(8,128)S(1)}, u32[]{:S(2)}, u32[]{:S(2)}) collective-permute-start(f32[2,512,128]{2,1,0:T(8,128)S(1)} %collective-permute-done.11.refs_3_), channel_id=1, source_target_pairs={{0,1},{1,0},{2,3},{3,2},{4,5},{5,4},{6,7},{7,6},{8,9},{9,8},{10,11... | collective-permute-start | bytes 1572872 | tf_op jit(solution)/shard_map/ppermute | solution.py:36
  81.3 6.8 %shard_map.47.refs_7_ = s32[4096,256]{1,0:T(8,128)} custom-call(s32[16]{0:T(128)} %stack.67.refs_0_, f32[256,256]{1,0:T(8,128)} %make_table.1.refs_1_, s32[1,256]{1,0:T(1,128)} %bitcast.35, f32[2,512,128]{2,1,0:T(8,128)} %copy-done.1, f32[2,512,128]{2,1,0:T(8,128)} %copy-done.2, ...), custom_call_target="tpu_custom_call", output_to_operand_aliasing={{}: (7, {})} | custom-call | tf_op jit(solution)/shard_map/pallas_call | solution.py:240
  88.6 0.8 copy-done.7
  89.4 0.8 copy-done.8
  90.2 6.8 %shard_map.48.refs_5_ = s32[4096,256]{1,0:T(8,128)} custom-call(s32[16]{0:T(128)} %stack.67.refs_0_, f32[256,256]{1,0:T(8,128)} %make_table.1.refs_1_, s32[1,256]{1,0:T(1,128)} %bitcast.36, f32[2,512,128]{2,1,0:T(8,128)} %copy-done.6, f32[2,512,128]{2,1,0:T(8,128)} %collective-permute-done.12.refs_4_, ...), custom_call_target="tpu_custom_call", output_to_operand_aliasing={{}: (7, {})} | custom-call | tf_op jit(solution)/shard_map/pallas_call | solution.py:240
  97.0 0.8 copy-done.9
  97.8 4.9 %shard_map.49 = s32[4096,256]{1,0:T(8,128)} custom-call(s32[16]{0:T(128)} %stack.67.refs_0_, f32[256,256]{1,0:T(8,128)} %make_table.1.refs_1_, s32[1,256]{1,0:T(1,128)} %bitcast.37, f32[2,512,128]{2,1,0:T(8,128)} %collective-permute-done.6.refs_3_, f32[2,512,128]{2,1,0:T(8,128)} %copy-done.9, ...), custom_call_target="tpu_custom_call", output_to_operand_aliasing={{}: (5, {})} | custom-call | tf_op jit(solution)/shard_map/pallas_call | solution.py:240
  (51 shorter events, 3.5 us)
Async XLA Ops:
  0.0 39.5 %copy-start.11 = (s32[4096]{0:T(1024)S(1)}, s32[4096]{0:T(1024)}, u32[]{:S(2)}) copy-start(s32[4096]{0:T(1024)} %param.6) | copy-start | bytes 49156
  0.0 39.5 %copy-start.12 = (s32[4096]{0:T(1024)S(1)}, s32[4096]{0:T(1024)}, u32[]{:S(2)}) copy-start(s32[4096]{0:T(1024)} %param.7) | copy-start | bytes 49156
  1.9 22.1 %all-to-all-start = ((f32[16,32,256]{2,1,0:T(8,128)}), f32[16,32,256]{2,1,0:T(8,128)S(1)}, u32[]{:S(2)}, u32[]{:S(2)}) async-start(f32[16,32,256]{2,1,0:T(8,128)} %broadcast_in_dim.43), calls=%async_computation | async-start | bytes 1048576 | tf_op jit(solution)/shard_map/all_to_all | solution.py:271
  20.0 12.9 %collective-permute-start.9 = (f32[2,512,128]{2,1,0:T(8,128)}, f32[2,512,128]{2,1,0:T(8,128)S(1)}, u32[]{:S(2)}, u32[]{:S(2)}) collective-permute-start(f32[2,512,128]{2,1,0:T(8,128)} %bitcast.44), channel_id=1, source_target_pairs={{0,8},{1,9},{2,10},{3,11},{4,12},{5,13},{6,14},{7,15},{8,0},{9,1},... | collective-permute-start | bytes 1572872 | tf_op jit(solution)/shard_map/ppermute | solution.py:45
  21.4 13.7 %collective-permute-start.10 = (f32[2,512,128]{2,1,0:T(8,128)}, f32[2,512,128]{2,1,0:T(8,128)S(1)}, u32[]{:S(2)}, u32[]{:S(2)}) collective-permute-start(f32[2,512,128]{2,1,0:T(8,128)} %bitcast.43), channel_id=1, source_target_pairs={{0,4},{1,5},{2,6},{3,7},{4,0},{5,1},{6,2},{7,3},{8,12},{9,13},{10,... | collective-permute-start | bytes 1572872 | tf_op jit(solution)/shard_map/ppermute | solution.py:45
  24.1 18.0 %copy-start = (f32[16,32,256]{2,1,0:T(8,128)}, f32[16,32,256]{2,1,0:T(8,128)S(1)}, u32[]{:S(2)}) copy-start(f32[16,32,256]{2,1,0:T(8,128)S(1)} %all-to-all-done) | copy-start | bytes 1572868
  24.1 15.4 %collective-permute-start = (f32[512,256]{1,0:T(8,128)S(1)}, f32[512,256]{1,0:T(8,128)}, u32[]{:S(2)}, u32[]{:S(2)}) collective-permute-start(f32[512,256]{1,0:T(8,128)S(1)} %bitcast.29), channel_id=1, source_target_pairs={{0,1},{1,0},{2,3},{3,2},{4,5},{5,4},{6,7},{7,6},{8,9},{9,8},{10,11... | collective-permute-start | bytes 1572872 | tf_op jit(solution)/shard_map/ppermute | solution.py:36
  25.9 22.2 %collective-permute-start.4 = (f32[2,512,128]{2,1,0:T(8,128)}, f32[2,512,128]{2,1,0:T(8,128)S(1)}, u32[]{:S(2)}, u32[]{:S(2)}) collective-permute-start(f32[2,512,128]{2,1,0:T(8,128)} %bitcast.42), channel_id=1, source_target_pairs={{0,10},{1,11},{2,12},{3,13},{4,14},{5,15},{6,8},{7,9},{8,2},{9,3},... | collective-permute-start | bytes 1572872 | tf_op jit(solution)/shard_map/ppermute | solution.py:45
  26.1 25.5 %collective-permute-start.5 = (f32[2,512,128]{2,1,0:T(8,128)}, f32[2,512,128]{2,1,0:T(8,128)S(1)}, u32[]{:S(2)}, u32[]{:S(2)}) collective-permute-start(f32[2,512,128]{2,1,0:T(8,128)} %bitcast.41), channel_id=1, source_target_pairs={{0,6},{1,7},{2,0},{3,1},{4,2},{5,3},{6,4},{7,5},{8,14},{9,15},{10,... | collective-permute-start | bytes 1572872 | tf_op jit(solution)/shard_map/ppermute | solution.py:45
  32.9 38.5 %copy-start.3 = (f32[2,512,128]{2,1,0:T(8,128)}, f32[2,512,128]{2,1,0:T(8,128)S(1)}, u32[]{:S(2)}) copy-start(f32[2,512,128]{2,1,0:T(8,128)S(1)} %collective-permute-done.9.refs_4_) | copy-start | bytes 1572868
  32.9 19.5 %collective-permute-start.13 = (f32[2,512,128]{2,1,0:T(8,128)}, f32[2,512,128]{2,1,0:T(8,128)S(1)}, u32[]{:S(2)}, u32[]{:S(2)}) collective-permute-start(f32[2,512,128]{2,1,0:T(8,128)} %bitcast.31), channel_id=1, source_target_pairs={{0,1},{1,0},{2,3},{3,2},{4,5},{5,4},{6,7},{7,6},{8,9},{9,8},{10,11... | collective-permute-start | bytes 1572872 | tf_op jit(solution)/shard_map/ppermute | solution.py:36
  35.1 36.3 %copy-start.4 = (f32[2,512,128]{2,1,0:T(8,128)}, f32[2,512,128]{2,1,0:T(8,128)S(1)}, u32[]{:S(2)}) copy-start(f32[2,512,128]{2,1,0:T(8,128)S(1)} %collective-permute-done.10.refs_5_) | copy-start | bytes 1572868
  35.1 19.3 %collective-permute-start.14 = (f32[2,512,128]{2,1,0:T(8,128)S(1)}, f32[2,512,128]{2,1,0:T(8,128)}, u32[]{:S(2)}, u32[]{:S(2)}) collective-permute-start(f32[2,512,128]{2,1,0:T(8,128)S(1)} %collective-permute-done.9.refs_4_), channel_id=1, source_target_pairs={{0,1},{1,0},{2,3},{3,2},{4,5},{5,4},{6,7},{7,6},{8,9},{9,8},{10,11... | collective-permute-start | bytes 1572872 | tf_op jit(solution)/shard_map/ppermute | solution.py:36
  39.5 15.0 %collective-permute-start.15 = (f32[2,512,128]{2,1,0:T(8,128)S(1)}, f32[2,512,128]{2,1,0:T(8,128)}, u32[]{:S(2)}, u32[]{:S(2)}) collective-permute-start(f32[2,512,128]{2,1,0:T(8,128)S(1)} %collective-permute-done.10.refs_5_), channel_id=1, source_target_pairs={{0,1},{1,0},{2,3},{3,2},{4,5},{5,4},{6,7},{7,6},{8,9},{9,8},{10,11... | collective-permute-start | bytes 1572872 | tf_op jit(solution)/shard_map/ppermute | solution.py:36
  48.1 31.9 %copy-start.1 = (f32[2,512,128]{2,1,0:T(8,128)}, f32[2,512,128]{2,1,0:T(8,128)S(1)}, u32[]{:S(2)}) copy-start(f32[2,512,128]{2,1,0:T(8,128)S(1)} %collective-permute-done.4.refs_3_) | copy-start | bytes 1572868
  48.1 10.1 %collective-permute-start.3 = (f32[256,256]{1,0:T(8,128)}, f32[256,256]{1,0:T(8,128)S(1)}, u32[]{:S(2)}, u32[]{:S(2)}) collective-permute-start(f32[256,256]{1,0:T(8,128)} %choose.1.a_ref), channel_id=1, source_target_pairs={{32,0},{48,16},{0,32},{16,48},{96,64},{112,80},{64,96},{80,112},{3... | collective-permute-start | bytes 786440 | tf_op jit(solution)/shard_map/ppermute | solution.py:32
  51.7 28.3 %copy-start.2 = (f32[2,512,128]{2,1,0:T(8,128)}, f32[2,512,128]{2,1,0:T(8,128)S(1)}, u32[]{:S(2)}) copy-start(f32[2,512,128]{2,1,0:T(8,128)S(1)} %collective-permute-done.5.refs_4_) | copy-start | bytes 1572868
  51.7 12.7 %collective-permute-start.2 = (f32[256,256]{1,0:T(8,128)}, f32[256,256]{1,0:T(8,128)}, u32[]{:S(2)}, u32[]{:S(2)}) collective-permute-start(f32[256,256]{1,0:T(8,128)} %choose.1.a_ref), channel_id=1, source_target_pairs={{48,0},{0,16},{16,32},{32,48},{112,64},{64,80},{80,96},{96,112},{4... | collective-permute-start | bytes 786440 | tf_op jit(solution)/shard_map/ppermute | solution.py:32
  52.4 18.9 %copy-start.5 = (f32[2,512,128]{2,1,0:T(8,128)}, f32[2,512,128]{2,1,0:T(8,128)S(1)}, u32[]{:S(2)}) copy-start(f32[2,512,128]{2,1,0:T(8,128)S(1)} %collective-permute-done.13.refs_6_) | copy-start | bytes 1572868
  52.4 12.4 %collective-permute-start.1 = (f32[256,256]{1,0:T(8,128)}, f32[256,256]{1,0:T(8,128)}, u32[]{:S(2)}, u32[]{:S(2)}) collective-permute-start(f32[256,256]{1,0:T(8,128)} %choose.1.a_ref), channel_id=1, source_target_pairs={{16,0},{32,16},{48,32},{0,48},{80,64},{96,80},{112,96},{64,112},{1... | collective-permute-start | bytes 786440 | tf_op jit(solution)/shard_map/ppermute | solution.py:32
  54.4 25.6 %collective-permute-start.11 = (f32[2,512,128]{2,1,0:T(8,128)}, f32[2,512,128]{2,1,0:T(8,128)S(1)}, u32[]{:S(2)}, u32[]{:S(2)}) collective-permute-start(f32[2,512,128]{2,1,0:T(8,128)} %bitcast.40), channel_id=1, source_target_pairs={{0,14},{1,15},{2,8},{3,9},{4,10},{5,11},{6,12},{7,13},{8,6},{9,7},... | collective-permute-start | bytes 1572872 | tf_op jit(solution)/shard_map/ppermute | solution.py:45
  54.4 25.6 %collective-permute-start.12 = (f32[2,512,128]{2,1,0:T(8,128)}, f32[2,512,128]{2,1,0:T(8,128)}, u32[]{:S(2)}, u32[]{:S(2)}) collective-permute-start(f32[2,512,128]{2,1,0:T(8,128)} %bitcast.39), channel_id=1, source_target_pairs={{0,2},{1,3},{2,4},{3,5},{4,6},{5,7},{6,0},{7,1},{8,10},{9,11},{10,... | collective-permute-start | bytes 1572872 | tf_op jit(solution)/shard_map/ppermute | solution.py:45
  58.2 11.1 %copy-start.10 = (f32[256,256]{1,0:T(8,128)}, f32[256,256]{1,0:T(8,128)S(1)}, u32[]{:S(2)}) copy-start(f32[256,256]{1,0:T(8,128)S(1)} %collective-permute-done.3.d_ref) | copy-start | bytes 786436
  58.2 23.1 %collective-permute-start.7 = (f32[2,512,128]{2,1,0:T(8,128)S(1)}, f32[2,512,128]{2,1,0:T(8,128)}, u32[]{:S(2)}, u32[]{:S(2)}) collective-permute-start(f32[2,512,128]{2,1,0:T(8,128)S(1)} %collective-permute-done.4.refs_3_), channel_id=1, source_target_pairs={{0,1},{1,0},{2,3},{3,2},{4,5},{5,4},{6,7},{7,6},{8,9},{9,8},{10,11... | collective-permute-start | bytes 1572872 | tf_op jit(solution)/shard_map/ppermute | solution.py:36
  64.4 16.9 %collective-permute-start.8 = (f32[2,512,128]{2,1,0:T(8,128)S(1)}, f32[2,512,128]{2,1,0:T(8,128)}, u32[]{:S(2)}, u32[]{:S(2)}) collective-permute-start(f32[2,512,128]{2,1,0:T(8,128)S(1)} %collective-permute-done.5.refs_4_), channel_id=1, source_target_pairs={{0,1},{1,0},{2,3},{3,2},{4,5},{5,4},{6,7},{7,6},{8,9},{9,8},{10,11... | collective-permute-start | bytes 1572872 | tf_op jit(solution)/shard_map/ppermute | solution.py:36
  64.9 23.2 %collective-permute-start.6 = (f32[2,512,128]{2,1,0:T(8,128)}, f32[2,512,128]{2,1,0:T(8,128)}, u32[]{:S(2)}, u32[]{:S(2)}) collective-permute-start(f32[2,512,128]{2,1,0:T(8,128)} %bitcast.38), channel_id=1, source_target_pairs={{0,12},{1,13},{2,14},{3,15},{4,8},{5,9},{6,10},{7,11},{8,4},{9,5},... | collective-permute-start | bytes 1572872 | tf_op jit(solution)/shard_map/ppermute | solution.py:45
  80.0 8.0 %copy-start.6 = (f32[2,512,128]{2,1,0:T(8,128)}, f32[2,512,128]{2,1,0:T(8,128)S(1)}, u32[]{:S(2)}) copy-start(f32[2,512,128]{2,1,0:T(8,128)S(1)} %collective-permute-done.11.refs_3_) | copy-start | bytes 1572868
  80.0 8.5 %collective-permute-start.17 = (f32[2,512,128]{2,1,0:T(8,128)S(1)}, f32[2,512,128]{2,1,0:T(8,128)S(1)}, u32[]{:S(2)}, u32[]{:S(2)}) collective-permute-start(f32[2,512,128]{2,1,0:T(8,128)S(1)} %collective-permute-done.11.refs_3_), channel_id=1, source_target_pairs={{0,1},{1,0},{2,3},{3,2},{4,5},{5,4},{6,7},{7,6},{8,9},{9,8},{10,11... | collective-permute-start | bytes 1572872 | tf_op jit(solution)/shard_map/ppermute | solution.py:36
  81.2 7.4 %collective-permute-start.18 = (f32[2,512,128]{2,1,0:T(8,128)}, f32[2,512,128]{2,1,0:T(8,128)S(1)}, u32[]{:S(2)}, u32[]{:S(2)}) collective-permute-start(f32[2,512,128]{2,1,0:T(8,128)} %collective-permute-done.12.refs_4_), channel_id=1, source_target_pairs={{0,1},{1,0},{2,3},{3,2},{4,5},{5,4},{6,7},{7,6},{8,9},{9,8},{10,11... | collective-permute-start | bytes 1572872 | tf_op jit(solution)/shard_map/ppermute | solution.py:36
  88.1 8.9 %collective-permute-start.16 = (f32[2,512,128]{2,1,0:T(8,128)}, f32[2,512,128]{2,1,0:T(8,128)S(1)}, u32[]{:S(2)}, u32[]{:S(2)}) collective-permute-start(f32[2,512,128]{2,1,0:T(8,128)} %collective-permute-done.6.refs_3_), channel_id=1, source_target_pairs={{0,1},{1,0},{2,3},{3,2},{4,5},{5,4},{6,7},{7,6},{8,9},{9,8},{10,11... | collective-permute-start | bytes 1572872 | tf_op jit(solution)/shard_map/ppermute | solution.py:36
  89.4 0.8 copy-start.8
  97.0 0.8 copy-start.9
  (1 other events, 0.8 us)

commit v2 on v1

--- a/solution.py
+++ b/solution.py
@@ -164,28 +164,40 @@
     )(row, mine, other)
 
 
-def table_kernel(a_ref, b_ref, c_ref, d_ref, out_ref):
+def table_kernel(a_ref, b_ref, c_ref, d_ref, offset_ref, out_ref):
     total = (a_ref[...] + b_ref[...]) + (c_ref[...] + d_ref[...])
-    out_ref[...] = total.T
-
-
-def make_table(parts):
+    turned = total.T
+    line = lax.broadcasted_iota(jnp.int32, turned.shape, 0)
+    out_ref[...] = jnp.where(line == EDGES - 1, offset_ref[...].astype(jnp.float32), turned)
+
+
+def make_table(parts, offset):
     return pl.pallas_call(
         table_kernel, out_shape=jax.ShapeDtypeStruct((EDGES, SPAN), jnp.float32), name="make_table"
-    )(*parts)
-
-
-def bin_kernel(row_ref, table_hbm, offset_ref, *refs, count, fresh, first):
+    )(*parts, offset)
+
+
+def bin_kernel(table_hbm, *refs, chips, fresh):
+    count = len(chips)
     own, swapped = refs[:count], refs[count : 2 * count]
-    out_ref, stage, turned, result, table_ref, in_sems, out_sems = refs[2 * count + (0 if fresh else 1) :]
+    bundle = lax.axis_index("bundle")
+    x, y_low, core = (bundle // 2) % SIDE, bundle // 8, bundle % 2
+    out_ref, stage, turned, result, table_ref, bases, in_sems, out_sems = refs[2 * count + (0 if fresh else 1) :]
 
     def take(i, side):
         source = own[i].at[0] if side == 0 else swapped[i].at[1]
         return pltpu.make_async_copy(source, stage.at[2 * i + side], in_sems.at[2 * i + side])
 
-    def give(part):
-        rows = pl.ds(pl.multiple_of(row_ref[first + part], 256), 256)
-        return pltpu.make_async_copy(result.at[part], out_ref.at[rows, :], out_sems.at[part])
+    for i, (dy, dx) in enumerate(chips):
+        base = (jnp.where(y_low == dy, 0, SIDE) + (x - dx + SIDE) % SIDE) * 512
+        bases[2 * i] = base + core * 256
+        bases[2 * i + 1] = base + (1 - core) * 256
+
+    def give(tile):
+        part = tile // 4
+        rows = pl.ds(pl.multiple_of(bases[part] + (tile % 2) * 128, 128), 128)
+        lanes = pl.ds(pl.multiple_of((tile % 4 // 2) * 128, 128), 128)
+        return pltpu.make_async_copy(result.at[tile], out_ref.at[rows, lanes], out_sems.at[tile])
 
     tables = pltpu.make_async_copy(table_hbm, table_ref, in_sems.at[2 * count])
     for i in range(count):
@@ -214,52 +226,44 @@
             arrive(following // 4)
 
         lanes = pl.ds(pl.multiple_of((t % 4 // 2) * 128, 128), 128)
-        offset = jnp.broadcast_to(offset_ref[:, lanes], (8, 128))
+        offset = jnp.broadcast_to(table_ref[EDGES - 1 :, lanes].astype(jnp.int32), (8, 128))
         for r in range(0, 128, 8):
             below = count_below(
                 turned[t % 2, r : r + 8, :], lambda o: table_ref[8 * o : 8 * o + 8, lanes]
             )
-            rows = pl.ds(pl.multiple_of((t % 2) * 128 + r, 8), 8)
-            result[t // 4, rows, lanes] = below + offset
+            result[t, r : r + 8, :] = below + offset
         turn(following, 1 - t % 2)
-
-        @pl.when(t % 4 == 3)
-        def _():
-            give(t // 4).start()
-
+        give(t).start()
         return carry
 
     lax.fori_loop(0, 8 * count, one_tile, 0)
-    for part in range(2 * count):
-        give(part).wait()
-
-
-def bin_chips(row, first, table, offset, own, swapped, out):
+
+    def drain(t, carry):
+        give(t).wait()
+        return carry
+
+    lax.fori_loop(0, 8 * count, drain, 0)
+
+
+def bin_chips(chips, table, own, swapped, out):
     count, fresh = len(own), out is None
     anywhere = pl.BlockSpec(memory_space=pltpu.HBM)
     return pl.pallas_call(
-        lambda *refs: bin_kernel(*refs, count=count, fresh=fresh, first=first),
-        grid_spec=pltpu.PrefetchScalarGridSpec(
-            num_scalar_prefetch=1,
-            grid=(1,),
-            in_specs=[
-                anywhere,
-                pl.BlockSpec((1, SPAN), lambda g, s: (0, 0)),
-            ]
-            + [anywhere] * (2 * count + (0 if fresh else 1)),
-            out_specs=anywhere,
-            scratch_shapes=[
-                pltpu.VMEM((2 * count, 512, 128), jnp.float32),
-                pltpu.VMEM((2, 128, 128), jnp.float32),
-                pltpu.VMEM((2 * count, 256, SPAN), jnp.int32),
-                pltpu.VMEM((EDGES, SPAN), jnp.float32),
-                pltpu.SemaphoreType.DMA((2 * count + 1,)),
-                pltpu.SemaphoreType.DMA((2 * count,)),
-            ],
-        ),
+        lambda *refs: bin_kernel(*refs, chips=chips, fresh=fresh),
+        in_specs=[anywhere] * (1 + 2 * count + (0 if fresh else 1)),
+        out_specs=anywhere,
+        scratch_shapes=[
+            pltpu.VMEM((2 * count, 512, 128), jnp.float32),
+            pltpu.VMEM((2, 128, 128), jnp.float32),
+            pltpu.VMEM((8 * count, 128, 128), jnp.int32),
+            pltpu.VMEM((EDGES, SPAN), jnp.float32),
+            pltpu.SMEM((2 * count,), jnp.int32),
+            pltpu.SemaphoreType.DMA((2 * count + 1,)),
+            pltpu.SemaphoreType.DMA((8 * count,)),
+        ],
         out_shape=jax.ShapeDtypeStruct((16 * 256, SPAN), jnp.int32),
-        input_output_aliases={} if fresh else {3 + 2 * count: 0},
-    )(row, table, offset, *own, *swapped, *([] if fresh else [out]))
+        input_output_aliases={} if fresh else {1 + 2 * count: 0},
+    )(table, *own, *swapped, *([] if fresh else [out]))
 
 
 def step(raw_values, bin_edges, feature_column, bin_offset):
@@ -301,32 +305,22 @@
     turned = []
     for step in (1, 3, 2):
         turned.append(along_z(part, step))
-    for phase in (2, 3):
-        *values, arrived[phase - 2] = lax.optimization_barrier((*picked(phase), arrived[phase - 2]))
-        arrived.append(carry(PHASES[phase], values))
-    table = make_table([part] + turned)
-    groups = [((0, 0), *PHASES[0])] + list(PHASES[1:])
+    arrived.append(carry(PHASES[2], picked(2)))
+    *values, arrived[1] = lax.optimization_barrier((*picked(3), arrived[1]))
+    arrived.append(carry(PHASES[3], values))
+    table = make_table([part] + turned, offset[None])
     arrived[0] = [sent[0]] + arrived[0]
-    row = []
-    for dy, dx in sum(map(tuple, groups), ()):
-        base = ((y_low ^ dy) * SIDE + (x - dx) % SIDE) * 512
-        row += [base + core * 256, base + (1 - core) * 256]
-    row = jnp.stack(row).astype(jnp.int32)
+    chips = [((0, 0), *PHASES[0])] + list(PHASES[1:])
     swapped = []
     for n in range(2):
         swapped.append([])
         for value in arrived[n]:
             swapped[n].append(swap_cores(value))
-    out, first = None, 0
-    for n in range(4):
-        own, other = arrived[n], swapped[n]
-        if n < 2:
-            out = bin_chips(row, first, table, offset[None], own, other, out)
-            arrived[n + 2], out = lax.optimization_barrier((arrived[n + 2], out))
-            swapped.append([swap_cores(value) for value in arrived[n + 2]])
-        else:
-            out = bin_chips(row, first, table, offset[None], own, other, out)
-        first += 2 * len(own)
+    out = bin_chips(chips[0] + chips[1], table, arrived[0] + arrived[1], swapped[0] + swapped[1], None)
+    for n in (2, 3):
+        arrived[n], out = lax.optimization_barrier((arrived[n], out))
+        swapped.append([swap_cores(value) for value in arrived[n]])
+        out = bin_chips(chips[n], table, arrived[n], swapped[n], out)
     return out
 
 

time: 103 us -> 101 us (0.981)
  waiting for transfers between devices: 13.3 us -> 22 us
  Pallas kernels: 41.5 us -> 35.1 us
  starting transfers between devices: 38.8 us -> 33.8 us
    ppermute x7, waiting for transfers between devices: 7.43 us -> 14.9 us  [to_chip(): return lax.ppermute(value, 'bundle', pairs)]
    pallas_call x4 -> x3, Pallas kernels: 27.1 us -> 20.8 us  [bin_chips(): pl.pallas_call(lambda *refs: bin_kernel(*refs, chips=chips, fresh=fresh),...]
    ppermute x7, starting transfers between devices: 13 us -> 10.3 us  [to_chip(): return lax.ppermute(value, 'bundle', pairs)]
    ppermute x9, starting transfers between devices: 11.9 us -> 9.19 us  [swap_cores(): return lax.ppermute(value, 'bundle', [(i, i ^ 1) for i in range(16)])]
    ppermute x9, waiting for transfers between devices: 0.02 us -> 1.56 us  [swap_cores(): return lax.ppermute(value, 'bundle', [(i, i ^ 1) for i in range(16)])]
    unnamed x26 -> x28, local copies, waits for them, and re-layouts: 2.47 us -> 3.22 us
  transfers between devices with their start and end apart: 20 -> 20, of which waited for: 5 -> 5; matrix products, arithmetic and copies ran while one was open for 4% -> 4% of each run, Pallas kernels for 36% -> 31%
where the time goes in v2:
time: 101 us; the launch traced here: 100 us
  Pallas kernels  35.1 us (35%)
  starting transfers between devices  33.8 us (33%)
  waiting for transfers between devices  22 us (22%)
  local copies, waits for them, and re-layouts  5.13 us (5%)
  other arithmetic  3.89 us (4%)
    pallas_call x3, Pallas kernels, bin_chips(): pl.pallas_call(lambda *refs: bin_kernel(*refs, chips=chips, fresh=fresh),...  20.8 us
    ppermute x7, waiting for transfers between devices, to_chip(): return lax.ppermute(value, 'bundle', pairs)  14.9 us
    ppermute x7, starting transfers between devices, to_chip(): return lax.ppermute(value, 'bundle', pairs)  10.3 us
    ppermute x9, starting transfers between devices, swap_cores(): return lax.ppermute(value, 'bundle', [(i, i ^ 1) for i in range(16)])  9.19 us
    pallas_call x1, Pallas kernels, prep(): pl.pallas_call(prep_kernel, grid_spec=pltpu.PrefetchScalarGridSpec(num_sc...  9.03 us
    all_to_all x1, starting transfers between devices, step(): lax.all_to_all(copies, AXES, split_axis=0, concat_axis=0, axis_index_grou...  7.57 us
    ppermute x3, starting transfers between devices, along_z(): return lax.ppermute(value, 'rows', pairs)  6.72 us
    ppermute x3, waiting for transfers between devices, along_z(): return lax.ppermute(value, 'rows', pairs)  5.56 us
  transfers between devices with their start and end apart: 20, of which 5 were waited for; matrix products, arithmetic and copies ran while one was open for 4% of the time, Pallas kernels for 31%

profile of v2, /device:TPU:1, one launch (start us, length us, event | category | flops | bytes accessed | tf_op | source)
XLA Modules:
  0.0 100.2 jit_solution(13081509605963354741)
XLA Ops:
  0.0 0.8 pad.4
  1.1 0.9 broadcast_in_dim.40
  1.9 7.6 %all-to-all-start = ((f32[16,32,256]{2,1,0:T(8,128)}), f32[16,32,256]{2,1,0:T(8,128)S(1)}, u32[]{:S(2)}, u32[]{:S(2)}) async-start(f32[16,32,256]{2,1,0:T(8,128)} %broadcast_in_dim.40), calls=%async_computation | async-start | bytes 1048576 | tf_op jit(solution)/shard_map/all_to_all | solution.py:275
  9.6 1.4 %fusion.8.spot_ref = s32[4096]{0:T(1024)} fusion(s32[4096]{0:T(1024)} %param.6, s32[]{:T(128)S(6)} %select_n.110, s32[]{:T(128)S(6)} %select_n.126, s32[]{:T(128)S(6)} %select_n.122), kind=kLoop, calls=%fused_computation.29 | loop fusion | flops 323584 | bytes 32780 | tf_op jit(solution)/shard_map/add | solution.py:281
  10.9 9.0 %prep.1 = (f32[512,2,128]{2,1,0:T(2,128)}, f32[512,2,128]{2,1,0:T(2,128)}, f32[512,2,128]{2,1,0:T(2,128)}, f32[512,2,128]{2,1,0:T(2,128)}, f32[512,2,128]{2,1,0:...) custom-call(s32[4096]{0:T(1024)} %fusion.8.spot_ref, f32[256,4096]{1,0:T(8,128)} %raw_ref.1), custom_call_target="tpu_custom_call" | custom-call | tf_op jit(solution)/shard_map/prep/pallas_call | solution.py:123
  20.0 2.3 %collective-permute-start.4 = (f32[2,512,128]{2,1,0:T(8,128)}, f32[2,512,128]{2,1,0:T(8,128)S(1)}, u32[]{:S(2)}, u32[]{:S(2)}) collective-permute-start(f32[2,512,128]{2,1,0:T(8,128)} %bitcast.25), channel_id=1, source_target_pairs={{0,10},{1,11},{2,12},{3,13},{4,14},{5,15},{6,8},{7,9},{8,2},{9,3},... | collective-permute-start | bytes 1572872 | tf_op jit(solution)/shard_map/ppermute | solution.py:45
  22.3 1.5 %collective-permute-start.5 = (f32[2,512,128]{2,1,0:T(8,128)}, f32[2,512,128]{2,1,0:T(8,128)S(1)}, u32[]{:S(2)}, u32[]{:S(2)}) collective-permute-start(f32[2,512,128]{2,1,0:T(8,128)} %bitcast.24), channel_id=1, source_target_pairs={{0,6},{1,7},{2,0},{3,1},{4,2},{5,3},{6,4},{7,5},{8,14},{9,15},{10,... | collective-permute-start | bytes 1572872 | tf_op jit(solution)/shard_map/ppermute | solution.py:45
  23.8 1.8 %collective-permute-start.11 = (f32[2,512,128]{2,1,0:T(8,128)}, f32[2,512,128]{2,1,0:T(8,128)S(1)}, u32[]{:S(2)}, u32[]{:S(2)}) collective-permute-start(f32[2,512,128]{2,1,0:T(8,128)} %bitcast.15), channel_id=1, source_target_pairs={{0,1},{1,0},{2,3},{3,2},{4,5},{5,4},{6,7},{7,6},{8,9},{9,8},{10,11... | collective-permute-start | bytes 1572872 | tf_op jit(solution)/shard_map/ppermute | solution.py:36
  25.7 9.2 %collective-permute-done.4.refs_4_ = f32[2,512,128]{2,1,0:T(8,128)S(1)} collective-permute-done((f32[2,512,128]{2,1,0:T(8,128)}, f32[2,512,128]{2,1,0:T(8,128)S(1)}, u32[]{:S(2)}, u32[]{:S(2)}) %collective-permute-start.4) | collective-permute-done | bytes 524320 | tf_op jit(solution)/shard_map/ppermute | solution.py:45
  34.9 1.3 %collective-permute-start.10 = (f32[2,512,128]{2,1,0:T(8,128)}, f32[2,512,128]{2,1,0:T(8,128)S(1)}, u32[]{:S(2)}, u32[]{:S(2)}) collective-permute-start(f32[2,512,128]{2,1,0:T(8,128)} %bitcast.22), channel_id=1, source_target_pairs={{0,4},{1,5},{2,6},{3,7},{4,0},{5,1},{6,2},{7,3},{8,12},{9,13},{10,... | collective-permute-start | bytes 1572872 | tf_op jit(solution)/shard_map/ppermute | solution.py:45
  36.3 2.4 %collective-permute-start.14 = (f32[2,512,128]{2,1,0:T(8,128)S(1)}, f32[2,512,128]{2,1,0:T(8,128)}, u32[]{:S(2)}, u32[]{:S(2)}) collective-permute-start(f32[2,512,128]{2,1,0:T(8,128)S(1)} %collective-permute-done.4.refs_4_), channel_id=1, source_target_pairs={{0,1},{1,0},{2,3},{3,2},{4,5},{5,4},{6,7},{7,6},{8,9},{9,8},{10,11... | collective-permute-start | bytes 1572872 | tf_op jit(solution)/shard_map/ppermute | solution.py:36
  38.7 1.9 %fusion.1 = (s32[256]{0:T(256)}, s32[256]{0:T(256)S(1)}) fusion(s32[4096]{0:T(1024)S(1)} %copy-done.13, s32[4096]{0:T(1024)S(1)} %copy-done.12, s32[256]{0:T(256)S(1)} %iota_add_fusion), kind=kLoop, calls=%fused_computation.3 | loop fusion | flops 5242368 | bytes 35840 | tf_op jit(solution)/shard_map/reduce_max | solution.py:298
  41.2 3.3 %choose.1.a_ref = f32[256,256]{1,0:T(8,128)} custom-call(s32[256]{0:T(256)} %compare_select_fusion.9.row_ref, f32[512,256]{1,0:T(8,128)} %bitcast.14, f32[512,256]{1,0:T(8,128)} %collective-permute-done.other_ref), custom_call_target="tpu_custom_call" | custom-call | tf_op jit(solution)/shard_map/choose/pallas_call | solution.py:153
  44.5 3.6 %collective-permute-start.3 = (f32[256,256]{1,0:T(8,128)}, f32[256,256]{1,0:T(8,128)S(1)}, u32[]{:S(2)}, u32[]{:S(2)}) collective-permute-start(f32[256,256]{1,0:T(8,128)} %choose.1.a_ref), channel_id=1, source_target_pairs={{32,0},{48,16},{0,32},{16,48},{96,64},{112,80},{64,96},{80,112},{3... | collective-permute-start | bytes 786440 | tf_op jit(solution)/shard_map/ppermute | solution.py:32
  48.9 2.4 %collective-permute-start.1 = (f32[256,256]{1,0:T(8,128)}, f32[256,256]{1,0:T(8,128)}, u32[]{:S(2)}, u32[]{:S(2)}) collective-permute-start(f32[256,256]{1,0:T(8,128)} %choose.1.a_ref), channel_id=1, source_target_pairs={{16,0},{32,16},{48,32},{0,48},{80,64},{96,80},{112,96},{64,112},{1... | collective-permute-start | bytes 786440 | tf_op jit(solution)/shard_map/ppermute | solution.py:32
  51.3 2.2 %collective-permute-start.7 = (f32[2,512,128]{2,1,0:T(8,128)}, f32[2,512,128]{2,1,0:T(8,128)}, u32[]{:S(2)}, u32[]{:S(2)}) collective-permute-start(f32[2,512,128]{2,1,0:T(8,128)} %bitcast.21), channel_id=1, source_target_pairs={{0,14},{1,15},{2,8},{3,9},{4,10},{5,11},{6,12},{7,13},{8,6},{9,7},... | collective-permute-start | bytes 1572872 | tf_op jit(solution)/shard_map/ppermute | solution.py:45
  53.5 1.0 collective-permute-start.15
  55.0 0.8 collective-permute-start.12
  55.8 5.0 %collective-permute-done.2.c_ref = f32[256,256]{1,0:T(8,128)} collective-permute-done((f32[256,256]{1,0:T(8,128)}, f32[256,256]{1,0:T(8,128)}, u32[]{:S(2)}, u32[]{:S(2)}) %collective-permute-start.2) | collective-permute-done | bytes 262176 | tf_op jit(solution)/shard_map/ppermute | solution.py:32
  61.6 2.0 %make_table.1.refs_0_ = f32[256,256]{1,0:T(8,128)} custom-call(f32[256,256]{1,0:T(8,128)} %choose.1.a_ref, f32[256,256]{1,0:T(8,128)} %collective-permute-done.1.b_ref, f32[256,256]{1,0:T(8,128)} %collective-permute-done.2.c_ref, f32[256,256]{1,0:T(8,128)} %copy-done.11, s32[1,256]{1,0:T(1,128)} %bitcast.18), custom_call_target="tpu_custom_call" | custom-call | tf_op jit(solution)/shard_map/make_table/pallas_call | solution.py:175
  63.7 0.7 copy-done.6
  64.5 11.5 %shard_map.46.refs_5_ = s32[4096,256]{1,0:T(8,128)} custom-call(f32[256,256]{1,0:T(8,128)} %make_table.1.refs_0_, f32[2,512,128]{2,1,0:T(8,128)} %bitcast.16, f32[2,512,128]{2,1,0:T(8,128)} %copy-done.4, f32[2,512,128]{2,1,0:T(8,128)} %copy-done.5, f32[2,512,128]{2,1,0:T(8,128)} %copy-done.1, f32[2,512,128]{2,1,0:T(8,128)} %copy-done.2, ...), custom_call_target="tpu_custom_call" | custom-call | tf_op jit(solution)/shard_map/pallas_call | solution.py:251
  76.0 1.2 %collective-permute-start.16 = (f32[2,512,128]{2,1,0:T(8,128)}, f32[2,512,128]{2,1,0:T(8,128)S(1)}, u32[]{:S(2)}, u32[]{:S(2)}) collective-permute-start(f32[2,512,128]{2,1,0:T(8,128)} %collective-permute-done.7.refs_1_), channel_id=1, source_target_pairs={{0,1},{1,0},{2,3},{3,2},{4,5},{5,4},{6,7},{7,6},{8,9},{9,8},{10,11... | collective-permute-start | bytes 1572872 | tf_op jit(solution)/shard_map/ppermute | solution.py:36
  77.2 2.7 %collective-permute-start.6 = (f32[2,512,128]{2,1,0:T(8,128)}, f32[2,512,128]{2,1,0:T(8,128)S(1)}, u32[]{:S(2)}, u32[]{:S(2)}) collective-permute-start(f32[2,512,128]{2,1,0:T(8,128)} %bitcast.19), channel_id=1, source_target_pairs={{0,12},{1,13},{2,14},{3,15},{4,8},{5,9},{6,10},{7,11},{8,4},{9,5},... | collective-permute-start | bytes 1572872 | tf_op jit(solution)/shard_map/ppermute | solution.py:45
  79.9 0.8 copy-done.9
  80.7 0.8 copy-done.10
  81.6 5.6 %shard_map.47.refs_3_ = s32[4096,256]{1,0:T(8,128)} custom-call(f32[256,256]{1,0:T(8,128)} %make_table.1.refs_0_, f32[2,512,128]{2,1,0:T(8,128)} %collective-permute-done.7.refs_1_, f32[2,512,128]{2,1,0:T(8,128)} %collective-permute-done.8.refs_2_, f32[2,512,128]{2,1,0:T(8,128)} %copy-done.9, ...), custom_call_target="tpu_custom_call", output_to_operand_aliasing={{}: (5, {})} | custom-call | tf_op jit(solution)/shard_map/pallas_call | solution.py:251
  87.2 5.7 %collective-permute-done.6.refs_1_ = f32[2,512,128]{2,1,0:T(8,128)S(1)} collective-permute-done((f32[2,512,128]{2,1,0:T(8,128)}, f32[2,512,128]{2,1,0:T(8,128)S(1)}, u32[]{:S(2)}, u32[]{:S(2)}) %collective-permute-start.6) | collective-permute-done | bytes 524320 | tf_op jit(solution)/shard_map/ppermute | solution.py:45
  92.9 1.3 %collective-permute-start.18 = (f32[2,512,128]{2,1,0:T(8,128)S(1)}, f32[2,512,128]{2,1,0:T(8,128)S(1)}, u32[]{:S(2)}, u32[]{:S(2)}) collective-permute-start(f32[2,512,128]{2,1,0:T(8,128)S(1)} %collective-permute-done.6.refs_1_), channel_id=1, source_target_pairs={{0,1},{1,0},{2,3},{3,2},{4,5},{5,4},{6,7},{7,6},{8,9},{9,8},{10,11... | collective-permute-start | bytes 1572872 | tf_op jit(solution)/shard_map/ppermute | solution.py:36
  94.2 1.5 %collective-permute-done.18.refs_2_ = f32[2,512,128]{2,1,0:T(8,128)S(1)} collective-permute-done((f32[2,512,128]{2,1,0:T(8,128)S(1)}, f32[2,512,128]{2,1,0:T(8,128)S(1)}, u32[]{:S(2)}, u32[]{:S(2)}) %collective-permute-start.18) | collective-permute-done | bytes 524320 | tf_op jit(solution)/shard_map/ppermute | solution.py:36
  95.7 0.8 copy-done.8
  96.5 3.6 %shard_map.48 = s32[4096,256]{1,0:T(8,128)} custom-call(f32[256,256]{1,0:T(8,128)} %make_table.1.refs_0_, f32[2,512,128]{2,1,0:T(8,128)} %copy-done.7, f32[2,512,128]{2,1,0:T(8,128)} %copy-done.8, s32[4096,256]{1,0:T(8,128)} %shard_map.47.refs_3_), custom_call_target="tpu_custom_call", output_to_operand_aliasing={{}: (3, {})} | custom-call | tf_op jit(solution)/shard_map/pallas_call | solution.py:251
  (51 shorter events, 3.2 us)
Async XLA Ops:
  0.0 38.7 %copy-start.12 = (s32[4096]{0:T(1024)S(1)}, s32[4096]{0:T(1024)}, u32[]{:S(2)}) copy-start(s32[4096]{0:T(1024)} %param.6) | copy-start | bytes 49156
  0.0 38.7 %copy-start.13 = (s32[4096]{0:T(1024)S(1)}, s32[4096]{0:T(1024)}, u32[]{:S(2)}) copy-start(s32[4096]{0:T(1024)} %param.7) | copy-start | bytes 49156
  1.9 23.6 %all-to-all-start = ((f32[16,32,256]{2,1,0:T(8,128)}), f32[16,32,256]{2,1,0:T(8,128)S(1)}, u32[]{:S(2)}, u32[]{:S(2)}) async-start(f32[16,32,256]{2,1,0:T(8,128)} %broadcast_in_dim.40), calls=%async_computation | async-start | bytes 1048576 | tf_op jit(solution)/shard_map/all_to_all | solution.py:275
  20.0 15.0 %collective-permute-start.4 = (f32[2,512,128]{2,1,0:T(8,128)}, f32[2,512,128]{2,1,0:T(8,128)S(1)}, u32[]{:S(2)}, u32[]{:S(2)}) collective-permute-start(f32[2,512,128]{2,1,0:T(8,128)} %bitcast.25), channel_id=1, source_target_pairs={{0,10},{1,11},{2,12},{3,13},{4,14},{5,15},{6,8},{7,9},{8,2},{9,3},... | collective-permute-start | bytes 1572872 | tf_op jit(solution)/shard_map/ppermute | solution.py:45
  22.3 14.0 %collective-permute-start.5 = (f32[2,512,128]{2,1,0:T(8,128)}, f32[2,512,128]{2,1,0:T(8,128)S(1)}, u32[]{:S(2)}, u32[]{:S(2)}) collective-permute-start(f32[2,512,128]{2,1,0:T(8,128)} %bitcast.24), channel_id=1, source_target_pairs={{0,6},{1,7},{2,0},{3,1},{4,2},{5,3},{6,4},{7,5},{8,14},{9,15},{10,... | collective-permute-start | bytes 1572872 | tf_op jit(solution)/shard_map/ppermute | solution.py:45
  23.8 24.4 %collective-permute-start.11 = (f32[2,512,128]{2,1,0:T(8,128)}, f32[2,512,128]{2,1,0:T(8,128)S(1)}, u32[]{:S(2)}, u32[]{:S(2)}) collective-permute-start(f32[2,512,128]{2,1,0:T(8,128)} %bitcast.15), channel_id=1, source_target_pairs={{0,1},{1,0},{2,3},{3,2},{4,5},{5,4},{6,7},{7,6},{8,9},{9,8},{10,11... | collective-permute-start | bytes 1572872 | tf_op jit(solution)/shard_map/ppermute | solution.py:36
  25.6 23.3 %collective-permute-start.9 = (f32[2,512,128]{2,1,0:T(8,128)}, f32[2,512,128]{2,1,0:T(8,128)S(1)}, u32[]{:S(2)}, u32[]{:S(2)}) collective-permute-start(f32[2,512,128]{2,1,0:T(8,128)} %bitcast.23), channel_id=1, source_target_pairs={{0,8},{1,9},{2,10},{3,11},{4,12},{5,13},{6,14},{7,15},{8,0},{9,1},... | collective-permute-start | bytes 1572872 | tf_op jit(solution)/shard_map/ppermute | solution.py:45
  25.6 15.7 %copy-start = (f32[16,32,256]{2,1,0:T(8,128)}, f32[16,32,256]{2,1,0:T(8,128)S(1)}, u32[]{:S(2)}) copy-start(f32[16,32,256]{2,1,0:T(8,128)S(1)} %all-to-all-done) | copy-start | bytes 1572868
  25.6 15.7 %collective-permute-start = (f32[512,256]{1,0:T(8,128)S(1)}, f32[512,256]{1,0:T(8,128)}, u32[]{:S(2)}, u32[]{:S(2)}) collective-permute-start(f32[512,256]{1,0:T(8,128)S(1)} %bitcast.13), channel_id=1, source_target_pairs={{0,1},{1,0},{2,3},{3,2},{4,5},{5,4},{6,7},{7,6},{8,9},{9,8},{10,11... | collective-permute-start | bytes 1572872 | tf_op jit(solution)/shard_map/ppermute | solution.py:36
  34.9 28.7 %copy-start.1 = (f32[2,512,128]{2,1,0:T(8,128)}, f32[2,512,128]{2,1,0:T(8,128)S(1)}, u32[]{:S(2)}) copy-start(f32[2,512,128]{2,1,0:T(8,128)S(1)} %collective-permute-done.4.refs_4_) | copy-start | bytes 1572868
  34.9 16.3 %collective-permute-start.10 = (f32[2,512,128]{2,1,0:T(8,128)}, f32[2,512,128]{2,1,0:T(8,128)S(1)}, u32[]{:S(2)}, u32[]{:S(2)}) collective-permute-start(f32[2,512,128]{2,1,0:T(8,128)} %bitcast.22), channel_id=1, source_target_pairs={{0,4},{1,5},{2,6},{3,7},{4,0},{5,1},{6,2},{7,3},{8,12},{9,13},{10,... | collective-permute-start | bytes 1572872 | tf_op jit(solution)/shard_map/ppermute | solution.py:45
  36.3 27.4 %copy-start.2 = (f32[2,512,128]{2,1,0:T(8,128)}, f32[2,512,128]{2,1,0:T(8,128)S(1)}, u32[]{:S(2)}) copy-start(f32[2,512,128]{2,1,0:T(8,128)S(1)} %collective-permute-done.5.refs_5_) | copy-start | bytes 1572868
  36.3 17.2 %collective-permute-start.14 = (f32[2,512,128]{2,1,0:T(8,128)S(1)}, f32[2,512,128]{2,1,0:T(8,128)}, u32[]{:S(2)}, u32[]{:S(2)}) collective-permute-start(f32[2,512,128]{2,1,0:T(8,128)S(1)} %collective-permute-done.4.refs_4_), channel_id=1, source_target_pairs={{0,1},{1,0},{2,3},{3,2},{4,5},{5,4},{6,7},{7,6},{8,9},{9,8},{10,11... | collective-permute-start | bytes 1572872 | tf_op jit(solution)/shard_map/ppermute | solution.py:36
  44.5 10.5 %collective-permute-start.3 = (f32[256,256]{1,0:T(8,128)}, f32[256,256]{1,0:T(8,128)S(1)}, u32[]{:S(2)}, u32[]{:S(2)}) collective-permute-start(f32[256,256]{1,0:T(8,128)} %choose.1.a_ref), channel_id=1, source_target_pairs={{32,0},{48,16},{0,32},{16,48},{96,64},{112,80},{64,96},{80,112},{3... | collective-permute-start | bytes 786440 | tf_op jit(solution)/shard_map/ppermute | solution.py:32
  48.1 15.6 %copy-start.3 = (f32[2,512,128]{2,1,0:T(8,128)}, f32[2,512,128]{2,1,0:T(8,128)S(1)}, u32[]{:S(2)}) copy-start(f32[2,512,128]{2,1,0:T(8,128)S(1)} %collective-permute-done.11.refs_6_) | copy-start | bytes 1572868
  48.1 12.7 %collective-permute-start.2 = (f32[256,256]{1,0:T(8,128)}, f32[256,256]{1,0:T(8,128)}, u32[]{:S(2)}, u32[]{:S(2)}) collective-permute-start(f32[256,256]{1,0:T(8,128)} %choose.1.a_ref), channel_id=1, source_target_pairs={{48,0},{0,16},{16,32},{32,48},{112,64},{64,80},{80,96},{96,112},{4... | collective-permute-start | bytes 786440 | tf_op jit(solution)/shard_map/ppermute | solution.py:32
  48.9 14.8 %copy-start.4 = (f32[2,512,128]{2,1,0:T(8,128)}, f32[2,512,128]{2,1,0:T(8,128)S(1)}, u32[]{:S(2)}) copy-start(f32[2,512,128]{2,1,0:T(8,128)S(1)} %collective-permute-done.9.refs_2_) | copy-start | bytes 1572868
  48.9 12.4 %collective-permute-start.1 = (f32[256,256]{1,0:T(8,128)}, f32[256,256]{1,0:T(8,128)}, u32[]{:S(2)}, u32[]{:S(2)}) collective-permute-start(f32[256,256]{1,0:T(8,128)} %choose.1.a_ref), channel_id=1, source_target_pairs={{16,0},{32,16},{48,32},{0,48},{80,64},{96,80},{112,96},{64,112},{1... | collective-permute-start | bytes 786440 | tf_op jit(solution)/shard_map/ppermute | solution.py:32
  51.3 12.4 %copy-start.5 = (f32[2,512,128]{2,1,0:T(8,128)}, f32[2,512,128]{2,1,0:T(8,128)S(1)}, u32[]{:S(2)}) copy-start(f32[2,512,128]{2,1,0:T(8,128)S(1)} %collective-permute-done.10.refs_3_) | copy-start | bytes 1572868
  51.3 24.7 %collective-permute-start.7 = (f32[2,512,128]{2,1,0:T(8,128)}, f32[2,512,128]{2,1,0:T(8,128)}, u32[]{:S(2)}, u32[]{:S(2)}) collective-permute-start(f32[2,512,128]{2,1,0:T(8,128)} %bitcast.21), channel_id=1, source_target_pairs={{0,14},{1,15},{2,8},{3,9},{4,10},{5,11},{6,12},{7,13},{8,6},{9,7},... | collective-permute-start | bytes 1572872 | tf_op jit(solution)/shard_map/ppermute | solution.py:45
  53.5 10.2 %collective-permute-start.15 = (f32[2,512,128]{2,1,0:T(8,128)S(1)}, f32[2,512,128]{2,1,0:T(8,128)S(1)}, u32[]{:S(2)}, u32[]{:S(2)}) collective-permute-start(f32[2,512,128]{2,1,0:T(8,128)S(1)} %collective-permute-done.5.refs_5_), channel_id=1, source_target_pairs={{0,1},{1,0},{2,3},{3,2},{4,5},{5,4},{6,7},{7,6},{8,9},{9,8},{10,11... | collective-permute-start | bytes 1572872 | tf_op jit(solution)/shard_map/ppermute | solution.py:36
  55.0 6.6 %copy-start.11 = (f32[256,256]{1,0:T(8,128)}, f32[256,256]{1,0:T(8,128)S(1)}, u32[]{:S(2)}) copy-start(f32[256,256]{1,0:T(8,128)S(1)} %collective-permute-done.3.d_ref) | copy-start | bytes 786436
  55.0 8.6 %collective-permute-start.12 = (f32[2,512,128]{2,1,0:T(8,128)S(1)}, f32[2,512,128]{2,1,0:T(8,128)}, u32[]{:S(2)}, u32[]{:S(2)}) collective-permute-start(f32[2,512,128]{2,1,0:T(8,128)S(1)} %collective-permute-done.9.refs_2_), channel_id=1, source_target_pairs={{0,1},{1,0},{2,3},{3,2},{4,5},{5,4},{6,7},{7,6},{8,9},{9,8},{10,11... | collective-permute-start | bytes 1572872 | tf_op jit(solution)/shard_map/ppermute | solution.py:36
  60.9 2.8 %collective-permute-start.13 = (f32[2,512,128]{2,1,0:T(8,128)S(1)}, f32[2,512,128]{2,1,0:T(8,128)}, u32[]{:S(2)}, u32[]{:S(2)}) collective-permute-start(f32[2,512,128]{2,1,0:T(8,128)S(1)} %collective-permute-done.10.refs_3_), channel_id=1, source_target_pairs={{0,1},{1,0},{2,3},{3,2},{4,5},{5,4},{6,7},{7,6},{8,9},{9,8},{10,11... | collective-permute-start | bytes 1572872 | tf_op jit(solution)/shard_map/ppermute | solution.py:36
  61.3 14.7 %collective-permute-start.8 = (f32[2,512,128]{2,1,0:T(8,128)}, f32[2,512,128]{2,1,0:T(8,128)}, u32[]{:S(2)}, u32[]{:S(2)}) collective-permute-start(f32[2,512,128]{2,1,0:T(8,128)} %bitcast.20), channel_id=1, source_target_pairs={{0,2},{1,3},{2,4},{3,5},{4,6},{5,7},{6,0},{7,1},{8,10},{9,11},{10,... | collective-permute-start | bytes 1572872 | tf_op jit(solution)/shard_map/ppermute | solution.py:45
  76.0 3.9 %collective-permute-start.16 = (f32[2,512,128]{2,1,0:T(8,128)}, f32[2,512,128]{2,1,0:T(8,128)S(1)}, u32[]{:S(2)}, u32[]{:S(2)}) collective-permute-start(f32[2,512,128]{2,1,0:T(8,128)} %collective-permute-done.7.refs_1_), channel_id=1, source_target_pairs={{0,1},{1,0},{2,3},{3,2},{4,5},{5,4},{6,7},{7,6},{8,9},{9,8},{10,11... | collective-permute-start | bytes 1572872 | tf_op jit(solution)/shard_map/ppermute | solution.py:36
  77.2 2.7 %collective-permute-start.17 = (f32[2,512,128]{2,1,0:T(8,128)}, f32[2,512,128]{2,1,0:T(8,128)S(1)}, u32[]{:S(2)}, u32[]{:S(2)}) collective-permute-start(f32[2,512,128]{2,1,0:T(8,128)} %collective-permute-done.8.refs_2_), channel_id=1, source_target_pairs={{0,1},{1,0},{2,3},{3,2},{4,5},{5,4},{6,7},{7,6},{8,9},{9,8},{10,11... | collective-permute-start | bytes 1572872 | tf_op jit(solution)/shard_map/ppermute | solution.py:36
  77.2 15.6 %collective-permute-start.6 = (f32[2,512,128]{2,1,0:T(8,128)}, f32[2,512,128]{2,1,0:T(8,128)S(1)}, u32[]{:S(2)}, u32[]{:S(2)}) collective-permute-start(f32[2,512,128]{2,1,0:T(8,128)} %bitcast.19), channel_id=1, source_target_pairs={{0,12},{1,13},{2,14},{3,15},{4,8},{5,9},{6,10},{7,11},{8,4},{9,5},... | collective-permute-start | bytes 1572872 | tf_op jit(solution)/shard_map/ppermute | solution.py:45
  79.9 0.8 copy-start.9
  92.8 2.9 %copy-start.7 = (f32[2,512,128]{2,1,0:T(8,128)}, f32[2,512,128]{2,1,0:T(8,128)S(1)}, u32[]{:S(2)}) copy-start(f32[2,512,128]{2,1,0:T(8,128)S(1)} %collective-permute-done.6.refs_1_) | copy-start | bytes 1572868
  92.9 2.9 %collective-permute-start.18 = (f32[2,512,128]{2,1,0:T(8,128)S(1)}, f32[2,512,128]{2,1,0:T(8,128)S(1)}, u32[]{:S(2)}, u32[]{:S(2)}) collective-permute-start(f32[2,512,128]{2,1,0:T(8,128)S(1)} %collective-permute-done.6.refs_1_), channel_id=1, source_target_pairs={{0,1},{1,0},{2,3},{3,2},{4,5},{5,4},{6,7},{7,6},{8,9},{9,8},{10,11... | collective-permute-start | bytes 1572872 | tf_op jit(solution)/shard_map/ppermute | solution.py:36
  95.7 0.8 copy-start.8
  (2 other events, 1.6 us)

commit v3 on v2

--- a/solution.py
+++ b/solution.py
@@ -12,10 +12,14 @@
 EDGES = 256
 SPAN = 256
 FEATURES = 4096
-CHIPS = 8
-PHASES = (((1, 0), (0, 2)), ((1, 1), (0, 3)), ((1, 3), (0, 1)), ((1, 2),))
+EARLY = ((1, 0), (0, 2), (1, 1), (0, 3))
+LATE = ((1, 3), (0, 1), (1, 2))
 GROUP = 1024
 SUB = 256
+
+
+CUTS = [((dy * SIDE + dx) * 512, 512) for dy, dx in ((0, 0), *EARLY)]
+CUTS += [((dy * SIDE + dx) * 512 + dc * 256, 256) for dy, dx in LATE for dc in range(2)]
 
 
 def device_at(y, z, x, core):
@@ -36,12 +40,12 @@
     return lax.ppermute(value, "bundle", [(i, i ^ 1) for i in range(16)])
 
 
-def to_chip(value, dy, dx):
+def to_chip(value, dy, dx, dc=0):
     pairs = []
     for y in range(2):
         for x in range(SIDE):
             for core in range(2):
-                pairs.append((y * 8 + x * 2 + core, (y ^ dy) * 8 + (x + dx) % SIDE * 2 + core))
+                pairs.append((y * 8 + x * 2 + core, (y ^ dy) * 8 + (x + dx) % SIDE * 2 + (core ^ dc)))
     return lax.ppermute(value, "bundle", pairs)
 
 
@@ -84,7 +88,8 @@
 
 
 def prep_kernel(spot_ref, raw_ref, *refs):
-    outs, buffer, sems, turned = refs[:CHIPS], refs[CHIPS], refs[CHIPS + 1], refs[CHIPS + 2 :]
+    outs = refs[: len(CUTS)]
+    buffer, sems, *turned = refs[len(CUTS) :]
     i = pl.program_id(0)
 
     def turn(j):
@@ -111,8 +116,8 @@
     @pl.when(i == pl.num_programs(0) - 1)
     def _():
         copies = []
-        for k, ref in enumerate(outs):
-            copies.append(pltpu.make_async_copy(buffer.at[pl.ds(512 * k, 512)], ref, sems.at[k]))
+        for k, (ref, (start, size)) in enumerate(zip(outs, CUTS)):
+            copies.append(pltpu.make_async_copy(buffer.at[pl.ds(start, size)], ref, sems.at[k]))
         for copy in copies:
             copy.start()
         for copy in copies:
@@ -126,11 +131,11 @@
             num_scalar_prefetch=1,
             grid=(FEATURES // GROUP,),
             in_specs=[pl.BlockSpec((256, GROUP), lambda i, c: (0, i))],
-            out_specs=[pl.BlockSpec(memory_space=pltpu.HBM)] * CHIPS,
-            scratch_shapes=[pltpu.VMEM((FEATURES, 2, 128), jnp.float32), pltpu.SemaphoreType.DMA((CHIPS,))]
+            out_specs=[pl.BlockSpec(memory_space=pltpu.HBM)] * len(CUTS),
+            scratch_shapes=[pltpu.VMEM((FEATURES, 2, 128), jnp.float32), pltpu.SemaphoreType.DMA((len(CUTS),))]
             + [pltpu.VMEM((SUB * 2, 128), jnp.float32)] * (GROUP // SUB),
         ),
-        out_shape=[jax.ShapeDtypeStruct((512, 2, 128), jnp.float32)] * CHIPS,
+        out_shape=[jax.ShapeDtypeStruct((size, 2, 128), jnp.float32) for _, size in CUTS],
         name="prep",
     )(spot, raw)
 
@@ -179,13 +184,14 @@
 
 def bin_kernel(table_hbm, *refs, chips, fresh):
     count = len(chips)
-    own, swapped = refs[:count], refs[count : 2 * count]
+    parts = refs[: 2 * count]
     bundle = lax.axis_index("bundle")
     x, y_low, core = (bundle // 2) % SIDE, bundle // 8, bundle % 2
     out_ref, stage, turned, result, table_ref, bases, in_sems, out_sems = refs[2 * count + (0 if fresh else 1) :]
 
     def take(i, side):
-        source = own[i].at[0] if side == 0 else swapped[i].at[1]
+        source = parts[2 * i + side]
+        source = source.at[side] if len(source.shape) == 3 else source
         return pltpu.make_async_copy(source, stage.at[2 * i + side], in_sems.at[2 * i + side])
 
     for i, (dy, dx) in enumerate(chips):
@@ -207,7 +213,7 @@
         take(i, 1).start()
 
     def arrive(part):
-        pltpu.make_async_copy(own[0].at[0], stage.at[part], in_sems.at[part]).wait()
+        pltpu.make_async_copy(stage.at[0], stage.at[part], in_sems.at[part]).wait()
 
     def turn(tile, slot):
         line = (tile % 4 // 2) * 256 + tile % 2
@@ -245,8 +251,8 @@
     lax.fori_loop(0, 8 * count, drain, 0)
 
 
-def bin_chips(chips, table, own, swapped, out):
-    count, fresh = len(own), out is None
+def bin_chips(chips, table, parts, out):
+    count, fresh = len(chips), out is None
     anywhere = pl.BlockSpec(memory_space=pltpu.HBM)
     return pl.pallas_call(
         lambda *refs: bin_kernel(*refs, chips=chips, fresh=fresh),
@@ -263,7 +269,7 @@
         ],
         out_shape=jax.ShapeDtypeStruct((16 * 256, SPAN), jnp.int32),
         input_output_aliases={} if fresh else {1 + 2 * count: 0},
-    )(table, *own, *swapped, *([] if fresh else [out]))
+    )(table, *parts, *([] if fresh else [out]))
 
 
 def step(raw_values, bin_edges, feature_column, bin_offset):
@@ -279,18 +285,16 @@
     owner, inside = feature_column // SPAN, feature_column % SPAN
     chip = (owner // 8 ^ y_low) * SIDE + ((owner // 2) % SIDE - x) % SIDE
     spot = chip * 512 + (owner % 2 ^ core) * 256 + inside
-    sent = [value.reshape(2, 512, 128) for value in prep(spot, raw_values)]
-
-    def carry(chips, values):
-        arrived = []
-        for (dy, dx), value in zip(chips, values):
-            arrived.append(to_chip(value, dy, dx))
-        return arrived
-
-    def picked(phase):
-        return [sent[dy * SIDE + dx] for dy, dx in PHASES[phase]]
-
-    arrived = [carry(PHASES[0], picked(0)), carry(PHASES[1], picked(1))]
+    pieces = prep(spot, raw_values)
+    sent = [value.reshape(2, 512, 128) for value in pieces[: 1 + len(EARLY)]]
+    halves = [value.reshape(512, 128) for value in pieces[1 + len(EARLY) :]]
+    arrived = [sent[0]]
+    for (dy, dx), value in zip(EARLY, sent[1:]):
+        arrived.append(to_chip(value, dy, dx))
+    direct = []
+    for i, (dy, dx) in enumerate(LATE):
+        for dc in range(2):
+            direct.append(to_chip(halves[2 * i + dc], dy, dx, dc))
 
     wanted = bundle * SPAN + jnp.arange(SPAN, dtype=jnp.int32)
     named = feature_column[None, :] == wanted[:, None]
@@ -305,23 +309,13 @@
     turned = []
     for step in (1, 3, 2):
         turned.append(along_z(part, step))
-    arrived.append(carry(PHASES[2], picked(2)))
-    *values, arrived[1] = lax.optimization_barrier((*picked(3), arrived[1]))
-    arrived.append(carry(PHASES[3], values))
     table = make_table([part] + turned, offset[None])
-    arrived[0] = [sent[0]] + arrived[0]
-    chips = [((0, 0), *PHASES[0])] + list(PHASES[1:])
-    swapped = []
-    for n in range(2):
-        swapped.append([])
-        for value in arrived[n]:
-            swapped[n].append(swap_cores(value))
-    out = bin_chips(chips[0] + chips[1], table, arrived[0] + arrived[1], swapped[0] + swapped[1], None)
-    for n in (2, 3):
-        arrived[n], out = lax.optimization_barrier((arrived[n], out))
-        swapped.append([swap_cores(value) for value in arrived[n]])
-        out = bin_chips(chips[n], table, arrived[n], swapped[n], out)
-    return out
+    parts = []
+    for value in arrived:
+        parts += [value, swap_cores(value)]
+    out = bin_chips(((0, 0), *EARLY), table, parts, None)
+    *direct, out = lax.optimization_barrier((*direct, out))
+    return bin_chips(LATE, table, direct, out)
 
 
 def solution(mesh):

time: 101 us -> 104 us (1.030)
  waiting for transfers between devices: 22 us -> 28.5 us
  local copies, waits for them, and re-layouts: 5.13 us -> 1.96 us
  starting transfers between devices: 33.8 us -> 35.9 us
  Pallas kernels: 35.1 us -> 33.5 us
    ppermute x7 -> x10, starting transfers between devices: 10.3 us -> 20.8 us  [to_chip(): return lax.ppermute(value, 'bundle', pairs)]
    ppermute x7 -> x10, waiting for transfers between devices: 14.9 us -> 25.3 us  [to_chip(): return lax.ppermute(value, 'bundle', pairs)]
    ppermute x9 -> x6, starting transfers between devices: 9.19 us -> 1.19 us  [swap_cores(): return lax.ppermute(value, 'bundle', [(i, i ^ 1) for i in range(16)])]
    unnamed x28 -> x22, local copies, waits for them, and re-layouts: 3.22 us -> 0.04 us
    ppermute x3, waiting for transfers between devices: 5.56 us -> 3.14 us  [along_z(): return lax.ppermute(value, 'rows', pairs)]
    pallas_call x3 -> x2, Pallas kernels: 20.8 us -> 19.1 us  [bin_chips(): pl.pallas_call(lambda *refs: bin_kernel(*refs, chips=chips, fresh=fresh),...]
    ppermute x9 -> x6, waiting for transfers between devices: 1.56 us -> 0.02 us  [swap_cores(): return lax.ppermute(value, 'bundle', [(i, i ^ 1) for i in range(16)])]
  transfers between devices with their start and end apart: 20 -> 20, of which waited for: 5 -> 5; matrix products, arithmetic and copies ran while one was open for 4% -> 4% of each run, Pallas kernels for 31% -> 25%
where the time goes in v3:
time: 104 us
  starting transfers between devices  35.9 us (35%)
  Pallas kernels  33.5 us (32%)
  waiting for transfers between devices  28.5 us (27%)
  other arithmetic  3.91 us (4%)
  local copies, waits for them, and re-layouts  1.96 us (2%)
    ppermute x10, waiting for transfers between devices, to_chip(): return lax.ppermute(value, 'bundle', pairs)  25.3 us
    ppermute x10, starting transfers between devices, to_chip(): return lax.ppermute(value, 'bundle', pairs)  20.8 us
    pallas_call x2, Pallas kernels, bin_chips(): pl.pallas_call(lambda *refs: bin_kernel(*refs, chips=chips, fresh=fresh),...  19.1 us
    pallas_call x1, Pallas kernels, prep(): pl.pallas_call(prep_kernel, grid_spec=pltpu.PrefetchScalarGridSpec(num_sc...  9.05 us
    all_to_all x1, starting transfers between devices, step(): lax.all_to_all(copies, AXES, split_axis=0, concat_axis=0, axis_index_grou...  7.57 us
    ppermute x3, starting transfers between devices, along_z(): return lax.ppermute(value, 'rows', pairs)  6.28 us
    pallas_call x1, Pallas kernels, choose(): pl.pallas_call(choose_kernel, grid_spec=pltpu.PrefetchScalarGridSpec(num_...  3.33 us
    ppermute x3, waiting for transfers between devices, along_z(): return lax.ppermute(value, 'rows', pairs)  3.14 us
  transfers between devices with their start and end apart: 20, of which 5 were waited for; matrix products, arithmetic and copies ran while one was open for 4% of the time, Pallas kernels for 25%

profile of v3, /device:TPU:1, one launch (start us, length us, event | category | flops | bytes accessed | tf_op | source)
XLA Modules:
  0.0 103.9 jit_solution(12362269123697035192)
XLA Ops:
  0.0 0.8 pad.4
  0.9 0.1 copy.8
  1.1 0.9 broadcast_in_dim.40
  1.9 7.6 %all-to-all-start = ((f32[16,32,256]{2,1,0:T(8,128)}), f32[16,32,256]{2,1,0:T(8,128)S(1)}, u32[]{:S(2)}, u32[]{:S(2)}) async-start(f32[16,32,256]{2,1,0:T(8,128)} %broadcast_in_dim.40), calls=%async_computation | async-start | bytes 1048576 | tf_op jit(solution)/shard_map/all_to_all | solution.py:281
  9.6 1.4 %fusion.8.spot_ref = s32[4096]{0:T(1024)} fusion(s32[4096]{0:T(1024)} %param.6, s32[]{:T(128)S(6)} %select_n.110, s32[]{:T(128)S(6)} %select_n.126, s32[]{:T(128)S(6)} %select_n.122), kind=kLoop, calls=%fused_computation.29 | loop fusion | flops 323584 | bytes 32780 | tf_op jit(solution)/shard_map/add | solution.py:287
  10.9 9.1 %prep.1 = (f32[512,2,128]{2,1,0:T(2,128)}, f32[512,2,128]{2,1,0:T(2,128)}, f32[512,2,128]{2,1,0:T(2,128)}, f32[512,2,128]{2,1,0:T(2,128)}, f32[512,2,128]{2,1,0:...) custom-call(s32[4096]{0:T(1024)} %fusion.8.spot_ref, ...), custom_call_target="tpu_custom_call" | custom-call | tf_op jit(solution)/shard_map/prep/pallas_call | solution.py:128
  20.0 4.6 %collective-permute-start.5 = (f32[512,128]{1,0:T(8,128)}, f32[512,128]{1,0:T(8,128)S(1)}, u32[]{:S(2)}, u32[]{:S(2)}) collective-permute-start(f32[512,128]{1,0:T(8,128)} %bitcast.31), channel_id=1, source_target_pairs={{0,15},{1,14},{2,9},{3,8},{4,11},{5,10},{6,13},{7,12},{8,7},{9,6},... | collective-permute-start | bytes 786440 | tf_op jit(solution)/shard_map/ppermute | solution.py:49
  24.6 0.3 collective-permute-start.11
  24.9 0.6 collective-permute-start.13
  25.5 1.5 %collective-permute-start.15 = (f32[2,512,128]{2,1,0:T(8,128)}, f32[2,512,128]{2,1,0:T(8,128)S(1)}, u32[]{:S(2)}, u32[]{:S(2)}) collective-permute-start(f32[2,512,128]{2,1,0:T(8,128)} %bitcast.23), channel_id=1, source_target_pairs={{0,10},{1,11},{2,12},{3,13},{4,14},{5,15},{6,8},{7,9},{8,2},{9,3},... | collective-permute-start | bytes 1572872 | tf_op jit(solution)/shard_map/ppermute | solution.py:49
  27.0 2.1 %collective-permute-start.17 = (f32[2,512,128]{2,1,0:T(8,128)}, f32[2,512,128]{2,1,0:T(8,128)S(1)}, u32[]{:S(2)}, u32[]{:S(2)}) collective-permute-start(f32[2,512,128]{2,1,0:T(8,128)} %bitcast.22), channel_id=1, source_target_pairs={{0,6},{1,7},{2,0},{3,1},{4,2},{5,3},{6,4},{7,5},{8,14},{9,15},{10,... | collective-permute-start | bytes 1572872 | tf_op jit(solution)/shard_map/ppermute | solution.py:49
  29.1 13.1 %collective-permute-done.5.refs_2_ = f32[512,128]{1,0:T(8,128)S(1)} collective-permute-done((f32[512,128]{1,0:T(8,128)}, f32[512,128]{1,0:T(8,128)S(1)}, u32[]{:S(2)}, u32[]{:S(2)}) %collective-permute-start.5) | collective-permute-done | bytes 262176 | tf_op jit(solution)/shard_map/ppermute | solution.py:49
  42.2 10.5 %collective-permute-done.11.refs_3_ = f32[2,512,128]{2,1,0:T(8,128)S(1)} collective-permute-done((f32[2,512,128]{2,1,0:T(8,128)}, f32[2,512,128]{2,1,0:T(8,128)S(1)}, u32[]{:S(2)}, u32[]{:S(2)}) %collective-permute-start.11) | collective-permute-done | bytes 524320 | tf_op jit(solution)/shard_map/ppermute | solution.py:49
  52.8 0.5 collective-permute-start.12
  53.4 0.5 collective-permute-start.16
  53.9 0.1 collective-permute-start.18
  54.0 1.9 %fusion.1 = (s32[256]{0:T(256)}, s32[256]{0:T(256)S(1)}) fusion(s32[4096]{0:T(1024)S(1)} %copy-done.10, s32[4096]{0:T(1024)S(1)} %copy-done.9, s32[256]{0:T(256)S(1)} %iota_add_fusion), kind=kLoop, calls=%fused_computation.3 | loop fusion | flops 5242368 | bytes 35840 | tf_op jit(solution)/shard_map/reduce_max | solution.py:302
  55.9 0.6 compare_select_fusion.9.row_ref
  56.5 3.3 %choose.1.a_ref = f32[256,256]{1,0:T(8,128)} custom-call(s32[256]{0:T(256)} %compare_select_fusion.9.row_ref, f32[512,256]{1,0:T(8,128)} %bitcast.17, f32[512,256]{1,0:T(8,128)} %collective-permute-done.other_ref), custom_call_target="tpu_custom_call" | custom-call | tf_op jit(solution)/shard_map/choose/pallas_call | solution.py:158
  59.8 3.6 %collective-permute-start.3 = (f32[256,256]{1,0:T(8,128)}, f32[256,256]{1,0:T(8,128)}, u32[]{:S(2)}, u32[]{:S(2)}) collective-permute-start(f32[256,256]{1,0:T(8,128)} %choose.1.a_ref), channel_id=1, source_target_pairs={{32,0},{48,16},{0,32},{16,48},{96,64},{112,80},{64,96},{80,112},{3... | collective-permute-start | bytes 786440 | tf_op jit(solution)/shard_map/ppermute | solution.py:36
  63.4 0.7 collective-permute-start.2
  64.2 1.9 %collective-permute-start.1 = (f32[256,256]{1,0:T(8,128)}, f32[256,256]{1,0:T(8,128)}, u32[]{:S(2)}, u32[]{:S(2)}) collective-permute-start(f32[256,256]{1,0:T(8,128)} %choose.1.a_ref), channel_id=1, source_target_pairs={{16,0},{32,16},{48,32},{0,48},{80,64},{96,80},{112,96},{64,112},{1... | collective-permute-start | bytes 786440 | tf_op jit(solution)/shard_map/ppermute | solution.py:36
  66.1 3.8 %collective-permute-start.4 = (f32[512,128]{1,0:T(8,128)}, f32[512,128]{1,0:T(8,128)S(1)}, u32[]{:S(2)}, u32[]{:S(2)}) collective-permute-start(f32[512,128]{1,0:T(8,128)} %bitcast.30), channel_id=1, source_target_pairs={{0,14},{1,15},{2,8},{3,9},{4,10},{5,11},{6,12},{7,13},{8,6},{9,7},... | collective-permute-start | bytes 786440 | tf_op jit(solution)/shard_map/ppermute | solution.py:49
  69.9 0.2 collective-permute-done.3.d_ref
  70.1 3.1 %collective-permute-start.7 = (f32[512,128]{1,0:T(8,128)}, f32[512,128]{1,0:T(8,128)}, u32[]{:S(2)}, u32[]{:S(2)}) collective-permute-start(f32[512,128]{1,0:T(8,128)} %bitcast.28), channel_id=1, source_target_pairs={{0,3},{1,2},{2,5},{3,4},{4,7},{5,6},{6,1},{7,0},{8,11},{9,10},{10,... | collective-permute-start | bytes 786440 | tf_op jit(solution)/shard_map/ppermute | solution.py:49
  73.2 3.0 %collective-permute-done.2.c_ref = f32[256,256]{1,0:T(8,128)} collective-permute-done((f32[256,256]{1,0:T(8,128)}, f32[256,256]{1,0:T(8,128)}, u32[]{:S(2)}, u32[]{:S(2)}) %collective-permute-start.2) | collective-permute-done | bytes 262176 | tf_op jit(solution)/shard_map/ppermute | solution.py:36
  76.1 3.8 %collective-permute-start.8 = (f32[512,128]{1,0:T(8,128)}, f32[512,128]{1,0:T(8,128)}, u32[]{:S(2)}, u32[]{:S(2)}) collective-permute-start(f32[512,128]{1,0:T(8,128)} %bitcast.27), channel_id=1, source_target_pairs={{0,12},{1,13},{2,14},{3,15},{4,8},{5,9},{6,10},{7,11},{8,4},{9,5},... | collective-permute-start | bytes 786440 | tf_op jit(solution)/shard_map/ppermute | solution.py:49
  79.9 1.1 %collective-permute-start.9 = (f32[512,128]{1,0:T(8,128)}, f32[512,128]{1,0:T(8,128)}, u32[]{:S(2)}, u32[]{:S(2)}) collective-permute-start(f32[512,128]{1,0:T(8,128)} %bitcast.26), channel_id=1, source_target_pairs={{0,13},{1,12},{2,15},{3,14},{4,9},{5,8},{6,11},{7,10},{8,5},{9,4},... | collective-permute-start | bytes 786440 | tf_op jit(solution)/shard_map/ppermute | solution.py:49
  81.0 2.0 %make_table.1.refs_0_ = f32[256,256]{1,0:T(8,128)} custom-call(f32[256,256]{1,0:T(8,128)} %choose.1.a_ref, f32[256,256]{1,0:T(8,128)} %collective-permute-done.1.b_ref, f32[256,256]{1,0:T(8,128)} %collective-permute-done.2.c_ref, f32[256,256]{1,0:T(8,128)} %collective-permute-done.3.d_ref, s32[1,256]{1,0:T(1,128)} %bitcast.21), custom_call_target="tpu_custom_call" | custom-call | tf_op jit(solution)/shard_map/make_table/pallas_call | solution.py:180
  83.1 11.5 %shard_map.46.refs_7_ = s32[4096,256]{1,0:T(8,128)} custom-call(f32[256,256]{1,0:T(8,128)} %make_table.1.refs_0_, f32[2,512,128]{2,1,0:T(8,128)} %bitcast.19, f32[2,512,128]{2,1,0:T(8,128)} %copy-done.5, f32[2,512,128]{2,1,0:T(8,128)} %copy-done.1, f32[2,512,128]{2,1,0:T(8,128)} %collective-permute-done.12.refs_4_, f32[2,512,128]{2,1,0:T(8,128)} %copy-done.2, ...), custom_call_target="tpu_custom_call" | custom-call | tf_op jit(solution)/shard_map/pallas_call | solution.py:257
  94.7 1.6 %collective-permute-done.7.refs_4_ = f32[512,128]{1,0:T(8,128)} collective-permute-done((f32[512,128]{1,0:T(8,128)}, f32[512,128]{1,0:T(8,128)}, u32[]{:S(2)}, u32[]{:S(2)}) %collective-permute-start.7) | collective-permute-done | bytes 262176 | tf_op jit(solution)/shard_map/ppermute | solution.py:49
  96.3 7.6 %shard_map.47 = s32[4096,256]{1,0:T(8,128)} custom-call(f32[256,256]{1,0:T(8,128)} %make_table.1.refs_0_, f32[512,128]{1,0:T(8,128)} %copy-done.7, f32[512,128]{1,0:T(8,128)} %copy-done.6, f32[512,128]{1,0:T(8,128)} %copy-done.8, f32[512,128]{1,0:T(8,128)} %collective-permute-done.7.refs_4_, ...), custom_call_target="tpu_custom_call", output_to_operand_aliasing={{}: (7, {})} | custom-call | tf_op jit(solution)/shard_map/pallas_call | solution.py:257
  (44 shorter events, 0.3 us)
Async XLA Ops:
  0.0 54.0 %copy-start.9 = (s32[4096]{0:T(1024)S(1)}, s32[4096]{0:T(1024)}, u32[]{:S(2)}) copy-start(s32[4096]{0:T(1024)} %param.6) | copy-start | bytes 49156
  0.0 54.0 %copy-start.10 = (s32[4096]{0:T(1024)S(1)}, s32[4096]{0:T(1024)}, u32[]{:S(2)}) copy-start(s32[4096]{0:T(1024)} %param.7) | copy-start | bytes 49156
  1.9 40.3 %all-to-all-start = ((f32[16,32,256]{2,1,0:T(8,128)}), f32[16,32,256]{2,1,0:T(8,128)S(1)}, u32[]{:S(2)}, u32[]{:S(2)}) async-start(f32[16,32,256]{2,1,0:T(8,128)} %broadcast_in_dim.40), calls=%async_computation | async-start | bytes 1048576 | tf_op jit(solution)/shard_map/all_to_all | solution.py:281
  20.0 22.2 %collective-permute-start.5 = (f32[512,128]{1,0:T(8,128)}, f32[512,128]{1,0:T(8,128)S(1)}, u32[]{:S(2)}, u32[]{:S(2)}) collective-permute-start(f32[512,128]{1,0:T(8,128)} %bitcast.31), channel_id=1, source_target_pairs={{0,15},{1,14},{2,9},{3,8},{4,11},{5,10},{6,13},{7,12},{8,7},{9,6},... | collective-permute-start | bytes 786440 | tf_op jit(solution)/shard_map/ppermute | solution.py:49
  24.6 28.1 %collective-permute-start.11 = (f32[2,512,128]{2,1,0:T(8,128)}, f32[2,512,128]{2,1,0:T(8,128)S(1)}, u32[]{:S(2)}, u32[]{:S(2)}) collective-permute-start(f32[2,512,128]{2,1,0:T(8,128)} %bitcast.25), channel_id=1, source_target_pairs={{0,8},{1,9},{2,10},{3,11},{4,12},{5,13},{6,14},{7,15},{8,0},{9,1},... | collective-permute-start | bytes 1572872 | tf_op jit(solution)/shard_map/ppermute | solution.py:49
  24.9 27.8 %collective-permute-start.13 = (f32[2,512,128]{2,1,0:T(8,128)}, f32[2,512,128]{2,1,0:T(8,128)S(1)}, u32[]{:S(2)}, u32[]{:S(2)}) collective-permute-start(f32[2,512,128]{2,1,0:T(8,128)} %bitcast.24), channel_id=1, source_target_pairs={{0,4},{1,5},{2,6},{3,7},{4,0},{5,1},{6,2},{7,3},{8,12},{9,13},{10,... | collective-permute-start | bytes 1572872 | tf_op jit(solution)/shard_map/ppermute | solution.py:49
  25.5 27.8 %collective-permute-start.15 = (f32[2,512,128]{2,1,0:T(8,128)}, f32[2,512,128]{2,1,0:T(8,128)S(1)}, u32[]{:S(2)}, u32[]{:S(2)}) collective-permute-start(f32[2,512,128]{2,1,0:T(8,128)} %bitcast.23), channel_id=1, source_target_pairs={{0,10},{1,11},{2,12},{3,13},{4,14},{5,15},{6,8},{7,9},{8,2},{9,3},... | collective-permute-start | bytes 1572872 | tf_op jit(solution)/shard_map/ppermute | solution.py:49
  27.0 26.4 %collective-permute-start.17 = (f32[2,512,128]{2,1,0:T(8,128)}, f32[2,512,128]{2,1,0:T(8,128)S(1)}, u32[]{:S(2)}, u32[]{:S(2)}) collective-permute-start(f32[2,512,128]{2,1,0:T(8,128)} %bitcast.22), channel_id=1, source_target_pairs={{0,6},{1,7},{2,0},{3,1},{4,2},{5,3},{6,4},{7,5},{8,14},{9,15},{10,... | collective-permute-start | bytes 1572872 | tf_op jit(solution)/shard_map/ppermute | solution.py:49
  42.2 54.1 %copy-start.6 = (f32[512,128]{1,0:T(8,128)}, f32[512,128]{1,0:T(8,128)S(1)}, u32[]{:S(2)}) copy-start(f32[512,128]{1,0:T(8,128)S(1)} %collective-permute-done.5.refs_2_) | copy-start | bytes 786436
  42.2 14.3 %copy-start = (f32[16,32,256]{2,1,0:T(8,128)}, f32[16,32,256]{2,1,0:T(8,128)S(1)}, u32[]{:S(2)}) copy-start(f32[16,32,256]{2,1,0:T(8,128)S(1)} %all-to-all-done) | copy-start | bytes 1572868
  42.2 11.7 %collective-permute-start = (f32[512,256]{1,0:T(8,128)S(1)}, f32[512,256]{1,0:T(8,128)}, u32[]{:S(2)}, u32[]{:S(2)}) collective-permute-start(f32[512,256]{1,0:T(8,128)S(1)} %bitcast.16), channel_id=1, source_target_pairs={{0,1},{1,0},{2,3},{3,2},{4,5},{5,4},{6,7},{7,6},{8,9},{9,8},{10,11... | collective-permute-start | bytes 1572872 | tf_op jit(solution)/shard_map/ppermute | solution.py:40
  52.7 30.3 %copy-start.1 = (f32[2,512,128]{2,1,0:T(8,128)}, f32[2,512,128]{2,1,0:T(8,128)S(1)}, u32[]{:S(2)}) copy-start(f32[2,512,128]{2,1,0:T(8,128)S(1)} %collective-permute-done.11.refs_3_) | copy-start | bytes 1572868
  52.7 7.1 %collective-permute-start.10 = (f32[2,512,128]{2,1,0:T(8,128)}, f32[2,512,128]{2,1,0:T(8,128)S(1)}, u32[]{:S(2)}, u32[]{:S(2)}) collective-permute-start(f32[2,512,128]{2,1,0:T(8,128)} %bitcast.18), channel_id=1, source_target_pairs={{0,1},{1,0},{2,3},{3,2},{4,5},{5,4},{6,7},{7,6},{8,9},{9,8},{10,11... | collective-permute-start | bytes 1572872 | tf_op jit(solution)/shard_map/ppermute | solution.py:40
  52.7 30.3 %copy-start.2 = (f32[2,512,128]{2,1,0:T(8,128)}, f32[2,512,128]{2,1,0:T(8,128)S(1)}, u32[]{:S(2)}) copy-start(f32[2,512,128]{2,1,0:T(8,128)S(1)} %collective-permute-done.13.refs_5_) | copy-start | bytes 1572868
  52.8 10.7 %collective-permute-start.12 = (f32[2,512,128]{2,1,0:T(8,128)S(1)}, f32[2,512,128]{2,1,0:T(8,128)}, u32[]{:S(2)}, u32[]{:S(2)}) collective-permute-start(f32[2,512,128]{2,1,0:T(8,128)S(1)} %collective-permute-done.11.refs_3_), channel_id=1, source_target_pairs={{0,1},{1,0},{2,3},{3,2},{4,5},{5,4},{6,7},{7,6},{8,9},{9,8},{10,11... | collective-permute-start | bytes 1572872 | tf_op jit(solution)/shard_map/ppermute | solution.py:40
  53.3 29.8 %copy-start.3 = (f32[2,512,128]{2,1,0:T(8,128)}, f32[2,512,128]{2,1,0:T(8,128)S(1)}, u32[]{:S(2)}) copy-start(f32[2,512,128]{2,1,0:T(8,128)S(1)} %collective-permute-done.15.refs_7_) | copy-start | bytes 1572868
  53.3 10.9 %collective-permute-start.14 = (f32[2,512,128]{2,1,0:T(8,128)S(1)}, f32[2,512,128]{2,1,0:T(8,128)}, u32[]{:S(2)}, u32[]{:S(2)}) collective-permute-start(f32[2,512,128]{2,1,0:T(8,128)S(1)} %collective-permute-done.13.refs_5_), channel_id=1, source_target_pairs={{0,1},{1,0},{2,3},{3,2},{4,5},{5,4},{6,7},{7,6},{8,9},{9,8},{10,11... | collective-permute-start | bytes 1572872 | tf_op jit(solution)/shard_map/ppermute | solution.py:40
  53.4 29.7 %copy-start.4 = (f32[2,512,128]{2,1,0:T(8,128)}, f32[2,512,128]{2,1,0:T(8,128)S(1)}, u32[]{:S(2)}) copy-start(f32[2,512,128]{2,1,0:T(8,128)S(1)} %collective-permute-done.17.refs_9_) | copy-start | bytes 1572868
  53.4 12.7 %collective-permute-start.16 = (f32[2,512,128]{2,1,0:T(8,128)S(1)}, f32[2,512,128]{2,1,0:T(8,128)}, u32[]{:S(2)}, u32[]{:S(2)}) collective-permute-start(f32[2,512,128]{2,1,0:T(8,128)S(1)} %collective-permute-done.15.refs_7_), channel_id=1, source_target_pairs={{0,1},{1,0},{2,3},{3,2},{4,5},{5,4},{6,7},{7,6},{8,9},{9,8},{10,11... | collective-permute-start | bytes 1572872 | tf_op jit(solution)/shard_map/ppermute | solution.py:40
  53.9 16.0 %collective-permute-start.18 = (f32[2,512,128]{2,1,0:T(8,128)S(1)}, f32[2,512,128]{2,1,0:T(8,128)}, u32[]{:S(2)}, u32[]{:S(2)}) collective-permute-start(f32[2,512,128]{2,1,0:T(8,128)S(1)} %collective-permute-done.17.refs_9_), channel_id=1, source_target_pairs={{0,1},{1,0},{2,3},{3,2},{4,5},{5,4},{6,7},{7,6},{8,9},{9,8},{10,11... | collective-permute-start | bytes 1572872 | tf_op jit(solution)/shard_map/ppermute | solution.py:40
  59.8 23.3 %copy-start.5 = (f32[2,512,128]{2,1,0:T(8,128)}, f32[2,512,128]{2,1,0:T(8,128)S(1)}, u32[]{:S(2)}) copy-start(f32[2,512,128]{2,1,0:T(8,128)S(1)} %collective-permute-done.10.refs_2_) | copy-start | bytes 1572868
  59.8 10.2 %collective-permute-start.3 = (f32[256,256]{1,0:T(8,128)}, f32[256,256]{1,0:T(8,128)}, u32[]{:S(2)}, u32[]{:S(2)}) collective-permute-start(f32[256,256]{1,0:T(8,128)} %choose.1.a_ref), channel_id=1, source_target_pairs={{32,0},{48,16},{0,32},{16,48},{96,64},{112,80},{64,96},{80,112},{3... | collective-permute-start | bytes 786440 | tf_op jit(solution)/shard_map/ppermute | solution.py:36
  63.4 12.7 %collective-permute-start.2 = (f32[256,256]{1,0:T(8,128)}, f32[256,256]{1,0:T(8,128)}, u32[]{:S(2)}, u32[]{:S(2)}) collective-permute-start(f32[256,256]{1,0:T(8,128)} %choose.1.a_ref), channel_id=1, source_target_pairs={{48,0},{0,16},{16,32},{32,48},{112,64},{64,80},{80,96},{96,112},{4... | collective-permute-start | bytes 786440 | tf_op jit(solution)/shard_map/ppermute | solution.py:36
  64.2 15.7 %collective-permute-start.1 = (f32[256,256]{1,0:T(8,128)}, f32[256,256]{1,0:T(8,128)}, u32[]{:S(2)}, u32[]{:S(2)}) collective-permute-start(f32[256,256]{1,0:T(8,128)} %choose.1.a_ref), channel_id=1, source_target_pairs={{16,0},{32,16},{48,32},{0,48},{80,64},{96,80},{112,96},{64,112},{1... | collective-permute-start | bytes 786440 | tf_op jit(solution)/shard_map/ppermute | solution.py:36
  66.1 28.5 %collective-permute-start.4 = (f32[512,128]{1,0:T(8,128)}, f32[512,128]{1,0:T(8,128)S(1)}, u32[]{:S(2)}, u32[]{:S(2)}) collective-permute-start(f32[512,128]{1,0:T(8,128)} %bitcast.30), channel_id=1, source_target_pairs={{0,14},{1,15},{2,8},{3,9},{4,10},{5,11},{6,12},{7,13},{8,6},{9,7},... | collective-permute-start | bytes 786440 | tf_op jit(solution)/shard_map/ppermute | solution.py:49
  69.9 24.8 %collective-permute-start.6 = (f32[512,128]{1,0:T(8,128)}, f32[512,128]{1,0:T(8,128)S(1)}, u32[]{:S(2)}, u32[]{:S(2)}) collective-permute-start(f32[512,128]{1,0:T(8,128)} %bitcast.29), channel_id=1, source_target_pairs={{0,2},{1,3},{2,4},{3,5},{4,6},{5,7},{6,0},{7,1},{8,10},{9,11},{10,... | collective-permute-start | bytes 786440 | tf_op jit(solution)/shard_map/ppermute | solution.py:49
  70.1 26.2 %collective-permute-start.7 = (f32[512,128]{1,0:T(8,128)}, f32[512,128]{1,0:T(8,128)}, u32[]{:S(2)}, u32[]{:S(2)}) collective-permute-start(f32[512,128]{1,0:T(8,128)} %bitcast.28), channel_id=1, source_target_pairs={{0,3},{1,2},{2,5},{3,4},{4,7},{5,6},{6,1},{7,0},{8,11},{9,10},{10,... | collective-permute-start | bytes 786440 | tf_op jit(solution)/shard_map/ppermute | solution.py:49
  76.1 20.2 %collective-permute-start.8 = (f32[512,128]{1,0:T(8,128)}, f32[512,128]{1,0:T(8,128)}, u32[]{:S(2)}, u32[]{:S(2)}) collective-permute-start(f32[512,128]{1,0:T(8,128)} %bitcast.27), channel_id=1, source_target_pairs={{0,12},{1,13},{2,14},{3,15},{4,8},{5,9},{6,10},{7,11},{8,4},{9,5},... | collective-permute-start | bytes 786440 | tf_op jit(solution)/shard_map/ppermute | solution.py:49
  79.9 16.4 %collective-permute-start.9 = (f32[512,128]{1,0:T(8,128)}, f32[512,128]{1,0:T(8,128)}, u32[]{:S(2)}, u32[]{:S(2)}) collective-permute-start(f32[512,128]{1,0:T(8,128)} %bitcast.26), channel_id=1, source_target_pairs={{0,13},{1,12},{2,15},{3,14},{4,9},{5,8},{6,11},{7,10},{8,5},{9,4},... | collective-permute-start | bytes 786440 | tf_op jit(solution)/shard_map/ppermute | solution.py:49
  94.6 1.7 %copy-start.7 = (f32[512,128]{1,0:T(8,128)}, f32[512,128]{1,0:T(8,128)S(1)}, u32[]{:S(2)}) copy-start(f32[512,128]{1,0:T(8,128)S(1)} %collective-permute-done.4.refs_1_) | copy-start | bytes 786436
  94.7 1.7 %copy-start.8 = (f32[512,128]{1,0:T(8,128)}, f32[512,128]{1,0:T(8,128)S(1)}, u32[]{:S(2)}) copy-start(f32[512,128]{1,0:T(8,128)S(1)} %collective-permute-done.6.refs_3_) | copy-start | bytes 786436

commit v4 on v3

--- a/solution.py
+++ b/solution.py
@@ -13,7 +13,7 @@
 SPAN = 256
 FEATURES = 4096
 EARLY = ((1, 0), (0, 2), (1, 1), (0, 3))
-LATE = ((1, 3), (0, 1), (1, 2))
+LATE = ((0, 1), (1, 3), (1, 2))
 GROUP = 1024
 SUB = 256
 
@@ -169,16 +169,23 @@
     )(row, mine, other)
 
 
-def table_kernel(a_ref, b_ref, c_ref, d_ref, offset_ref, out_ref):
+def table_kernel(a_ref, b_ref, c_ref, d_ref, offset_ref, out_ref, turned):
     total = (a_ref[...] + b_ref[...]) + (c_ref[...] + d_ref[...])
-    turned = total.T
-    line = lax.broadcasted_iota(jnp.int32, turned.shape, 0)
-    out_ref[...] = jnp.where(line == EDGES - 1, offset_ref[...].astype(jnp.float32), turned)
+    for half in range(2):
+        turned[half] = total[half * 128 : half * 128 + 128, :].T
+    for o in range(32):
+        for half in range(2):
+            lanes = slice(half * 128, half * 128 + 128)
+            out_ref[8 * o : 8 * o + 8, lanes] = turned[half, pl.ds(o, 8, stride=32), :]
+    out_ref[EDGES - 1 :, :] = offset_ref[...].astype(jnp.float32)
 
 
 def make_table(parts, offset):
     return pl.pallas_call(
-        table_kernel, out_shape=jax.ShapeDtypeStruct((EDGES, SPAN), jnp.float32), name="make_table"
+        table_kernel,
+        out_shape=jax.ShapeDtypeStruct((EDGES, SPAN), jnp.float32),
+        scratch_shapes=[pltpu.VMEM((2, EDGES, 128), jnp.float32)],
+        name="make_table",
     )(*parts, offset)
 
 
@@ -275,17 +282,17 @@
 def step(raw_values, bin_edges, feature_column, bin_offset):
     row, bundle = lax.axis_index("rows"), lax.axis_index("bundle")
     z, core = row % SIDE, bundle % 2
-    padded = jnp.pad(bin_edges, ((0, 0), (0, 1)))
-    ordered = padded.reshape(PIECE, 8, 32).transpose(0, 2, 1).reshape(PIECE, EDGES)
-    copies = jnp.broadcast_to(ordered[None], (16, PIECE, EDGES))
-    mine = lax.all_to_all(copies, AXES, split_axis=0, concat_axis=0, axis_index_groups=planes(), tiled=True)
-    mine = mine.reshape(512, EDGES)
-
     x, y_low = (bundle // 2) % SIDE, bundle // 8
     owner, inside = feature_column // SPAN, feature_column % SPAN
     chip = (owner // 8 ^ y_low) * SIDE + ((owner // 2) % SIDE - x) % SIDE
     spot = chip * 512 + (owner % 2 ^ core) * 256 + inside
-    pieces = prep(spot, raw_values)
+    pieces = list(prep(spot, raw_values))
+    copies = jnp.broadcast_to(jnp.pad(bin_edges, ((0, 0), (0, 1)))[None], (16, PIECE, EDGES))
+    copies, pieces[0] = lax.optimization_barrier((copies, pieces[0]))
+    mine = lax.all_to_all(
+        copies, AXES, split_axis=0, concat_axis=0, axis_index_groups=planes(), tiled=True
+    )
+    mine = mine.reshape(512, EDGES)
     sent = [value.reshape(2, 512, 128) for value in pieces[: 1 + len(EARLY)]]
     halves = [value.reshape(512, 128) for value in pieces[1 + len(EARLY) :]]
     arrived = [sent[0]]
@@ -314,8 +321,10 @@
     for value in arrived:
         parts += [value, swap_cores(value)]
     out = bin_chips(((0, 0), *EARLY), table, parts, None)
-    *direct, out = lax.optimization_barrier((*direct, out))
-    return bin_chips(LATE, table, direct, out)
+    *middle, out = lax.optimization_barrier((*direct[:2], out))
+    out = bin_chips(LATE[:1], table, middle, out)
+    *last, out = lax.optimization_barrier((*direct[2:], out))
+    return bin_chips(LATE[1:], table, last, out)
 
 
 def solution(mesh):

time: 104 us -> 110 us (1.058)
  Pallas kernels: 33.5 us -> 35.3 us
  starting transfers between devices: 35.9 us -> 37.6 us
  waiting for transfers between devices: 28.5 us -> 29.7 us
  local copies, waits for them, and re-layouts: 1.96 us -> 3.11 us
    ppermute x6, starting transfers between devices: 1.19 us -> 7.53 us  [swap_cores(): return lax.ppermute(value, 'bundle', [(i, i ^ 1) for i in range(16)])]
    ppermute x10, starting transfers between devices: 20.8 us -> 16.2 us  [to_chip(): return lax.ppermute(value, 'bundle', pairs)]
    ppermute x3, waiting for transfers between devices: 3.14 us -> 5.24 us  [along_z(): return lax.ppermute(value, 'rows', pairs)]
    pallas_call x2 -> x3, Pallas kernels: 19.1 us -> 20.8 us  [bin_chips(): pl.pallas_call(lambda *refs: bin_kernel(*refs, chips=chips, fresh=fresh),...]
    unnamed x22 -> x24, local copies, waits for them, and re-layouts: 0.04 us -> 1.48 us
  transfers between devices with their start and end apart: 20 -> 20, of which waited for: 5 -> 6; matrix products, arithmetic and copies ran while one was open for 4% -> 2% of each run, Pallas kernels for 25% -> 19%
where the time goes in v4:
time: 110 us
  starting transfers between devices  37.6 us (34%)
  Pallas kernels  35.3 us (32%)
  waiting for transfers between devices  29.7 us (27%)
  other arithmetic  3.86 us (4%)
  local copies, waits for them, and re-layouts  3.11 us (3%)
    ppermute x10, waiting for transfers between devices, to_chip(): return lax.ppermute(value, 'bundle', pairs)  24.5 us
    pallas_call x3, Pallas kernels, bin_chips(): pl.pallas_call(lambda *refs: bin_kernel(*refs, chips=chips, fresh=fresh),...  20.8 us
    ppermute x10, starting transfers between devices, to_chip(): return lax.ppermute(value, 'bundle', pairs)  16.2 us
    pallas_call x1, Pallas kernels, prep(): pl.pallas_call(prep_kernel, grid_spec=pltpu.PrefetchScalarGridSpec(num_sc...  9.05 us
    all_to_all x1, starting transfers between devices, step(): lax.all_to_all(copies, AXES, split_axis=0, concat_axis=0, axis_index_grou...  7.57 us
    ppermute x6, starting transfers between devices, swap_cores(): return lax.ppermute(value, 'bundle', [(i, i ^ 1) for i in range(16)])  7.53 us
    ppermute x3, starting transfers between devices, along_z(): return lax.ppermute(value, 'rows', pairs)  6.27 us
    ppermute x3, waiting for transfers between devices, along_z(): return lax.ppermute(value, 'rows', pairs)  5.24 us
  transfers between devices with their start and end apart: 20, of which 6 were waited for; matrix products, arithmetic and copies ran while one was open for 2% of the time, Pallas kernels for 19%

profile of v4, /device:TPU:1, one launch (start us, length us, event | category | flops | bytes accessed | tf_op | source)
XLA Modules:
  0.0 109.7 jit_solution(159036974579131004)
XLA Ops:
  0.0 0.8 pad.4
  0.8 1.4 %fusion.8.spot_ref = s32[4096]{0:T(1024)} fusion(s32[4096]{0:T(1024)} %param.6, s32[]{:T(128)S(6)} %select_n.110, s32[]{:T(128)S(6)} %select_n.125, s32[]{:T(128)S(6)} %select_n.121), kind=kLoop, calls=%fused_computation.29 | loop fusion | flops 323584 | bytes 32780 | tf_op jit(solution)/shard_map/add | solution.py:288
  2.2 9.1 %prep.1 = (f32[512,2,128]{2,1,0:T(2,128)}, f32[512,2,128]{2,1,0:T(2,128)}, f32[512,2,128]{2,1,0:T(2,128)}, f32[512,2,128]{2,1,0:T(2,128)}, f32[512,2,128]{2,1,0:...) custom-call(s32[4096]{0:T(1024)} %fusion.8.spot_ref, ...), custom_call_target="tpu_custom_call" | custom-call | tf_op jit(solution)/shard_map/prep/pallas_call | solution.py:128
  11.2 0.8 broadcast_in_dim.38
  12.1 7.6 %all-to-all-start = ((f32[16,32,256]{2,1,0:T(8,128)}), f32[16,32,256]{2,1,0:T(8,128)S(1)}, u32[]{:S(2)}, u32[]{:S(2)}) async-start(f32[16,32,256]{2,1,0:T(8,128)} %broadcast_in_dim.38), calls=%async_computation | async-start | bytes 1048576 | tf_op jit(solution)/shard_map/all_to_all | solution.py:292
  19.7 1.4 %collective-permute-start.8 = (f32[512,128]{1,0:T(8,128)}, f32[512,128]{1,0:T(8,128)S(1)}, u32[]{:S(2)}, u32[]{:S(2)}) collective-permute-start(f32[512,128]{1,0:T(8,128)} %bitcast.27), channel_id=1, source_target_pairs={{0,2},{1,3},{2,4},{3,5},{4,6},{5,7},{6,0},{7,1},{8,10},{9,11},{10,... | collective-permute-start | bytes 786440 | tf_op jit(solution)/shard_map/ppermute | solution.py:49
  21.0 1.2 %collective-permute-start.11 = (f32[2,512,128]{2,1,0:T(8,128)}, f32[2,512,128]{2,1,0:T(8,128)S(1)}, u32[]{:S(2)}, u32[]{:S(2)}) collective-permute-start(f32[2,512,128]{2,1,0:T(8,128)} %bitcast.21), channel_id=1, source_target_pairs={{0,8},{1,9},{2,10},{3,11},{4,12},{5,13},{6,14},{7,15},{8,0},{9,1},... | collective-permute-start | bytes 1572872 | tf_op jit(solution)/shard_map/ppermute | solution.py:49
  22.2 2.4 %collective-permute-start.13 = (f32[2,512,128]{2,1,0:T(8,128)}, f32[2,512,128]{2,1,0:T(8,128)S(1)}, u32[]{:S(2)}, u32[]{:S(2)}) collective-permute-start(f32[2,512,128]{2,1,0:T(8,128)} %bitcast.20), channel_id=1, source_target_pairs={{0,4},{1,5},{2,6},{3,7},{4,0},{5,1},{6,2},{7,3},{8,12},{9,13},{10,... | collective-permute-start | bytes 1572872 | tf_op jit(solution)/shard_map/ppermute | solution.py:49
  24.6 2.7 %collective-permute-start.17 = (f32[2,512,128]{2,1,0:T(8,128)}, f32[2,512,128]{2,1,0:T(8,128)S(1)}, u32[]{:S(2)}, u32[]{:S(2)}) collective-permute-start(f32[2,512,128]{2,1,0:T(8,128)} %bitcast.18), channel_id=1, source_target_pairs={{0,6},{1,7},{2,0},{3,1},{4,2},{5,3},{6,4},{7,5},{8,14},{9,15},{10,... | collective-permute-start | bytes 1572872 | tf_op jit(solution)/shard_map/ppermute | solution.py:49
  27.3 7.9 %collective-permute-done.8.refs_1_ = f32[512,128]{1,0:T(8,128)S(1)} collective-permute-done((f32[512,128]{1,0:T(8,128)}, f32[512,128]{1,0:T(8,128)S(1)}, u32[]{:S(2)}, u32[]{:S(2)}) %collective-permute-start.8) | collective-permute-done | bytes 262176 | tf_op jit(solution)/shard_map/ppermute | solution.py:49
  35.2 2.0 %collective-permute-start = (f32[512,256]{1,0:T(8,128)S(1)}, f32[512,256]{1,0:T(8,128)}, u32[]{:S(2)}, u32[]{:S(2)}) collective-permute-start(f32[512,256]{1,0:T(8,128)S(1)} %bitcast.13), channel_id=1, source_target_pairs={{0,1},{1,0},{2,3},{3,2},{4,5},{5,4},{6,7},{7,6},{8,9},{9,8},{10,11... | collective-permute-start | bytes 1572872 | tf_op jit(solution)/shard_map/ppermute | solution.py:40
  37.2 2.7 %collective-permute-done.11.refs_3_ = f32[2,512,128]{2,1,0:T(8,128)S(1)} collective-permute-done((f32[2,512,128]{2,1,0:T(8,128)}, f32[2,512,128]{2,1,0:T(8,128)S(1)}, u32[]{:S(2)}, u32[]{:S(2)}) %collective-permute-start.11) | collective-permute-done | bytes 524320 | tf_op jit(solution)/shard_map/ppermute | solution.py:49
  39.8 1.0 collective-permute-start.10
  40.9 4.3 %collective-permute-done.13.refs_5_ = f32[2,512,128]{2,1,0:T(8,128)S(1)} collective-permute-done((f32[2,512,128]{2,1,0:T(8,128)}, f32[2,512,128]{2,1,0:T(8,128)S(1)}, u32[]{:S(2)}, u32[]{:S(2)}) %collective-permute-start.13) | collective-permute-done | bytes 524320 | tf_op jit(solution)/shard_map/ppermute | solution.py:49
  45.2 3.1 %collective-permute-start.12 = (f32[2,512,128]{2,1,0:T(8,128)S(1)}, f32[2,512,128]{2,1,0:T(8,128)}, u32[]{:S(2)}, u32[]{:S(2)}) collective-permute-start(f32[2,512,128]{2,1,0:T(8,128)S(1)} %collective-permute-done.11.refs_3_), channel_id=1, source_target_pairs={{0,1},{1,0},{2,3},{3,2},{4,5},{5,4},{6,7},{7,6},{8,9},{9,8},{10,11... | collective-permute-start | bytes 1572872 | tf_op jit(solution)/shard_map/ppermute | solution.py:40
  48.3 9.6 %collective-permute-done.15.refs_7_ = f32[2,512,128]{2,1,0:T(8,128)S(1)} collective-permute-done((f32[2,512,128]{2,1,0:T(8,128)}, f32[2,512,128]{2,1,0:T(8,128)S(1)}, u32[]{:S(2)}, u32[]{:S(2)}) %collective-permute-start.15) | collective-permute-done | bytes 524320 | tf_op jit(solution)/shard_map/ppermute | solution.py:49
  57.9 0.8 collective-permute-start.14
  59.3 1.9 %fusion.1 = (s32[256]{0:T(256)}, s32[256]{0:T(256)S(1)}) fusion(s32[4096]{0:T(1024)S(1)} %copy-done.11, s32[4096]{0:T(1024)S(1)} %copy-done.10, s32[256]{0:T(256)S(1)} %iota_add_fusion), kind=kLoop, calls=%fused_computation.3 | loop fusion | flops 5242368 | bytes 35840 | tf_op jit(solution)/shard_map/reduce_max | solution.py:309
  61.8 3.3 %choose.1.a_ref = f32[256,256]{1,0:T(8,128)} custom-call(s32[256]{0:T(256)} %compare_select_fusion.9.row_ref, f32[512,256]{1,0:T(8,128)} %bitcast.14, f32[512,256]{1,0:T(8,128)} %collective-permute-done.other_ref), custom_call_target="tpu_custom_call" | custom-call | tf_op jit(solution)/shard_map/choose/pallas_call | solution.py:158
  65.1 3.6 %collective-permute-start.3 = (f32[256,256]{1,0:T(8,128)}, f32[256,256]{1,0:T(8,128)S(1)}, u32[]{:S(2)}, u32[]{:S(2)}) collective-permute-start(f32[256,256]{1,0:T(8,128)} %choose.1.a_ref), channel_id=1, source_target_pairs={{32,0},{48,16},{0,32},{16,48},{96,64},{112,80},{64,96},{80,112},{3... | collective-permute-start | bytes 786440 | tf_op jit(solution)/shard_map/ppermute | solution.py:36
  68.7 0.7 collective-permute-start.2
  69.4 1.9 %collective-permute-start.1 = (f32[256,256]{1,0:T(8,128)}, f32[256,256]{1,0:T(8,128)}, u32[]{:S(2)}, u32[]{:S(2)}) collective-permute-start(f32[256,256]{1,0:T(8,128)} %choose.1.a_ref), channel_id=1, source_target_pairs={{16,0},{32,16},{48,32},{0,48},{80,64},{96,80},{112,96},{64,112},{1... | collective-permute-start | bytes 786440 | tf_op jit(solution)/shard_map/ppermute | solution.py:36
  72.0 1.9 %collective-permute-start.9 = (f32[512,128]{1,0:T(8,128)}, f32[512,128]{1,0:T(8,128)}, u32[]{:S(2)}, u32[]{:S(2)}) collective-permute-start(f32[512,128]{1,0:T(8,128)} %bitcast.26), channel_id=1, source_target_pairs={{0,3},{1,2},{2,5},{3,4},{4,7},{5,6},{6,1},{7,0},{8,11},{9,10},{10,... | collective-permute-start | bytes 786440 | tf_op jit(solution)/shard_map/ppermute | solution.py:49
  74.0 1.6 %collective-permute-done.3.d_ref = f32[256,256]{1,0:T(8,128)S(1)} collective-permute-done((f32[256,256]{1,0:T(8,128)}, f32[256,256]{1,0:T(8,128)S(1)}, u32[]{:S(2)}, u32[]{:S(2)}) %collective-permute-start.3) | collective-permute-done | bytes 262176 | tf_op jit(solution)/shard_map/ppermute | solution.py:36
  75.5 0.7 copy-done.9
  76.2 1.5 %collective-permute-start.5 = (f32[512,128]{1,0:T(8,128)}, f32[512,128]{1,0:T(8,128)S(1)}, u32[]{:S(2)}, u32[]{:S(2)}) collective-permute-start(f32[512,128]{1,0:T(8,128)} %bitcast.24), channel_id=1, source_target_pairs={{0,15},{1,14},{2,9},{3,8},{4,11},{5,10},{6,13},{7,12},{8,7},{9,6},... | collective-permute-start | bytes 786440 | tf_op jit(solution)/shard_map/ppermute | solution.py:49
  77.7 3.7 %collective-permute-done.2.c_ref = f32[256,256]{1,0:T(8,128)} collective-permute-done((f32[256,256]{1,0:T(8,128)}, f32[256,256]{1,0:T(8,128)}, u32[]{:S(2)}, u32[]{:S(2)}) %collective-permute-start.2) | collective-permute-done | bytes 262176 | tf_op jit(solution)/shard_map/ppermute | solution.py:36
  81.7 4.2 %collective-permute-start.7 = (f32[512,128]{1,0:T(8,128)}, f32[512,128]{1,0:T(8,128)}, u32[]{:S(2)}, u32[]{:S(2)}) collective-permute-start(f32[512,128]{1,0:T(8,128)} %bitcast.22), channel_id=1, source_target_pairs={{0,13},{1,12},{2,15},{3,14},{4,9},{5,8},{6,11},{7,10},{8,5},{9,4},... | collective-permute-start | bytes 786440 | tf_op jit(solution)/shard_map/ppermute | solution.py:49
  85.9 2.1 %make_table.1.refs_0_ = f32[256,256]{1,0:T(8,128)} custom-call(f32[256,256]{1,0:T(8,128)} %choose.1.a_ref, f32[256,256]{1,0:T(8,128)} %collective-permute-done.1.b_ref, f32[256,256]{1,0:T(8,128)} %collective-permute-done.2.c_ref, f32[256,256]{1,0:T(8,128)} %copy-done.9, s32[1,256]{1,0:T(1,128)} %bitcast.17), custom_call_target="tpu_custom_call" | custom-call | tf_op jit(solution)/shard_map/make_table/pallas_call | solution.py:184
  88.1 11.5 %shard_map.46.refs_3_ = s32[4096,256]{1,0:T(8,128)} custom-call(f32[256,256]{1,0:T(8,128)} %make_table.1.refs_0_, f32[2,512,128]{2,1,0:T(8,128)} %bitcast.16, f32[2,512,128]{2,1,0:T(8,128)} %copy-done.5, f32[2,512,128]{2,1,0:T(8,128)} %copy-done.1, f32[2,512,128]{2,1,0:T(8,128)} %collective-permute-done.12.refs_4_, f32[2,512,128]{2,1,0:T(8,128)} %copy-done.2, ...), custom_call_target="tpu_custom_call" | custom-call | tf_op jit(solution)/shard_map/pallas_call | solution.py:264
  99.6 3.6 %shard_map.47.refs_5_ = s32[4096,256]{1,0:T(8,128)} custom-call(f32[256,256]{1,0:T(8,128)} %make_table.1.refs_0_, f32[512,128]{1,0:T(8,128)} %copy-done.6, f32[512,128]{1,0:T(8,128)} %collective-permute-done.9.refs_2_, s32[4096,256]{1,0:T(8,128)} %shard_map.46.refs_3_), custom_call_target="tpu_custom_call", output_to_operand_aliasing={{}: (3, {})} | custom-call | tf_op jit(solution)/shard_map/pallas_call | solution.py:264
  104.1 5.6 %shard_map.48 = s32[4096,256]{1,0:T(8,128)} custom-call(f32[256,256]{1,0:T(8,128)} %make_table.1.refs_0_, f32[512,128]{1,0:T(8,128)} %copy-done.7, f32[512,128]{1,0:T(8,128)} %copy-done.8, f32[512,128]{1,0:T(8,128)} %collective-permute-done.6.refs_3_, f32[512,128]{1,0:T(8,128)} %collective-permute-done.7.refs_4_, ...), custom_call_target="tpu_custom_call", output_to_operand_aliasing={{}: (5, {})} | custom-call | tf_op jit(solution)/shard_map/pallas_call | solution.py:264
  (44 shorter events, 3.0 us)
Async XLA Ops:
  0.0 59.3 %copy-start.10 = (s32[4096]{0:T(1024)S(1)}, s32[4096]{0:T(1024)}, u32[]{:S(2)}) copy-start(s32[4096]{0:T(1024)} %param.6) | copy-start | bytes 49156
  0.0 59.3 %copy-start.11 = (s32[4096]{0:T(1024)S(1)}, s32[4096]{0:T(1024)}, u32[]{:S(2)}) copy-start(s32[4096]{0:T(1024)} %param.7) | copy-start | bytes 49156
  12.1 23.1 %all-to-all-start = ((f32[16,32,256]{2,1,0:T(8,128)}), f32[16,32,256]{2,1,0:T(8,128)S(1)}, u32[]{:S(2)}, u32[]{:S(2)}) async-start(f32[16,32,256]{2,1,0:T(8,128)} %broadcast_in_dim.38), calls=%async_computation | async-start | bytes 1048576 | tf_op jit(solution)/shard_map/all_to_all | solution.py:292
  19.7 15.5 %collective-permute-start.8 = (f32[512,128]{1,0:T(8,128)}, f32[512,128]{1,0:T(8,128)S(1)}, u32[]{:S(2)}, u32[]{:S(2)}) collective-permute-start(f32[512,128]{1,0:T(8,128)} %bitcast.27), channel_id=1, source_target_pairs={{0,2},{1,3},{2,4},{3,5},{4,6},{5,7},{6,0},{7,1},{8,10},{9,11},{10,... | collective-permute-start | bytes 786440 | tf_op jit(solution)/shard_map/ppermute | solution.py:49
  21.0 18.8 %collective-permute-start.11 = (f32[2,512,128]{2,1,0:T(8,128)}, f32[2,512,128]{2,1,0:T(8,128)S(1)}, u32[]{:S(2)}, u32[]{:S(2)}) collective-permute-start(f32[2,512,128]{2,1,0:T(8,128)} %bitcast.21), channel_id=1, source_target_pairs={{0,8},{1,9},{2,10},{3,11},{4,12},{5,13},{6,14},{7,15},{8,0},{9,1},... | collective-permute-start | bytes 1572872 | tf_op jit(solution)/shard_map/ppermute | solution.py:49
  22.2 22.9 %collective-permute-start.13 = (f32[2,512,128]{2,1,0:T(8,128)}, f32[2,512,128]{2,1,0:T(8,128)S(1)}, u32[]{:S(2)}, u32[]{:S(2)}) collective-permute-start(f32[2,512,128]{2,1,0:T(8,128)} %bitcast.20), channel_id=1, source_target_pairs={{0,4},{1,5},{2,6},{3,7},{4,0},{5,1},{6,2},{7,3},{8,12},{9,13},{10,... | collective-permute-start | bytes 1572872 | tf_op jit(solution)/shard_map/ppermute | solution.py:49
  24.6 33.3 %collective-permute-start.15 = (f32[2,512,128]{2,1,0:T(8,128)}, f32[2,512,128]{2,1,0:T(8,128)S(1)}, u32[]{:S(2)}, u32[]{:S(2)}) collective-permute-start(f32[2,512,128]{2,1,0:T(8,128)} %bitcast.19), channel_id=1, source_target_pairs={{0,10},{1,11},{2,12},{3,13},{4,14},{5,15},{6,8},{7,9},{8,2},{9,3},... | collective-permute-start | bytes 1572872 | tf_op jit(solution)/shard_map/ppermute | solution.py:49
  24.6 34.1 %collective-permute-start.17 = (f32[2,512,128]{2,1,0:T(8,128)}, f32[2,512,128]{2,1,0:T(8,128)S(1)}, u32[]{:S(2)}, u32[]{:S(2)}) collective-permute-start(f32[2,512,128]{2,1,0:T(8,128)} %bitcast.18), channel_id=1, source_target_pairs={{0,6},{1,7},{2,0},{3,1},{4,2},{5,3},{6,4},{7,5},{8,14},{9,15},{10,... | collective-permute-start | bytes 1572872 | tf_op jit(solution)/shard_map/ppermute | solution.py:49
  35.2 64.5 %copy-start.6 = (f32[512,128]{1,0:T(8,128)}, f32[512,128]{1,0:T(8,128)S(1)}, u32[]{:S(2)}) copy-start(f32[512,128]{1,0:T(8,128)S(1)} %collective-permute-done.8.refs_1_) | copy-start | bytes 786436
  35.2 26.6 %copy-start = (f32[16,32,256]{2,1,0:T(8,128)}, f32[16,32,256]{2,1,0:T(8,128)S(1)}, u32[]{:S(2)}) copy-start(f32[16,32,256]{2,1,0:T(8,128)S(1)} %all-to-all-done) | copy-start | bytes 1572868
  35.2 23.6 %collective-permute-start = (f32[512,256]{1,0:T(8,128)S(1)}, f32[512,256]{1,0:T(8,128)}, u32[]{:S(2)}, u32[]{:S(2)}) collective-permute-start(f32[512,256]{1,0:T(8,128)S(1)} %bitcast.13), channel_id=1, source_target_pairs={{0,1},{1,0},{2,3},{3,2},{4,5},{5,4},{6,7},{7,6},{8,9},{9,8},{10,11... | collective-permute-start | bytes 1572872 | tf_op jit(solution)/shard_map/ppermute | solution.py:40
  39.8 48.2 %copy-start.1 = (f32[2,512,128]{2,1,0:T(8,128)}, f32[2,512,128]{2,1,0:T(8,128)S(1)}, u32[]{:S(2)}) copy-start(f32[2,512,128]{2,1,0:T(8,128)S(1)} %collective-permute-done.11.refs_3_) | copy-start | bytes 1572868
  39.8 25.3 %collective-permute-start.10 = (f32[2,512,128]{2,1,0:T(8,128)}, f32[2,512,128]{2,1,0:T(8,128)S(1)}, u32[]{:S(2)}, u32[]{:S(2)}) collective-permute-start(f32[2,512,128]{2,1,0:T(8,128)} %bitcast.15), channel_id=1, source_target_pairs={{0,1},{1,0},{2,3},{3,2},{4,5},{5,4},{6,7},{7,6},{8,9},{9,8},{10,11... | collective-permute-start | bytes 1572872 | tf_op jit(solution)/shard_map/ppermute | solution.py:40
  45.2 42.9 %copy-start.2 = (f32[2,512,128]{2,1,0:T(8,128)}, f32[2,512,128]{2,1,0:T(8,128)S(1)}, u32[]{:S(2)}) copy-start(f32[2,512,128]{2,1,0:T(8,128)S(1)} %collective-permute-done.13.refs_5_) | copy-start | bytes 1572868
  45.2 23.5 %collective-permute-start.12 = (f32[2,512,128]{2,1,0:T(8,128)S(1)}, f32[2,512,128]{2,1,0:T(8,128)}, u32[]{:S(2)}, u32[]{:S(2)}) collective-permute-start(f32[2,512,128]{2,1,0:T(8,128)S(1)} %collective-permute-done.11.refs_3_), channel_id=1, source_target_pairs={{0,1},{1,0},{2,3},{3,2},{4,5},{5,4},{6,7},{7,6},{8,9},{9,8},{10,11... | collective-permute-start | bytes 1572872 | tf_op jit(solution)/shard_map/ppermute | solution.py:40
  57.9 30.2 %copy-start.3 = (f32[2,512,128]{2,1,0:T(8,128)}, f32[2,512,128]{2,1,0:T(8,128)S(1)}, u32[]{:S(2)}) copy-start(f32[2,512,128]{2,1,0:T(8,128)S(1)} %collective-permute-done.15.refs_7_) | copy-start | bytes 1572868
  57.9 11.5 %collective-permute-start.14 = (f32[2,512,128]{2,1,0:T(8,128)S(1)}, f32[2,512,128]{2,1,0:T(8,128)}, u32[]{:S(2)}, u32[]{:S(2)}) collective-permute-start(f32[2,512,128]{2,1,0:T(8,128)S(1)} %collective-permute-done.13.refs_5_), channel_id=1, source_target_pairs={{0,1},{1,0},{2,3},{3,2},{4,5},{5,4},{6,7},{7,6},{8,9},{9,8},{10,11... | collective-permute-start | bytes 1572872 | tf_op jit(solution)/shard_map/ppermute | solution.py:40
  58.7 29.4 %copy-start.4 = (f32[2,512,128]{2,1,0:T(8,128)}, f32[2,512,128]{2,1,0:T(8,128)S(1)}, u32[]{:S(2)}) copy-start(f32[2,512,128]{2,1,0:T(8,128)S(1)} %collective-permute-done.17.refs_9_) | copy-start | bytes 1572868
  58.7 12.7 %collective-permute-start.16 = (f32[2,512,128]{2,1,0:T(8,128)S(1)}, f32[2,512,128]{2,1,0:T(8,128)}, u32[]{:S(2)}, u32[]{:S(2)}) collective-permute-start(f32[2,512,128]{2,1,0:T(8,128)S(1)} %collective-permute-done.15.refs_7_), channel_id=1, source_target_pairs={{0,1},{1,0},{2,3},{3,2},{4,5},{5,4},{6,7},{7,6},{8,9},{9,8},{10,11... | collective-permute-start | bytes 1572872 | tf_op jit(solution)/shard_map/ppermute | solution.py:40
  58.8 13.2 %collective-permute-start.18 = (f32[2,512,128]{2,1,0:T(8,128)S(1)}, f32[2,512,128]{2,1,0:T(8,128)}, u32[]{:S(2)}, u32[]{:S(2)}) collective-permute-start(f32[2,512,128]{2,1,0:T(8,128)S(1)} %collective-permute-done.17.refs_9_), channel_id=1, source_target_pairs={{0,1},{1,0},{2,3},{3,2},{4,5},{5,4},{6,7},{7,6},{8,9},{9,8},{10,11... | collective-permute-start | bytes 1572872 | tf_op jit(solution)/shard_map/ppermute | solution.py:40
  65.1 23.0 %copy-start.5 = (f32[2,512,128]{2,1,0:T(8,128)}, f32[2,512,128]{2,1,0:T(8,128)S(1)}, u32[]{:S(2)}) copy-start(f32[2,512,128]{2,1,0:T(8,128)S(1)} %collective-permute-done.10.refs_2_) | copy-start | bytes 1572868
  65.1 10.4 %collective-permute-start.3 = (f32[256,256]{1,0:T(8,128)}, f32[256,256]{1,0:T(8,128)S(1)}, u32[]{:S(2)}, u32[]{:S(2)}) collective-permute-start(f32[256,256]{1,0:T(8,128)} %choose.1.a_ref), channel_id=1, source_target_pairs={{32,0},{48,16},{0,32},{16,48},{96,64},{112,80},{64,96},{80,112},{3... | collective-permute-start | bytes 786440 | tf_op jit(solution)/shard_map/ppermute | solution.py:36
  68.7 12.7 %collective-permute-start.2 = (f32[256,256]{1,0:T(8,128)}, f32[256,256]{1,0:T(8,128)}, u32[]{:S(2)}, u32[]{:S(2)}) collective-permute-start(f32[256,256]{1,0:T(8,128)} %choose.1.a_ref), channel_id=1, source_target_pairs={{48,0},{0,16},{16,32},{32,48},{112,64},{64,80},{80,96},{96,112},{4... | collective-permute-start | bytes 786440 | tf_op jit(solution)/shard_map/ppermute | solution.py:36
  69.4 12.3 %collective-permute-start.1 = (f32[256,256]{1,0:T(8,128)}, f32[256,256]{1,0:T(8,128)}, u32[]{:S(2)}, u32[]{:S(2)}) collective-permute-start(f32[256,256]{1,0:T(8,128)} %choose.1.a_ref), channel_id=1, source_target_pairs={{16,0},{32,16},{48,32},{0,48},{80,64},{96,80},{112,96},{64,112},{1... | collective-permute-start | bytes 786440 | tf_op jit(solution)/shard_map/ppermute | solution.py:36
  71.4 31.9 %collective-permute-start.4 = (f32[512,128]{1,0:T(8,128)}, f32[512,128]{1,0:T(8,128)S(1)}, u32[]{:S(2)}, u32[]{:S(2)}) collective-permute-start(f32[512,128]{1,0:T(8,128)} %bitcast.25), channel_id=1, source_target_pairs={{0,14},{1,15},{2,8},{3,9},{4,10},{5,11},{6,12},{7,13},{8,6},{9,7},... | collective-permute-start | bytes 786440 | tf_op jit(solution)/shard_map/ppermute | solution.py:49
  72.0 27.6 %collective-permute-start.9 = (f32[512,128]{1,0:T(8,128)}, f32[512,128]{1,0:T(8,128)}, u32[]{:S(2)}, u32[]{:S(2)}) collective-permute-start(f32[512,128]{1,0:T(8,128)} %bitcast.26), channel_id=1, source_target_pairs={{0,3},{1,2},{2,5},{3,4},{4,7},{5,6},{6,1},{7,0},{8,11},{9,10},{10,... | collective-permute-start | bytes 786440 | tf_op jit(solution)/shard_map/ppermute | solution.py:49
  75.5 0.7 copy-start.9
  76.2 27.1 %collective-permute-start.5 = (f32[512,128]{1,0:T(8,128)}, f32[512,128]{1,0:T(8,128)S(1)}, u32[]{:S(2)}, u32[]{:S(2)}) collective-permute-start(f32[512,128]{1,0:T(8,128)} %bitcast.24), channel_id=1, source_target_pairs={{0,15},{1,14},{2,9},{3,8},{4,11},{5,10},{6,13},{7,12},{8,7},{9,6},... | collective-permute-start | bytes 786440 | tf_op jit(solution)/shard_map/ppermute | solution.py:49
  81.4 21.9 %collective-permute-start.6 = (f32[512,128]{1,0:T(8,128)}, f32[512,128]{1,0:T(8,128)}, u32[]{:S(2)}, u32[]{:S(2)}) collective-permute-start(f32[512,128]{1,0:T(8,128)} %bitcast.23), channel_id=1, source_target_pairs={{0,12},{1,13},{2,14},{3,15},{4,8},{5,9},{6,10},{7,11},{8,4},{9,5},... | collective-permute-start | bytes 786440 | tf_op jit(solution)/shard_map/ppermute | solution.py:49
  81.7 21.6 %collective-permute-start.7 = (f32[512,128]{1,0:T(8,128)}, f32[512,128]{1,0:T(8,128)}, u32[]{:S(2)}, u32[]{:S(2)}) collective-permute-start(f32[512,128]{1,0:T(8,128)} %bitcast.22), channel_id=1, source_target_pairs={{0,13},{1,12},{2,15},{3,14},{4,9},{5,8},{6,11},{7,10},{8,5},{9,4},... | collective-permute-start | bytes 786440 | tf_op jit(solution)/shard_map/ppermute | solution.py:49
  103.3 0.7 copy-start.7
  103.3 0.8 copy-start.8

commit v5 on v4

--- a/solution.py
+++ b/solution.py
@@ -13,7 +13,7 @@
 SPAN = 256
 FEATURES = 4096
 EARLY = ((1, 0), (0, 2), (1, 1), (0, 3))
-LATE = ((0, 1), (1, 3), (1, 2))
+LATE = ((1, 3), (0, 1), (1, 2))
 GROUP = 1024
 SUB = 256
 
@@ -282,17 +282,15 @@
 def step(raw_values, bin_edges, feature_column, bin_offset):
     row, bundle = lax.axis_index("rows"), lax.axis_index("bundle")
     z, core = row % SIDE, bundle % 2
+    copies = jnp.broadcast_to(jnp.pad(bin_edges, ((0, 0), (0, 1)))[None], (16, PIECE, EDGES))
+    mine = lax.all_to_all(copies, AXES, split_axis=0, concat_axis=0, axis_index_groups=planes(), tiled=True)
+    mine = mine.reshape(512, EDGES)
+
     x, y_low = (bundle // 2) % SIDE, bundle // 8
     owner, inside = feature_column // SPAN, feature_column % SPAN
     chip = (owner // 8 ^ y_low) * SIDE + ((owner // 2) % SIDE - x) % SIDE
     spot = chip * 512 + (owner % 2 ^ core) * 256 + inside
     pieces = list(prep(spot, raw_values))
-    copies = jnp.broadcast_to(jnp.pad(bin_edges, ((0, 0), (0, 1)))[None], (16, PIECE, EDGES))
-    copies, pieces[0] = lax.optimization_barrier((copies, pieces[0]))
-    mine = lax.all_to_all(
-        copies, AXES, split_axis=0, concat_axis=0, axis_index_groups=planes(), tiled=True
-    )
-    mine = mine.reshape(512, EDGES)
     sent = [value.reshape(2, 512, 128) for value in pieces[: 1 + len(EARLY)]]
     halves = [value.reshape(512, 128) for value in pieces[1 + len(EARLY) :]]
     arrived = [sent[0]]
@@ -321,10 +319,11 @@
     for value in arrived:
         parts += [value, swap_cores(value)]
     out = bin_chips(((0, 0), *EARLY), table, parts, None)
-    *middle, out = lax.optimization_barrier((*direct[:2], out))
-    out = bin_chips(LATE[:1], table, middle, out)
-    *last, out = lax.optimization_barrier((*direct[2:], out))
-    return bin_chips(LATE[1:], table, last, out)
+    *middle, out = lax.optimization_barrier((*direct[2:4], out))
+    out = bin_chips(LATE[1:2], table, middle, out)
+    last = direct[0:2] + direct[4:6]
+    *last, out = lax.optimization_barrier((*last, out))
+    return bin_chips((LATE[0], LATE[2]), table, last, out)
 
 
 def solution(mesh):

time: 110 us -> 105 us (0.955)
  waiting for transfers between devices: 29.7 us -> 20.7 us
  starting transfers between devices: 37.6 us -> 41.3 us
    ppermute x10, waiting for transfers between devices: 24.5 us -> 14.7 us  [to_chip(): return lax.ppermute(value, 'bundle', pairs)]
    ppermute x6, starting transfers between devices: 7.53 us -> 12 us  [swap_cores(): return lax.ppermute(value, 'bundle', [(i, i ^ 1) for i in range(16)])]
  transfers between devices with their start and end apart: 20 -> 20, of which waited for: 6 -> 6; matrix products, arithmetic and copies ran while one was open for 2% -> 4% of each run, Pallas kernels for 19% -> 28%
where the time goes in v5:
time: 105 us; the launch traced here: 104 us
  starting transfers between devices  41.3 us (39%)
  Pallas kernels  35.3 us (34%)
  waiting for transfers between devices  20.7 us (20%)
  other arithmetic  3.86 us (4%)
  local copies, waits for them, and re-layouts  3.11 us (3%)
    pallas_call x3, Pallas kernels, bin_chips(): pl.pallas_call(lambda *refs: bin_kernel(*refs, chips=chips, fresh=fresh),...  20.8 us
    ppermute x10, starting transfers between devices, to_chip(): return lax.ppermute(value, 'bundle', pairs)  15.4 us
    ppermute x10, waiting for transfers between devices, to_chip(): return lax.ppermute(value, 'bundle', pairs)  14.7 us
    ppermute x6, starting transfers between devices, swap_cores(): return lax.ppermute(value, 'bundle', [(i, i ^ 1) for i in range(16)])  12 us
    pallas_call x1, Pallas kernels, prep(): pl.pallas_call(prep_kernel, grid_spec=pltpu.PrefetchScalarGridSpec(num_sc...  9.05 us
    all_to_all x1, starting transfers between devices, step(): lax.all_to_all(copies, AXES, split_axis=0, concat_axis=0, axis_index_grou...  7.57 us
    ppermute x3, starting transfers between devices, along_z(): return lax.ppermute(value, 'rows', pairs)  6.28 us
    ppermute x3, waiting for transfers between devices, along_z(): return lax.ppermute(value, 'rows', pairs)  6.03 us
  transfers between devices with their start and end apart: 20, of which 6 were waited for; matrix products, arithmetic and copies ran while one was open for 4% of the time, Pallas kernels for 28%

profile of v5, /device:TPU:1, one launch (start us, length us, event | category | flops | bytes accessed | tf_op | source)
XLA Modules:
  0.0 104.5 jit_solution(3033793624499120092)
XLA Ops:
  0.0 0.8 pad.4
  0.8 0.8 broadcast_in_dim.38
  1.6 7.6 %all-to-all-start = ((f32[16,32,256]{2,1,0:T(8,128)}), f32[16,32,256]{2,1,0:T(8,128)S(1)}, u32[]{:S(2)}, u32[]{:S(2)}) async-start(f32[16,32,256]{2,1,0:T(8,128)} %broadcast_in_dim.38), calls=%async_computation | async-start | bytes 1048576 | tf_op jit(solution)/shard_map/all_to_all | solution.py:286
  9.3 1.4 %fusion.8.spot_ref = s32[4096]{0:T(1024)} fusion(s32[4096]{0:T(1024)} %param.6, s32[]{:T(128)S(6)} %select_n.110, s32[]{:T(128)S(6)} %select_n.126, s32[]{:T(128)S(6)} %select_n.122), kind=kLoop, calls=%fused_computation.29 | loop fusion | flops 323584 | bytes 32780 | tf_op jit(solution)/shard_map/add | solution.py:292
  10.6 9.1 %prep.1 = (f32[512,2,128]{2,1,0:T(2,128)}, f32[512,2,128]{2,1,0:T(2,128)}, f32[512,2,128]{2,1,0:T(2,128)}, f32[512,2,128]{2,1,0:T(2,128)}, f32[512,2,128]{2,1,0:...) custom-call(s32[4096]{0:T(1024)} %fusion.8.spot_ref, ...), custom_call_target="tpu_custom_call" | custom-call | tf_op jit(solution)/shard_map/prep/pallas_call | solution.py:128
  19.7 1.4 %collective-permute-start.8 = (f32[512,128]{1,0:T(8,128)}, f32[512,128]{1,0:T(8,128)S(1)}, u32[]{:S(2)}, u32[]{:S(2)}) collective-permute-start(f32[512,128]{1,0:T(8,128)} %bitcast.27), channel_id=1, source_target_pairs={{0,2},{1,3},{2,4},{3,5},{4,6},{5,7},{6,0},{7,1},{8,10},{9,11},{10,... | collective-permute-start | bytes 786440 | tf_op jit(solution)/shard_map/ppermute | solution.py:49
  21.1 1.2 %collective-permute-start.11 = (f32[2,512,128]{2,1,0:T(8,128)}, f32[2,512,128]{2,1,0:T(8,128)S(1)}, u32[]{:S(2)}, u32[]{:S(2)}) collective-permute-start(f32[2,512,128]{2,1,0:T(8,128)} %bitcast.21), channel_id=1, source_target_pairs={{0,8},{1,9},{2,10},{3,11},{4,12},{5,13},{6,14},{7,15},{8,0},{9,1},... | collective-permute-start | bytes 1572872 | tf_op jit(solution)/shard_map/ppermute | solution.py:49
  22.3 2.4 %collective-permute-start.13 = (f32[2,512,128]{2,1,0:T(8,128)}, f32[2,512,128]{2,1,0:T(8,128)S(1)}, u32[]{:S(2)}, u32[]{:S(2)}) collective-permute-start(f32[2,512,128]{2,1,0:T(8,128)} %bitcast.20), channel_id=1, source_target_pairs={{0,4},{1,5},{2,6},{3,7},{4,0},{5,1},{6,2},{7,3},{8,12},{9,13},{10,... | collective-permute-start | bytes 1572872 | tf_op jit(solution)/shard_map/ppermute | solution.py:49
  24.7 2.7 %collective-permute-start.17 = (f32[2,512,128]{2,1,0:T(8,128)}, f32[2,512,128]{2,1,0:T(8,128)S(1)}, u32[]{:S(2)}, u32[]{:S(2)}) collective-permute-start(f32[2,512,128]{2,1,0:T(8,128)} %bitcast.18), channel_id=1, source_target_pairs={{0,6},{1,7},{2,0},{3,1},{4,2},{5,3},{6,4},{7,5},{8,14},{9,15},{10,... | collective-permute-start | bytes 1572872 | tf_op jit(solution)/shard_map/ppermute | solution.py:49
  27.3 0.8 collective-permute-done.8.refs_1_
  28.1 4.0 %collective-permute-start = (f32[512,256]{1,0:T(8,128)S(1)}, f32[512,256]{1,0:T(8,128)}, u32[]{:S(2)}, u32[]{:S(2)}) collective-permute-start(f32[512,256]{1,0:T(8,128)S(1)} %bitcast.13), channel_id=1, source_target_pairs={{0,1},{1,0},{2,3},{3,2},{4,5},{5,4},{6,7},{7,6},{8,9},{9,8},{10,11... | collective-permute-start | bytes 1572872 | tf_op jit(solution)/shard_map/ppermute | solution.py:40
  32.1 2.2 %collective-permute-done.11.refs_3_ = f32[2,512,128]{2,1,0:T(8,128)S(1)} collective-permute-done((f32[2,512,128]{2,1,0:T(8,128)}, f32[2,512,128]{2,1,0:T(8,128)S(1)}, u32[]{:S(2)}, u32[]{:S(2)}) %collective-permute-start.11) | collective-permute-done | bytes 524320 | tf_op jit(solution)/shard_map/ppermute | solution.py:49
  34.3 2.4 %collective-permute-start.10 = (f32[2,512,128]{2,1,0:T(8,128)}, f32[2,512,128]{2,1,0:T(8,128)S(1)}, u32[]{:S(2)}, u32[]{:S(2)}) collective-permute-start(f32[2,512,128]{2,1,0:T(8,128)} %bitcast.15), channel_id=1, source_target_pairs={{0,1},{1,0},{2,3},{3,2},{4,5},{5,4},{6,7},{7,6},{8,9},{9,8},{10,11... | collective-permute-start | bytes 1572872 | tf_op jit(solution)/shard_map/ppermute | solution.py:40
  36.6 3.5 %collective-permute-done.13.refs_5_ = f32[2,512,128]{2,1,0:T(8,128)S(1)} collective-permute-done((f32[2,512,128]{2,1,0:T(8,128)}, f32[2,512,128]{2,1,0:T(8,128)S(1)}, u32[]{:S(2)}, u32[]{:S(2)}) %collective-permute-start.13) | collective-permute-done | bytes 524320 | tf_op jit(solution)/shard_map/ppermute | solution.py:49
  40.1 3.8 %collective-permute-start.12 = (f32[2,512,128]{2,1,0:T(8,128)S(1)}, f32[2,512,128]{2,1,0:T(8,128)}, u32[]{:S(2)}, u32[]{:S(2)}) collective-permute-start(f32[2,512,128]{2,1,0:T(8,128)S(1)} %collective-permute-done.11.refs_3_), channel_id=1, source_target_pairs={{0,1},{1,0},{2,3},{3,2},{4,5},{5,4},{6,7},{7,6},{8,9},{9,8},{10,11... | collective-permute-start | bytes 1572872 | tf_op jit(solution)/shard_map/ppermute | solution.py:40
  43.9 8.2 %collective-permute-done.15.refs_7_ = f32[2,512,128]{2,1,0:T(8,128)S(1)} collective-permute-done((f32[2,512,128]{2,1,0:T(8,128)}, f32[2,512,128]{2,1,0:T(8,128)S(1)}, u32[]{:S(2)}, u32[]{:S(2)}) %collective-permute-start.15) | collective-permute-done | bytes 524320 | tf_op jit(solution)/shard_map/ppermute | solution.py:49
  52.2 1.3 %collective-permute-start.14 = (f32[2,512,128]{2,1,0:T(8,128)S(1)}, f32[2,512,128]{2,1,0:T(8,128)}, u32[]{:S(2)}, u32[]{:S(2)}) collective-permute-start(f32[2,512,128]{2,1,0:T(8,128)S(1)} %collective-permute-done.13.refs_5_), channel_id=1, source_target_pairs={{0,1},{1,0},{2,3},{3,2},{4,5},{5,4},{6,7},{7,6},{8,9},{9,8},{10,11... | collective-permute-start | bytes 1572872 | tf_op jit(solution)/shard_map/ppermute | solution.py:40
  54.0 1.9 %fusion.1 = (s32[256]{0:T(256)}, s32[256]{0:T(256)S(1)}) fusion(s32[4096]{0:T(1024)S(1)} %copy-done.11, s32[4096]{0:T(1024)S(1)} %copy-done.10, s32[256]{0:T(256)S(1)} %iota_add_fusion), kind=kLoop, calls=%fused_computation.3 | loop fusion | flops 5242368 | bytes 35840 | tf_op jit(solution)/shard_map/reduce_max | solution.py:307
  56.5 3.3 %choose.1.a_ref = f32[256,256]{1,0:T(8,128)} custom-call(s32[256]{0:T(256)} %compare_select_fusion.9.row_ref, f32[512,256]{1,0:T(8,128)} %bitcast.14, f32[512,256]{1,0:T(8,128)} %collective-permute-done.other_ref), custom_call_target="tpu_custom_call" | custom-call | tf_op jit(solution)/shard_map/choose/pallas_call | solution.py:158
  59.8 3.6 %collective-permute-start.3 = (f32[256,256]{1,0:T(8,128)}, f32[256,256]{1,0:T(8,128)S(1)}, u32[]{:S(2)}, u32[]{:S(2)}) collective-permute-start(f32[256,256]{1,0:T(8,128)} %choose.1.a_ref), channel_id=1, source_target_pairs={{32,0},{48,16},{0,32},{16,48},{96,64},{112,80},{64,96},{80,112},{3... | collective-permute-start | bytes 786440 | tf_op jit(solution)/shard_map/ppermute | solution.py:36
  63.4 0.7 collective-permute-start.2
  64.2 1.9 %collective-permute-start.1 = (f32[256,256]{1,0:T(8,128)}, f32[256,256]{1,0:T(8,128)}, u32[]{:S(2)}, u32[]{:S(2)}) collective-permute-start(f32[256,256]{1,0:T(8,128)} %choose.1.a_ref), channel_id=1, source_target_pairs={{16,0},{32,16},{48,32},{0,48},{80,64},{96,80},{112,96},{64,112},{1... | collective-permute-start | bytes 786440 | tf_op jit(solution)/shard_map/ppermute | solution.py:36
  66.1 2.1 %collective-permute-start.5 = (f32[512,128]{1,0:T(8,128)}, f32[512,128]{1,0:T(8,128)S(1)}, u32[]{:S(2)}, u32[]{:S(2)}) collective-permute-start(f32[512,128]{1,0:T(8,128)} %bitcast.25), channel_id=1, source_target_pairs={{0,15},{1,14},{2,9},{3,8},{4,11},{5,10},{6,13},{7,12},{8,7},{9,6},... | collective-permute-start | bytes 786440 | tf_op jit(solution)/shard_map/ppermute | solution.py:49
  68.2 2.1 %collective-permute-done.3.d_ref = f32[256,256]{1,0:T(8,128)S(1)} collective-permute-done((f32[256,256]{1,0:T(8,128)}, f32[256,256]{1,0:T(8,128)S(1)}, u32[]{:S(2)}, u32[]{:S(2)}) %collective-permute-start.3) | collective-permute-done | bytes 262176 | tf_op jit(solution)/shard_map/ppermute | solution.py:36
  71.0 1.2 %collective-permute-start.4 = (f32[512,128]{1,0:T(8,128)}, f32[512,128]{1,0:T(8,128)S(1)}, u32[]{:S(2)}, u32[]{:S(2)}) collective-permute-start(f32[512,128]{1,0:T(8,128)} %bitcast.24), channel_id=1, source_target_pairs={{0,14},{1,15},{2,8},{3,9},{4,10},{5,11},{6,12},{7,13},{8,6},{9,7},... | collective-permute-start | bytes 786440 | tf_op jit(solution)/shard_map/ppermute | solution.py:49
  72.2 3.9 %collective-permute-done.2.c_ref = f32[256,256]{1,0:T(8,128)} collective-permute-done((f32[256,256]{1,0:T(8,128)}, f32[256,256]{1,0:T(8,128)}, u32[]{:S(2)}, u32[]{:S(2)}) %collective-permute-start.2) | collective-permute-done | bytes 262176 | tf_op jit(solution)/shard_map/ppermute | solution.py:36
  76.1 1.5 %collective-permute-start.6 = (f32[512,128]{1,0:T(8,128)}, f32[512,128]{1,0:T(8,128)}, u32[]{:S(2)}, u32[]{:S(2)}) collective-permute-start(f32[512,128]{1,0:T(8,128)} %bitcast.23), channel_id=1, source_target_pairs={{0,12},{1,13},{2,14},{3,15},{4,8},{5,9},{6,10},{7,11},{8,4},{9,5},... | collective-permute-start | bytes 786440 | tf_op jit(solution)/shard_map/ppermute | solution.py:49
  77.6 3.0 %collective-permute-start.7 = (f32[512,128]{1,0:T(8,128)}, f32[512,128]{1,0:T(8,128)}, u32[]{:S(2)}, u32[]{:S(2)}) collective-permute-start(f32[512,128]{1,0:T(8,128)} %bitcast.22), channel_id=1, source_target_pairs={{0,13},{1,12},{2,15},{3,14},{4,9},{5,8},{6,11},{7,10},{8,5},{9,4},... | collective-permute-start | bytes 786440 | tf_op jit(solution)/shard_map/ppermute | solution.py:49
  80.7 2.1 %make_table.1.refs_0_ = f32[256,256]{1,0:T(8,128)} custom-call(f32[256,256]{1,0:T(8,128)} %choose.1.a_ref, f32[256,256]{1,0:T(8,128)} %collective-permute-done.1.b_ref, f32[256,256]{1,0:T(8,128)} %collective-permute-done.2.c_ref, f32[256,256]{1,0:T(8,128)} %copy-done.9, s32[1,256]{1,0:T(1,128)} %bitcast.17), custom_call_target="tpu_custom_call" | custom-call | tf_op jit(solution)/shard_map/make_table/pallas_call | solution.py:184
  82.8 11.5 %shard_map.46.refs_3_ = s32[4096,256]{1,0:T(8,128)} custom-call(f32[256,256]{1,0:T(8,128)} %make_table.1.refs_0_, f32[2,512,128]{2,1,0:T(8,128)} %bitcast.16, f32[2,512,128]{2,1,0:T(8,128)} %copy-done.5, f32[2,512,128]{2,1,0:T(8,128)} %copy-done.1, f32[2,512,128]{2,1,0:T(8,128)} %collective-permute-done.12.refs_4_, f32[2,512,128]{2,1,0:T(8,128)} %copy-done.2, ...), custom_call_target="tpu_custom_call" | custom-call | tf_op jit(solution)/shard_map/pallas_call | solution.py:264
  94.4 3.6 %shard_map.47.refs_5_ = s32[4096,256]{1,0:T(8,128)} custom-call(f32[256,256]{1,0:T(8,128)} %make_table.1.refs_0_, f32[512,128]{1,0:T(8,128)} %copy-done.6, f32[512,128]{1,0:T(8,128)} %collective-permute-done.9.refs_2_, s32[4096,256]{1,0:T(8,128)} %shard_map.46.refs_3_), custom_call_target="tpu_custom_call", output_to_operand_aliasing={{}: (3, {})} | custom-call | tf_op jit(solution)/shard_map/pallas_call | solution.py:264
  98.8 5.6 %shard_map.48 = s32[4096,256]{1,0:T(8,128)} custom-call(f32[256,256]{1,0:T(8,128)} %make_table.1.refs_0_, f32[512,128]{1,0:T(8,128)} %copy-done.8, f32[512,128]{1,0:T(8,128)} %copy-done.7, f32[512,128]{1,0:T(8,128)} %collective-permute-done.6.refs_3_, f32[512,128]{1,0:T(8,128)} %collective-permute-done.7.refs_4_, ...), custom_call_target="tpu_custom_call", output_to_operand_aliasing={{}: (5, {})} | custom-call | tf_op jit(solution)/shard_map/pallas_call | solution.py:264
  (44 shorter events, 2.7 us)
Async XLA Ops:
  0.0 54.0 %copy-start.10 = (s32[4096]{0:T(1024)S(1)}, s32[4096]{0:T(1024)}, u32[]{:S(2)}) copy-start(s32[4096]{0:T(1024)} %param.6) | copy-start | bytes 49156
  0.0 54.0 %copy-start.11 = (s32[4096]{0:T(1024)S(1)}, s32[4096]{0:T(1024)}, u32[]{:S(2)}) copy-start(s32[4096]{0:T(1024)} %param.7) | copy-start | bytes 49156
  1.6 26.5 %all-to-all-start = ((f32[16,32,256]{2,1,0:T(8,128)}), f32[16,32,256]{2,1,0:T(8,128)S(1)}, u32[]{:S(2)}, u32[]{:S(2)}) async-start(f32[16,32,256]{2,1,0:T(8,128)} %broadcast_in_dim.38), calls=%async_computation | async-start | bytes 1048576 | tf_op jit(solution)/shard_map/all_to_all | solution.py:286
  19.7 8.4 %collective-permute-start.8 = (f32[512,128]{1,0:T(8,128)}, f32[512,128]{1,0:T(8,128)S(1)}, u32[]{:S(2)}, u32[]{:S(2)}) collective-permute-start(f32[512,128]{1,0:T(8,128)} %bitcast.27), channel_id=1, source_target_pairs={{0,2},{1,3},{2,4},{3,5},{4,6},{5,7},{6,0},{7,1},{8,10},{9,11},{10,... | collective-permute-start | bytes 786440 | tf_op jit(solution)/shard_map/ppermute | solution.py:49
  21.1 13.2 %collective-permute-start.11 = (f32[2,512,128]{2,1,0:T(8,128)}, f32[2,512,128]{2,1,0:T(8,128)S(1)}, u32[]{:S(2)}, u32[]{:S(2)}) collective-permute-start(f32[2,512,128]{2,1,0:T(8,128)} %bitcast.21), channel_id=1, source_target_pairs={{0,8},{1,9},{2,10},{3,11},{4,12},{5,13},{6,14},{7,15},{8,0},{9,1},... | collective-permute-start | bytes 1572872 | tf_op jit(solution)/shard_map/ppermute | solution.py:49
  22.3 17.9 %collective-permute-start.13 = (f32[2,512,128]{2,1,0:T(8,128)}, f32[2,512,128]{2,1,0:T(8,128)S(1)}, u32[]{:S(2)}, u32[]{:S(2)}) collective-permute-start(f32[2,512,128]{2,1,0:T(8,128)} %bitcast.20), channel_id=1, source_target_pairs={{0,4},{1,5},{2,6},{3,7},{4,0},{5,1},{6,2},{7,3},{8,12},{9,13},{10,... | collective-permute-start | bytes 1572872 | tf_op jit(solution)/shard_map/ppermute | solution.py:49
  24.7 27.5 %collective-permute-start.15 = (f32[2,512,128]{2,1,0:T(8,128)}, f32[2,512,128]{2,1,0:T(8,128)S(1)}, u32[]{:S(2)}, u32[]{:S(2)}) collective-permute-start(f32[2,512,128]{2,1,0:T(8,128)} %bitcast.19), channel_id=1, source_target_pairs={{0,10},{1,11},{2,12},{3,13},{4,14},{5,15},{6,8},{7,9},{8,2},{9,3},... | collective-permute-start | bytes 1572872 | tf_op jit(solution)/shard_map/ppermute | solution.py:49
  24.7 28.8 %collective-permute-start.17 = (f32[2,512,128]{2,1,0:T(8,128)}, f32[2,512,128]{2,1,0:T(8,128)S(1)}, u32[]{:S(2)}, u32[]{:S(2)}) collective-permute-start(f32[2,512,128]{2,1,0:T(8,128)} %bitcast.18), channel_id=1, source_target_pairs={{0,6},{1,7},{2,0},{3,1},{4,2},{5,3},{6,4},{7,5},{8,14},{9,15},{10,... | collective-permute-start | bytes 1572872 | tf_op jit(solution)/shard_map/ppermute | solution.py:49
  28.1 66.3 %copy-start.6 = (f32[512,128]{1,0:T(8,128)}, f32[512,128]{1,0:T(8,128)S(1)}, u32[]{:S(2)}) copy-start(f32[512,128]{1,0:T(8,128)S(1)} %collective-permute-done.8.refs_1_) | copy-start | bytes 786436
  28.1 28.4 %copy-start = (f32[16,32,256]{2,1,0:T(8,128)}, f32[16,32,256]{2,1,0:T(8,128)S(1)}, u32[]{:S(2)}) copy-start(f32[16,32,256]{2,1,0:T(8,128)S(1)} %all-to-all-done) | copy-start | bytes 1572868
  28.1 25.4 %collective-permute-start = (f32[512,256]{1,0:T(8,128)S(1)}, f32[512,256]{1,0:T(8,128)}, u32[]{:S(2)}, u32[]{:S(2)}) collective-permute-start(f32[512,256]{1,0:T(8,128)S(1)} %bitcast.13), channel_id=1, source_target_pairs={{0,1},{1,0},{2,3},{3,2},{4,5},{5,4},{6,7},{7,6},{8,9},{9,8},{10,11... | collective-permute-start | bytes 1572872 | tf_op jit(solution)/shard_map/ppermute | solution.py:40
  34.3 48.5 %copy-start.1 = (f32[2,512,128]{2,1,0:T(8,128)}, f32[2,512,128]{2,1,0:T(8,128)S(1)}, u32[]{:S(2)}) copy-start(f32[2,512,128]{2,1,0:T(8,128)S(1)} %collective-permute-done.11.refs_3_) | copy-start | bytes 1572868
  34.3 25.6 %collective-permute-start.10 = (f32[2,512,128]{2,1,0:T(8,128)}, f32[2,512,128]{2,1,0:T(8,128)S(1)}, u32[]{:S(2)}, u32[]{:S(2)}) collective-permute-start(f32[2,512,128]{2,1,0:T(8,128)} %bitcast.15), channel_id=1, source_target_pairs={{0,1},{1,0},{2,3},{3,2},{4,5},{5,4},{6,7},{7,6},{8,9},{9,8},{10,11... | collective-permute-start | bytes 1572872 | tf_op jit(solution)/shard_map/ppermute | solution.py:40
  40.1 42.7 %copy-start.2 = (f32[2,512,128]{2,1,0:T(8,128)}, f32[2,512,128]{2,1,0:T(8,128)S(1)}, u32[]{:S(2)}) copy-start(f32[2,512,128]{2,1,0:T(8,128)S(1)} %collective-permute-done.13.refs_5_) | copy-start | bytes 1572868
  40.1 23.3 %collective-permute-start.12 = (f32[2,512,128]{2,1,0:T(8,128)S(1)}, f32[2,512,128]{2,1,0:T(8,128)}, u32[]{:S(2)}, u32[]{:S(2)}) collective-permute-start(f32[2,512,128]{2,1,0:T(8,128)S(1)} %collective-permute-done.11.refs_3_), channel_id=1, source_target_pairs={{0,1},{1,0},{2,3},{3,2},{4,5},{5,4},{6,7},{7,6},{8,9},{9,8},{10,11... | collective-permute-start | bytes 1572872 | tf_op jit(solution)/shard_map/ppermute | solution.py:40
  52.2 30.6 %copy-start.3 = (f32[2,512,128]{2,1,0:T(8,128)}, f32[2,512,128]{2,1,0:T(8,128)S(1)}, u32[]{:S(2)}) copy-start(f32[2,512,128]{2,1,0:T(8,128)S(1)} %collective-permute-done.15.refs_7_) | copy-start | bytes 1572868
  52.2 12.0 %collective-permute-start.14 = (f32[2,512,128]{2,1,0:T(8,128)S(1)}, f32[2,512,128]{2,1,0:T(8,128)}, u32[]{:S(2)}, u32[]{:S(2)}) collective-permute-start(f32[2,512,128]{2,1,0:T(8,128)S(1)} %collective-permute-done.13.refs_5_), channel_id=1, source_target_pairs={{0,1},{1,0},{2,3},{3,2},{4,5},{5,4},{6,7},{7,6},{8,9},{9,8},{10,11... | collective-permute-start | bytes 1572872 | tf_op jit(solution)/shard_map/ppermute | solution.py:40
  53.4 29.4 %copy-start.4 = (f32[2,512,128]{2,1,0:T(8,128)}, f32[2,512,128]{2,1,0:T(8,128)S(1)}, u32[]{:S(2)}) copy-start(f32[2,512,128]{2,1,0:T(8,128)S(1)} %collective-permute-done.17.refs_9_) | copy-start | bytes 1572868
  53.4 12.7 %collective-permute-start.16 = (f32[2,512,128]{2,1,0:T(8,128)S(1)}, f32[2,512,128]{2,1,0:T(8,128)}, u32[]{:S(2)}, u32[]{:S(2)}) collective-permute-start(f32[2,512,128]{2,1,0:T(8,128)S(1)} %collective-permute-done.15.refs_7_), channel_id=1, source_target_pairs={{0,1},{1,0},{2,3},{3,2},{4,5},{5,4},{6,7},{7,6},{8,9},{9,8},{10,11... | collective-permute-start | bytes 1572872 | tf_op jit(solution)/shard_map/ppermute | solution.py:40
  53.5 14.6 %collective-permute-start.18 = (f32[2,512,128]{2,1,0:T(8,128)S(1)}, f32[2,512,128]{2,1,0:T(8,128)}, u32[]{:S(2)}, u32[]{:S(2)}) collective-permute-start(f32[2,512,128]{2,1,0:T(8,128)S(1)} %collective-permute-done.17.refs_9_), channel_id=1, source_target_pairs={{0,1},{1,0},{2,3},{3,2},{4,5},{5,4},{6,7},{7,6},{8,9},{9,8},{10,11... | collective-permute-start | bytes 1572872 | tf_op jit(solution)/shard_map/ppermute | solution.py:40
  59.8 23.0 %copy-start.5 = (f32[2,512,128]{2,1,0:T(8,128)}, f32[2,512,128]{2,1,0:T(8,128)S(1)}, u32[]{:S(2)}) copy-start(f32[2,512,128]{2,1,0:T(8,128)S(1)} %collective-permute-done.10.refs_2_) | copy-start | bytes 1572868
  59.8 10.4 %collective-permute-start.3 = (f32[256,256]{1,0:T(8,128)}, f32[256,256]{1,0:T(8,128)S(1)}, u32[]{:S(2)}, u32[]{:S(2)}) collective-permute-start(f32[256,256]{1,0:T(8,128)} %choose.1.a_ref), channel_id=1, source_target_pairs={{32,0},{48,16},{0,32},{16,48},{96,64},{112,80},{64,96},{80,112},{3... | collective-permute-start | bytes 786440 | tf_op jit(solution)/shard_map/ppermute | solution.py:36
  63.4 12.7 %collective-permute-start.2 = (f32[256,256]{1,0:T(8,128)}, f32[256,256]{1,0:T(8,128)}, u32[]{:S(2)}, u32[]{:S(2)}) collective-permute-start(f32[256,256]{1,0:T(8,128)} %choose.1.a_ref), channel_id=1, source_target_pairs={{48,0},{0,16},{16,32},{32,48},{112,64},{64,80},{80,96},{96,112},{4... | collective-permute-start | bytes 786440 | tf_op jit(solution)/shard_map/ppermute | solution.py:36
  64.2 13.4 %collective-permute-start.1 = (f32[256,256]{1,0:T(8,128)}, f32[256,256]{1,0:T(8,128)}, u32[]{:S(2)}, u32[]{:S(2)}) collective-permute-start(f32[256,256]{1,0:T(8,128)} %choose.1.a_ref), channel_id=1, source_target_pairs={{16,0},{32,16},{48,32},{0,48},{80,64},{96,80},{112,96},{64,112},{1... | collective-permute-start | bytes 786440 | tf_op jit(solution)/shard_map/ppermute | solution.py:36
  66.1 31.9 %collective-permute-start.5 = (f32[512,128]{1,0:T(8,128)}, f32[512,128]{1,0:T(8,128)S(1)}, u32[]{:S(2)}, u32[]{:S(2)}) collective-permute-start(f32[512,128]{1,0:T(8,128)} %bitcast.25), channel_id=1, source_target_pairs={{0,15},{1,14},{2,9},{3,8},{4,11},{5,10},{6,13},{7,12},{8,7},{9,6},... | collective-permute-start | bytes 786440 | tf_op jit(solution)/shard_map/ppermute | solution.py:49
  68.2 26.2 %collective-permute-start.9 = (f32[512,128]{1,0:T(8,128)}, f32[512,128]{1,0:T(8,128)}, u32[]{:S(2)}, u32[]{:S(2)}) collective-permute-start(f32[512,128]{1,0:T(8,128)} %bitcast.26), channel_id=1, source_target_pairs={{0,3},{1,2},{2,5},{3,4},{4,7},{5,6},{6,1},{7,0},{8,11},{9,10},{10,... | collective-permute-start | bytes 786440 | tf_op jit(solution)/shard_map/ppermute | solution.py:49
  70.3 0.7 copy-start.9
  71.0 27.1 %collective-permute-start.4 = (f32[512,128]{1,0:T(8,128)}, f32[512,128]{1,0:T(8,128)S(1)}, u32[]{:S(2)}, u32[]{:S(2)}) collective-permute-start(f32[512,128]{1,0:T(8,128)} %bitcast.24), channel_id=1, source_target_pairs={{0,14},{1,15},{2,8},{3,9},{4,10},{5,11},{6,12},{7,13},{8,6},{9,7},... | collective-permute-start | bytes 786440 | tf_op jit(solution)/shard_map/ppermute | solution.py:49
  76.1 21.9 %collective-permute-start.6 = (f32[512,128]{1,0:T(8,128)}, f32[512,128]{1,0:T(8,128)}, u32[]{:S(2)}, u32[]{:S(2)}) collective-permute-start(f32[512,128]{1,0:T(8,128)} %bitcast.23), channel_id=1, source_target_pairs={{0,12},{1,13},{2,14},{3,15},{4,8},{5,9},{6,10},{7,11},{8,4},{9,5},... | collective-permute-start | bytes 786440 | tf_op jit(solution)/shard_map/ppermute | solution.py:49
  77.6 20.5 %collective-permute-start.7 = (f32[512,128]{1,0:T(8,128)}, f32[512,128]{1,0:T(8,128)}, u32[]{:S(2)}, u32[]{:S(2)}) collective-permute-start(f32[512,128]{1,0:T(8,128)} %bitcast.22), channel_id=1, source_target_pairs={{0,13},{1,12},{2,15},{3,14},{4,9},{5,8},{6,11},{7,10},{8,5},{9,4},... | collective-permute-start | bytes 786440 | tf_op jit(solution)/shard_map/ppermute | solution.py:49
  98.0 0.7 copy-start.7
  98.1 0.8 copy-start.8
